TPU v7x, 32 devices: a whole 2x2x4 slice. The times are simulated.
32 devices in a mesh: seq: 4 (over z), fsdp: 8 (over y, x, core).
Axes of the slice: x: 2, y: 2, z: 4, core: 2. Of those that a mesh axis runs over, the one named last changes fastest.
Arguments:
- tokens: bfloat16 [8, 1024, 2048], P('fsdp', 'seq'), may hold values from -6 to 6
- cotangent: bfloat16 [8, 1024, 2048], P('fsdp', 'seq'), may hold values from -6 to 6
- lengths: int32 [8], P('fsdp'), may hold values from 256 to 1024, as said below
- routes: int32 [8, 1024, 8], P('fsdp', 'seq'), may hold values from 0 to 31, as said below
- slots: int32 [8, 1024, 8], P('fsdp', 'seq'), may hold values from -1 to 79, as said below
- w_qkv: bfloat16 [2048, 5120], P(('seq', 'fsdp')), may hold values from -0.125 to 0.125
- w_out: bfloat16 [4096, 2048], P(('seq', 'fsdp')), may hold values from -1.5 to 1.5
- w_router: bfloat16 [2048, 32], P(('seq', 'fsdp')), may hold values from -0.25 to 0.25
- norm_gains: bfloat16 [4352], P(('seq', 'fsdp')), may hold values from 0.25 to 1.75
- w_gate_up: bfloat16 [32, 2048, 1536], P('fsdp', 'seq'), may hold values from -0.125 to 0.125
- w_down: bfloat16 [32, 768, 2048], P('fsdp', None, 'seq'), may hold values from -0.625 to 0.625
Outputs:
- output: bfloat16 [8, 1024, 2048], P('fsdp', 'seq')
- d_input: float32 [8, 1024, 2048], P('fsdp', 'seq')
- grad_qkv: float32 [2048, 5120], P(('seq', 'fsdp'))
- grad_out: float32 [4096, 2048], P(('seq', 'fsdp'))
- grad_router: float32 [2048, 32], P(('seq', 'fsdp'))
- grad_gains: float32 [4352], P(('seq', 'fsdp'))
- grad_gate_up: float32 [32, 2048, 1536], P('fsdp', 'seq')
- grad_down: float32 [32, 768, 2048], P('fsdp', None, 'seq')
Inputs may be any that keep to these rules, and one draw needn't show every extreme that they name: `lengths`: every length is at least a quarter of 1024, and some sequence is 1024 long. `routes`: each token names 8 different experts. Among the valid tokens of one device (aligned blocks of 256 positions of a sequence) that route to one expert, the slots count 0, 1, 2 and so on in order of position while below 80; later ones and all padded slots are -1. In every draw some device sends 80 rows to some expert.
All inputs are finite; a program needn't handle non-finite values.
Results may differ from a plain program's by a relative error of at most 0.019.
Values may be sent and summed in bfloat16 or wider, within the bound.
A program may use at most 384 MiB of HBM per device.

v0:
```python
import functools

import jax
import jax.numpy as jnp
from jax import lax
from jax.experimental import pallas as pl
from jax.experimental.pallas import tpu as pltpu
from jax.sharding import PartitionSpec as P

QH = 32
KH = 4
HD = 128
FF = 768
TOPK = 8
EPSILON = 1e-06
THETA = 1000000.0
MASKED = -1e30
AHEAD = 2
BF = jnp.bfloat16
F32 = jnp.float32
MESH = pl.DeviceIdType.MESH
ANY = pl.BlockSpec(memory_space=pl.ANY)
VM = pl.BlockSpec(memory_space=pltpu.VMEM)
DMA = pltpu.SemaphoreType.DMA
EVERY = ("seq", "fsdp")

def index_of(sizes, axes):
    at = 0
    for axis in axes:
        at = at * sizes[axis] + lax.axis_index(axis)
    return at


def count_of(sizes, axes):
    number = 1
    for axis in axes:
        number *= sizes[axis]
    return number


def place_of(sizes, axes, at):
    if len(axes) == 1:
        return {axes[0]: at}
    return {axes[0]: at // sizes[axes[1]], axes[1]: at % sizes[axes[1]]}


def greet(sizes):
    total = count_of(sizes, EVERY)
    me = index_of(sizes, EVERY)
    barrier = pltpu.get_barrier_semaphore()
    for step in range(1, total):
        pl.semaphore_signal(
            barrier, inc=1, device_id=place_of(sizes, EVERY, lax.rem(me + step, total)),
            device_id_type=MESH,
        )
    return lambda: pl.semaphore_wait(barrier, total - 1)


def block_of(ref, dim, at, total):
    if dim == "columns":
        width = ref.shape[-1] // total
        return ref.at[:, :, pl.ds(pl.multiple_of(at * width, 128), width)]
    return ref.at[at] if dim == 0 else ref.at[:, at]


class Blocks:
    def __init__(self, sizes, specs, sources, results, sems):
        self.own, self.away = [], []
        if not specs:
            return
        send_sem, recv_sem, own_sem = sems
        for i, (axes, before, after) in enumerate(specs):
            me = index_of(sizes, axes)
            total = count_of(sizes, axes)
            self.own.append(
                pltpu.make_async_copy(
                    block_of(sources[i], before, me, total),
                    block_of(results[i], after, me, total),
                    own_sem.at[i],
                )
            )
            for step in range(1, total):
                target = lax.rem(me + step, total)
                self.away.append(
                    pltpu.make_async_remote_copy(
                        src_ref=block_of(sources[i], before, target, total),
                        dst_ref=block_of(results[i], after, me, total),
                        send_sem=send_sem.at[i, step],
                        recv_sem=recv_sem.at[i, step],
                        device_id=place_of(sizes, axes, target),
                        device_id_type=MESH,
                    )
                )

    def start(self):
        for copy in self.own + self.away:
            copy.start()

    def wait(self):
        for copy in self.own + self.away:
            copy.wait()


def block_sems(sizes, specs):
    if not specs:
        return []
    total = max(count_of(sizes, axes) for axes, _, _ in specs)
    return [DMA((len(specs), total)), DMA((len(specs), total)), DMA((len(specs),))]


def block_outs(sizes, arrays, specs):
    outs = []
    for array, (axes, before, after) in zip(arrays, specs):
        shape = list(array.shape)
        total = count_of(sizes, axes)
        if before == "columns":
            shape = [total, shape[0], shape[1], shape[2] // total]
        elif after == "columns":
            shape = [shape[1], shape[2], shape[3] * total]
        elif before != after:
            shape[0], shape[1] = shape[1], shape[0]
        outs.append(jax.ShapeDtypeStruct(tuple(shape), array.dtype))
    return outs


def exchange_kernel(sizes, specs, *refs):
    count = len(specs)
    met = greet(sizes)
    blocks = Blocks(sizes, specs, refs[:count], refs[count : 2 * count], refs[2 * count :])
    met()
    blocks.start()
    blocks.wait()


def exchange(arrays, specs, sizes, collective_id):
    count = len(arrays)
    return pl.pallas_call(
        functools.partial(exchange_kernel, sizes, specs),
        out_shape=block_outs(sizes, arrays, specs),
        in_specs=[ANY] * count,
        out_specs=[ANY] * count,
        scratch_shapes=block_sems(sizes, specs),
        compiler_params=pltpu.CompilerParams(collective_id=collective_id, has_side_effects=True),
        name=f"exchange_{collective_id}",
    )(*arrays)


def entry_kernel(
    sizes, tok_ref, cot_ref, table_ref, wqkv_ref, wout_ref, small_ref,
    tok_out, cot_out, table_out, wq_out, wo_out, small_out,
    tok_send, tok_recv, tab_send, tab_recv, wq_zsend, wq_zrecv,
    pl_send, pl_recv, sib_send, sib_recv, sm_send, sm_recv, own_sem,
):
    S, F = sizes["seq"], sizes["fsdp"]
    s = lax.axis_index("seq")
    f = lax.axis_index("fsdp")
    N = S * F
    chips = F // 2
    me = s * F + f
    other = f + 1 - 2 * lax.rem(f, 2)
    rows = tok_ref.shape[0]
    chunks = tok_recv.shape[2]
    span = rows // chunks
    met = greet(sizes)
    kv = KH * HD // S
    q_width = QH * HD // S
    starts = (0, q_width * S, (q_width + kv) * S)
    widths = (q_width, kv, kv)
    offsets = (0, q_width, q_width + kv)

    def columns(z, p):
        return pl.ds(pl.multiple_of(starts[p] + z * widths[p], 128), widths[p])

    own = [
        pltpu.make_async_copy(tok_ref, tok_out.at[s], own_sem.at[0]),
        pltpu.make_async_copy(table_ref, table_out.at[s], own_sem.at[1]),
        pltpu.make_async_copy(wout_ref, wo_out.at[f], own_sem.at[2]),
        pltpu.make_async_copy(small_ref, small_out.at[me], own_sem.at[3]),
        pltpu.make_async_copy(cot_ref, cot_out.at[s], own_sem.at[4]),
    ]
    for p in range(3):
        own.append(
            pltpu.make_async_copy(
                wqkv_ref.at[:, columns(s, p)],
                wq_out.at[s, f, :, pl.ds(offsets[p], widths[p])],
                own_sem.at[5 + p],
            )
        )
    for copy in own:
        copy.start()
    met()

    def remote(src, dst, send_sem, recv_sem, where):
        return pltpu.make_async_remote_copy(
            src_ref=src, dst_ref=dst, send_sem=send_sem, recv_sem=recv_sem,
            device_id=where, device_id_type=MESH,
        )

    wq_line = []
    tables = []
    for step in range(1, S):
        target = lax.rem(s + step, S)
        for p in range(3):
            copy = remote(
                wqkv_ref.at[:, columns(target, p)],
                wq_out.at[s, f, :, pl.ds(offsets[p], widths[p])],
                wq_zsend.at[step, p], wq_zrecv.at[step, p], {"seq": target},
            )
            copy.start()
            wq_line.append(copy)
        copy = remote(
            table_ref, table_out.at[s], tab_send.at[step], tab_recv.at[step], {"seq": target}
        )
        copy.start()
        tables.append(copy)

    def along(a, block, c, way, hop):
        source, result = ((tok_ref, tok_out), (cot_ref, cot_out))[a]
        here = result.at[block, pl.ds(c * span, span)]
        src = source.at[pl.ds(c * span, span)] if hop == 1 else here
        return remote(
            src, here, tok_send.at[a, way, c, hop], tok_recv.at[a, way, c, hop],
            {"seq": s + 1 if way == 0 else s - 1},
        )

    def depart(a):
        for c in range(chunks):
            @pl.when(s < S - 1)
            def _():
                along(a, s, c, 0, 1).start()

            @pl.when(s > 0)
            def _():
                along(a, s, c, 1, 1).start()

    def relay(a, hop):
        for c in range(chunks):
            @pl.when(s >= hop)
            def _():
                along(a, s - hop, c, 0, hop).wait_recv()
                if hop < S - 1:
                    @pl.when(s < S - 1)
                    def _():
                        along(a, s - hop, c, 0, hop + 1).start()

            @pl.when(s < S - hop)
            def _():
                along(a, s + hop, c, 1, hop).wait_recv()
                if hop < S - 1:
                    @pl.when(s > 0)
                    def _():
                        along(a, s + hop, c, 1, hop + 1).start()

    depart(0)

    def plane_block(slot, owner):
        if slot == S:
            return wo_out.at[owner]
        return wq_out.at[lax.rem(s - slot + S, S), owner]

    def to_chip(slot, step):
        block = plane_block(slot, f)
        return remote(block, block, pl_send.at[slot, step], pl_recv.at[slot, step],
                      {"fsdp": lax.rem(f + 2 * step, F)})

    def to_other(slot, step):
        block = plane_block(slot, lax.rem(f - 2 * step + F, F))
        return remote(block, block, sib_send.at[slot, step], sib_recv.at[slot, step],
                      {"fsdp": other})

    def spread(slot):
        for step in range(1, chips):
            to_chip(slot, step).start()
        to_other(slot, 0).start()

    def forward(slot):
        for step in range(1, chips):
            to_chip(slot, step).wait_recv()
            to_other(slot, step).start()

    smalls = []
    for step in range(1, N):
        target = lax.rem(me + step, N)
        copy = remote(small_ref, small_out.at[me], sm_send.at[step], sm_recv.at[step],
                      place_of(sizes, EVERY, target))
        copy.start()
        smalls.append(copy)
    for copy in own:
        copy.wait()
    spread(0)
    spread(S)
    relay(0, 1)
    depart(1)
    for step in range(1, S):
        for p in range(3):
            wq_line[(step - 1) * 3 + p].wait()
        spread(step)
    for hop in range(2, S):
        relay(0, hop)
        relay(1, hop - 1)
    for slot in range(S + 1):
        forward(slot)
    relay(1, S - 1)
    for a in range(2):
        for hop in range(1, S):
            for c in range(chunks):
                @pl.when((s < S - 1) & (s >= hop - 1))
                def _():
                    along(a, s, c, 0, hop).wait_send()

                @pl.when((s > 0) & (s <= S - hop))
                def _():
                    along(a, s, c, 1, hop).wait_send()
    for slot in range(S + 1):
        for step in range(1, chips):
            to_chip(slot, step).wait_send()
        for step in range(chips):
            to_other(slot, step).wait_send()
            block = plane_block(slot, lax.rem(other - 2 * step + F, F))
            remote(block, block, sib_send.at[slot, step], sib_recv.at[slot, step],
                   {"fsdp": other}).wait_recv()
    for copy in tables + smalls:
        copy.wait()


def entry(tokens, cotangent, table, w_qkv, w_out, small, sizes, collective_id, chunks=4):
    S, F = sizes["seq"], sizes["fsdp"]
    own_width = w_qkv.shape[1] // S
    N = S * F
    line_out = jax.ShapeDtypeStruct((S,) + tokens.shape, tokens.dtype)
    return pl.pallas_call(
        functools.partial(entry_kernel, sizes),
        out_shape=[
            line_out,
            line_out,
            jax.ShapeDtypeStruct((S,) + table.shape, table.dtype),
            jax.ShapeDtypeStruct((S, F, w_qkv.shape[0], own_width), w_qkv.dtype),
            jax.ShapeDtypeStruct((F,) + w_out.shape, w_out.dtype),
            jax.ShapeDtypeStruct((N,) + small.shape, small.dtype),
        ],
        in_specs=[ANY] * 6,
        out_specs=[ANY] * 6,
        scratch_shapes=[
            DMA((2, 2, chunks, S)), DMA((2, 2, chunks, S)), DMA((S,)), DMA((S,)),
            DMA((S, 3)), DMA((S, 3)), DMA((S + 1, F // 2)), DMA((S + 1, F // 2)),
            DMA((S + 1, F // 2)), DMA((S + 1, F // 2)), DMA((N,)), DMA((N,)), DMA((8,)),
        ],
        compiler_params=pltpu.CompilerParams(collective_id=collective_id, has_side_effects=True),
        name="entry",
    )(tokens, cotangent, table, w_qkv, w_out, small)


def line_kernel(sizes, chunks, mode, parts, extra, *refs):
    S = sizes["seq"]
    count = len(extra)
    names = {
        "ffn": (["base", "gain"], ["resid_out", "all_out"]),
        "grad": (["base", "gain", "resid", "add"], ["grad_out", "gain_out", "all_out"]),
        "sum": ([], ["sum_out"]),
    }[mode]
    refs = list(refs)

    def take(number):
        taken, refs[:number] = refs[:number], []
        return taken

    part_refs = take(parts)
    given = dict(zip(names[0], take(len(names[0]))))
    sources = take(count)
    given.update(zip(names[1], take(len(names[1]))))
    results = take(count)
    from_left, from_right = take(2)
    gather = mode != "sum"
    if gather:
        (stage,) = take(1)
    rs_send, rs_recv = take(2)
    if gather:
        ag_send, ag_recv, own_sem = take(3)
        all_out = given["all_out"]
    s = lax.axis_index("seq")
    rows = part_refs[0].shape[1]
    span = rows // chunks
    met = greet(sizes)
    blocks = Blocks(sizes, extra, sources, results, refs)
    met()

    def at(c):
        return pl.ds((c % chunks) * span, span)

    def mine(d, c):
        return part_refs[c // chunks].at[d, at(c)]

    def landed(way, d, c):
        return (from_left, from_right)[way].at[c // chunks, d, at(c)]

    def rs_copy(d, c, way, src):
        return pltpu.make_async_remote_copy(
            src_ref=src, dst_ref=landed(way, d, c),
            send_sem=rs_send.at[way, d, c], recv_sem=rs_recv.at[way, d, c],
            device_id={"seq": s + 1 if way == 0 else s - 1}, device_id_type=MESH,
        )

    def ag_copy(block, c, way, hop):
        src = stage.at[at(c)] if hop == 1 else all_out.at[block, at(c)]
        return pltpu.make_async_remote_copy(
            src_ref=src, dst_ref=all_out.at[block, at(c)],
            send_sem=ag_send.at[way, c, hop], recv_sem=ag_recv.at[way, c, hop],
            device_id={"seq": s + 1 if way == 0 else s - 1}, device_id_type=MESH,
        )

    def end_step(c):
        for d in range(S - 1, 0, -1):
            @pl.when((s == 0) & (d > s))
            def _():
                rs_copy(d, c, 0, mine(d, c)).start()
        for d in range(S - 1):
            @pl.when((s == S - 1) & (d < s))
            def _():
                rs_copy(d, c, 1, mine(d, c)).start()

    def middle_step(c):
        for way in range(2):
            order = range(S - 1, 0, -1) if way == 0 else range(S - 1)
            for d in order:
                inside = (s > 0) & (d > s) if way == 0 else (s < S - 1) & (d < s)

                @pl.when(inside)
                def _():
                    buffer = landed(way, d, c)
                    rs_copy(d, c, way, buffer).wait_recv()
                    total = buffer[...].astype(F32) + mine(d, c)[...].astype(F32)
                    buffer[...] = total.astype(BF)
                    rs_copy(d, c, way, buffer).start()

    def final_step(c):
        @pl.when(s > 0)
        def _():
            rs_copy(s, c, 0, mine(s, c)).wait_recv()

        @pl.when(s < S - 1)
        def _():
            rs_copy(s, c, 1, mine(s, c)).wait_recv()

        total = mine(s, c)[...].astype(F32)
        total = total + jnp.where(s > 0, landed(0, s, c)[...].astype(F32), 0.0)
        total = total + jnp.where(s < S - 1, landed(1, s, c)[...].astype(F32), 0.0)
        if mode == "sum":
            given["sum_out"][c // chunks, at(c), :] = total
            return
        if mode == "ffn":
            value = given["base"][at(c), :].astype(F32) + total
            given["resid_out"][at(c), :] = value
            factor = lax.rsqrt(jnp.mean(value * value, axis=-1, keepdims=True) + EPSILON)
            low = (value * factor * given["gain"][...]).astype(BF)
        else:
            upstream = total + given["add"][at(c), :]
            value = given["resid"][at(c), :]
            factor = lax.rsqrt(jnp.mean(value * value, axis=-1, keepdims=True) + EPSILON)
            normed = value * factor
            scaled = upstream * given["gain"][...]
            inner = jnp.mean(scaled * normed, axis=-1, keepdims=True)
            result = given["base"][at(c), :] + factor * (scaled - normed * inner)
            given["grad_out"][at(c), :] = result
            gained = jnp.sum(upstream * normed, axis=0, keepdims=True)
            gain_out = given["gain_out"]
            gain_out[...] = gained if c == 0 else gain_out[...] + gained
            low = result.astype(BF)
        stage[at(c), :] = low
        pltpu.make_async_copy(stage.at[at(c)], all_out.at[s, at(c)], own_sem.at[c]).start()

        @pl.when(s < S - 1)
        def _():
            ag_copy(s, c, 0, 1).start()

        @pl.when(s > 0)
        def _():
            ag_copy(s, c, 1, 1).start()

    def relay_step(c, hop):
        @pl.when(s >= hop)
        def _():
            ag_copy(s - hop, c, 0, hop).wait_recv()
            if hop < S - 1:
                @pl.when(s < S - 1)
                def _():
                    ag_copy(s - hop, c, 0, hop + 1).start()

        @pl.when(s < S - hop)
        def _():
            ag_copy(s + hop, c, 1, hop).wait_recv()
            if hop < S - 1:
                @pl.when(s > 0)
                def _():
                    ag_copy(s + hop, c, 1, hop + 1).start()

    steps = chunks * parts
    ahead = min(steps, AHEAD if gather else steps)
    for c in range(ahead):
        end_step(c)
    blocks.start()
    hops = S - 1 if gather else 0
    for t in range(steps + 1 + hops):
        if t < steps:
            middle_step(t)
        if t + ahead < steps:
            end_step(t + ahead)
        if 0 <= t - 1 < steps:
            final_step(t - 1)
        for hop in range(1, hops + 1):
            if 0 <= t - 1 - hop < steps:
                relay_step(t - 1 - hop, hop)

    for c in range(steps):
        for d in range(S - 1, 0, -1):
            @pl.when(d > s)
            def _():
                rs_copy(d, c, 0, mine(d, c)).wait_send()
        for d in range(S - 1):
            @pl.when(d < s)
            def _():
                rs_copy(d, c, 1, mine(d, c)).wait_send()
        if gather:
            pltpu.make_async_copy(stage.at[at(c)], all_out.at[s, at(c)], own_sem.at[c]).wait()
            for hop in range(1, S):
                @pl.when((s < S - 1) & (s >= hop - 1))
                def _():
                    ag_copy(s, c, 0, hop).wait_send()

                @pl.when((s > 0) & (s <= S - hop))
                def _():
                    ag_copy(s, c, 1, hop).wait_send()
    blocks.wait()


def line(mode, sizes, parts, others, extras, specs, collective_id, chunks=8):
    S = sizes["seq"]
    _, rows, width = parts[0].shape
    full = jax.ShapeDtypeStruct((rows, width), F32)
    everyone = jax.ShapeDtypeStruct((S, rows, width), BF)
    steps = chunks * len(parts)
    scratch = [pltpu.VMEM((len(parts), S, rows, width), BF)] * 2
    sems = [DMA((2, S, steps)), DMA((2, S, steps))]
    if mode == "ffn":
        outs, out_specs = [full, everyone], [VM, ANY]
    elif mode == "grad":
        outs, out_specs = [full, jax.ShapeDtypeStruct((1, width), F32), everyone], [VM, VM, ANY]
    else:
        outs, out_specs = [jax.ShapeDtypeStruct((len(parts), rows, width), F32)], [VM]
    if mode != "sum":
        scratch.append(pltpu.VMEM((rows, width), BF))
        sems += [DMA((2, chunks, S)), DMA((2, chunks, S)), DMA((chunks,))]
    return pl.pallas_call(
        functools.partial(line_kernel, sizes, chunks, mode, len(parts), specs),
        out_shape=outs + block_outs(sizes, extras, specs),
        in_specs=[VM] * (len(parts) + len(others)) + [ANY] * len(extras),
        out_specs=out_specs + [ANY] * len(extras),
        scratch_shapes=scratch + sems + block_sems(sizes, specs),
        compiler_params=pltpu.CompilerParams(
            collective_id=collective_id, has_side_effects=True, vmem_limit_bytes=56 << 20
        ),
        name=f"line_{mode}",
    )(*parts, *others, *extras)


def turn(values, cosine, sine):
    return values * cosine + pltpu.roll(values, HD // 2, 1) * sine


def softmax_block(query, keys, first_row, length, scale):
    scores = lax.dot_general(query, keys, (((1,), (1,)), ((), ())), preferred_element_type=F32) * scale
    row = first_row + lax.broadcasted_iota(jnp.int32, scores.shape, 0)
    column = lax.broadcasted_iota(jnp.int32, scores.shape, 1)
    scores = jnp.where((column <= row) & (column < length), scores, MASKED)
    peak = jnp.max(scores, axis=-1, keepdims=True)
    weights = jnp.exp(scores - peak)
    return weights * (1.0 / jnp.sum(weights, axis=-1, keepdims=True))


def attend_kernel(heads, blocks, length_ref, proj_ref, cos_ref, sin_ref, gains_ref, low_ref, out_ref, k_all, v_all):
    step = pl.program_id(0)
    rows = proj_ref.shape[0]
    length = length_ref[0]
    cosine = cos_ref[...]
    sine = sin_ref[...]
    q_gain = gains_ref[0:1, :]
    k_gain = gains_ref[1:2, :]
    scale = HD ** (-0.5)

    def normed(raw, gain):
        factor = lax.rsqrt(jnp.mean(raw * raw, axis=-1, keepdims=True) + EPSILON)
        return turn(raw * factor * gain, cosine, sine).astype(BF)

    key = normed(proj_ref[:, heads * HD : (heads + 1) * HD], k_gain)
    value = proj_ref[:, (heads + 1) * HD :].astype(BF)
    low_ref[:, heads * HD : (heads + 1) * HD] = key
    low_ref[:, (heads + 1) * HD :] = value
    here = pl.ds(pl.multiple_of(step * rows, rows), rows)
    k_all[here, :] = key
    v_all[here, :] = value
    for block in range(blocks):
        @pl.when(step == block)
        def _():
            width = (block + 1) * rows

            @pl.loop(0, heads)
            def _(h):
                column = pl.ds(pl.multiple_of(h * HD, HD), HD)
                query = normed(proj_ref[:, column], q_gain)
                low_ref[:, column] = query
                probs = softmax_block(query, k_all[:width, :], block * rows, length, scale)
                mixed = jnp.dot(probs.astype(BF), v_all[:width, :], preferred_element_type=F32)
                out_ref[:, column] = mixed.astype(BF)


def attend(length, projected, cosine, sine, gains, heads, blocks=4):
    total, width = projected.shape
    rows = total // blocks
    return pl.pallas_call(
        functools.partial(attend_kernel, heads, blocks),
        grid=(blocks,),
        out_shape=[
            jax.ShapeDtypeStruct((total, width), BF),
            jax.ShapeDtypeStruct((total, heads * HD), BF),
        ],
        in_specs=[
            pl.BlockSpec(memory_space=pltpu.SMEM),
            pl.BlockSpec((rows, width), lambda i: (i, 0)),
            pl.BlockSpec((rows, HD), lambda i: (i, 0)),
            pl.BlockSpec((rows, HD), lambda i: (i, 0)),
            pl.BlockSpec((2, HD), lambda i: (0, 0)),
        ],
        out_specs=[
            pl.BlockSpec((rows, width), lambda i: (i, 0)),
            pl.BlockSpec((rows, heads * HD), lambda i: (i, 0)),
        ],
        scratch_shapes=[pltpu.VMEM((total, HD), BF), pltpu.VMEM((total, HD), BF)],
        compiler_params=pltpu.CompilerParams(vmem_limit_bytes=56 << 20),
        cost_estimate=pl.CostEstimate(flops=4 * heads * total * total * HD, bytes_accessed=total * width * 8, transcendentals=heads * total * total),
        name="attend",
    )(length, projected, cosine, sine, gains)


def attend_back_kernel(heads, blocks, length_ref, proj_ref, low_ref, kv_ref, grad_ref, cos_ref, sin_ref, gains_ref,
                       out_ref, gains_out, gk_all, gv_all):
    step = pl.program_id(0)
    rows = proj_ref.shape[0]
    length = length_ref[0]
    cosine = cos_ref[...]
    sine = sin_ref[...]
    q_gain = gains_ref[0:1, :]
    k_gain = gains_ref[1:2, :]
    scale = HD ** (-0.5)
    block_at = blocks - 1 - step

    def back(raw, gain, grad):
        grad = turn(grad, cosine, -sine)
        factor = lax.rsqrt(jnp.mean(raw * raw, axis=-1, keepdims=True) + EPSILON)
        unit = raw * factor
        scaled = grad * gain
        inner = jnp.mean(scaled * unit, axis=-1, keepdims=True)
        return factor * (scaled - unit * inner), jnp.sum(grad * unit, axis=0, keepdims=True)

    @pl.when(step == 0)
    def _():
        gk_all[...] = jnp.zeros_like(gk_all)
        gv_all[...] = jnp.zeros_like(gv_all)
        gains_out[...] = jnp.zeros_like(gains_out)

    for block in range(blocks):
        @pl.when(block_at == block)
        def _():
            width = (block + 1) * rows
            keys = kv_ref[:width, :HD]
            values = kv_ref[:width, HD:]

            @pl.loop(0, heads)
            def _(h):
                column = pl.ds(pl.multiple_of(h * HD, HD), HD)
                query = low_ref[:, column]
                grad_o = grad_ref[:, column]
                probs = softmax_block(query, keys, block * rows, length, scale)
                grad_p = lax.dot_general(grad_o, values, (((1,), (1,)), ((), ())), preferred_element_type=F32)
                inner = jnp.sum(probs * grad_p, axis=-1, keepdims=True)
                grad_s = (probs * (grad_p - inner)).astype(BF)
                grad_q = jnp.dot(grad_s, keys, preferred_element_type=F32) * scale
                gk_all[:width, :] += lax.dot_general(
                    grad_s, query, (((0,), (0,)), ((), ())), preferred_element_type=F32
                )
                gv_all[:width, :] += lax.dot_general(
                    probs.astype(BF), grad_o, (((0,), (0,)), ((), ())), preferred_element_type=F32
                )
                grad_raw, gained = back(proj_ref[:, column], q_gain, grad_q.astype(BF).astype(F32))
                out_ref[:, column] = grad_raw.astype(BF)
                gains_out[0:1, :] += gained

    here = pl.ds(pl.multiple_of(block_at * rows, rows), rows)
    grad_k = (gk_all[here, :] * scale).astype(BF).astype(F32)
    grad_raw, gained = back(proj_ref[:, heads * HD : (heads + 1) * HD], k_gain, grad_k)
    out_ref[:, heads * HD : (heads + 1) * HD] = grad_raw.astype(BF)
    out_ref[:, (heads + 1) * HD :] = gv_all[here, :].astype(BF)
    gains_out[1:2, :] += gained


def attend_back(length, projected, low, grad_o, cosine, sine, gains, heads, blocks=4):
    total, width = projected.shape
    rows = total // blocks
    return pl.pallas_call(
        functools.partial(attend_back_kernel, heads, blocks),
        grid=(blocks,),
        out_shape=[
            jax.ShapeDtypeStruct((total, width), BF),
            jax.ShapeDtypeStruct((2, HD), F32),
        ],
        in_specs=[
            pl.BlockSpec(memory_space=pltpu.SMEM),
            pl.BlockSpec((rows, width), lambda i: (blocks - 1 - i, 0)),
            pl.BlockSpec((rows, heads * HD), lambda i: (blocks - 1 - i, 0)),
            pl.BlockSpec((total, 2 * HD), lambda i: (0, heads // 2)),
            pl.BlockSpec((rows, heads * HD), lambda i: (blocks - 1 - i, 0)),
            pl.BlockSpec((rows, HD), lambda i: (blocks - 1 - i, 0)),
            pl.BlockSpec((rows, HD), lambda i: (blocks - 1 - i, 0)),
            pl.BlockSpec((2, HD), lambda i: (0, 0)),
        ],
        out_specs=[
            pl.BlockSpec((rows, width), lambda i: (blocks - 1 - i, 0)),
            pl.BlockSpec((2, HD), lambda i: (0, 0)),
        ],
        scratch_shapes=[pltpu.VMEM((total, HD), F32), pltpu.VMEM((total, HD), F32)],
        compiler_params=pltpu.CompilerParams(vmem_limit_bytes=56 << 20),
        cost_estimate=pl.CostEstimate(flops=10 * heads * total * total * HD, bytes_accessed=total * width * 10, transcendentals=heads * total * total),
        name="attend_back",
    )(length, projected, low, low, grad_o, cosine, sine, gains)


def rms_factor(values):
    return lax.rsqrt(jnp.mean(values * values, axis=-1, keepdims=True) + EPSILON)


def dot(left, right):
    return jnp.dot(left, right, preferred_element_type=F32)


def mm(form, left, right):
    return jnp.einsum(form, left, right, preferred_element_type=F32)


def whole_columns(blocks):
    parts, rows, _ = blocks.shape
    q_width = QH * HD // parts
    kv_width = KH * HD // parts
    moved = blocks.transpose(1, 0, 2)
    return jnp.concatenate(
        [
            moved[..., :q_width].reshape(rows, -1),
            moved[..., q_width : q_width + kv_width].reshape(rows, -1),
            moved[..., q_width + kv_width :].reshape(rows, -1),
        ],
        axis=-1,
    )


def lanes(flat, lead):
    width = flat.shape[-1]
    rows = -(-width // 2048) * 16
    return jnp.pad(flat, ((0, 0), (0, rows * 128 - width))).reshape(lead, rows, 128)


def per_device(
    tokens, cotangent, lengths, routes, slots, w_qkv, w_out, w_router, norm_gains, w_gate_up, w_down
):
    tok_count = tokens.shape[1]
    width = tokens.shape[2]
    S = lax.axis_size("seq")
    F = lax.axis_size("fsdp")
    N = S * F
    sizes = {"seq": S, "fsdp": F}
    local_experts = w_gate_up.shape[0]
    own_experts = local_experts // S
    expert_count = w_router.shape[1]
    capacity = tok_count * TOPK * 5 // (4 * expert_count)
    heads = QH // S
    seq_total = tok_count * S
    q_width = heads * HD
    own_width = q_width + 2 * HD
    seq_at = lax.axis_index("seq")
    w_rows = w_qkv.shape[0]
    small = norm_gains.shape[0]
    router_size = w_router.size
    part_width = w_gate_up.shape[1]
    down_width = w_down.shape[2]
    assert KH == S and local_experts % S == 0

    small_send = lanes(jnp.concatenate([w_router.reshape(-1), norm_gains])[None], 1)[0]
    table = jnp.concatenate([routes[0].T, slots[0].T])
    tok_all, cot_all, table_all, w_proj, out_own, small_all = entry(
        tokens[0], cotangent[0], table, w_qkv, w_out, small_send, sizes, 1
    )
    w_proj = w_proj.reshape(width, own_width)
    out_own = out_own.reshape(q_width, width)
    small_flat = small_all.reshape(N, -1)
    full_router = small_flat[:, :router_size].reshape(width, expert_count)
    gain_values = small_flat[:, router_size : router_size + small].reshape(-1).astype(F32)
    gain_attn = gain_values[:width]
    gain_ffn = gain_values[width : 2 * width][None]
    gain_heads = gain_values[2 * width :].reshape(2, HD)

    inputs_all = tok_all.reshape(seq_total, width).astype(F32)
    attn_low = (inputs_all * rms_factor(inputs_all) * gain_attn).astype(BF)
    projected = dot(attn_low, w_proj)
    positions = jnp.arange(seq_total, dtype=jnp.int32)
    frequency = THETA ** (-jnp.arange(HD // 2, dtype=F32) / (HD // 2))
    angles = positions.astype(F32)[:, None] * frequency[None, :]
    cosine = jnp.concatenate([jnp.cos(angles)] * 2, axis=-1)
    sine = jnp.concatenate([-jnp.sin(angles), jnp.sin(angles)], axis=-1)
    qkv_low, o_low = attend(lengths, projected, cosine, sine, gain_heads, heads)
    o_part = dot(o_low, out_own).astype(BF).reshape(S, tok_count, width)

    expert_ids = jnp.arange(expert_count, dtype=jnp.int32)
    slot_ids = jnp.arange(capacity, dtype=jnp.int32)
    plane = (
        jnp.arange(F, dtype=jnp.int32)[:, None] * local_experts
        + seq_at * own_experts
        + jnp.arange(own_experts, dtype=jnp.int32)[None, :]
    ).reshape(-1)
    hit = table_all[:, None, :TOPK] == plane[None, :, None, None]
    plane_slots = jnp.max(jnp.where(hit, table_all[:, None, TOPK:], -1), axis=2)
    one_hot = plane_slots[:, :, None, :] == slot_ids[None, None, :, None]
    select = one_hot.astype(BF).reshape(S, F * own_experts * capacity, tok_count)
    grouped = (S, F, own_experts * capacity, width)
    shape5 = (F, S, own_experts, capacity, width)

    cot_rows = mm("brt,btd->brd", select, cot_all).astype(BF).reshape(grouped)
    residual, ffn_all, g_rows, down_w = line(
        "ffn", sizes, [o_part], [tokens[0], gain_ffn],
        [cot_rows, w_down.reshape((S, own_experts) + w_down.shape[1:])],
        ((("fsdp",), 1, 0), (("seq",), 0, "columns")), 2,
    )
    g_rows = g_rows.reshape(shape5)
    ffn_low = lax.dynamic_index_in_dim(ffn_all, seq_at, 0, keepdims=False)

    route_rows = routes[0]
    slot_rows = slots[0]
    router_scores = dot(ffn_low, full_router)
    picked = route_rows[:, :, None] == expert_ids[None, None, :]
    selected = jnp.sum(jnp.where(picked, router_scores[:, None, :], 0.0), axis=-1)
    gate_prob = jax.nn.softmax(selected, axis=-1)
    gate_table = jnp.sum(jnp.where(picked, gate_prob[:, :, None], 0.0), axis=1).T
    hit = table[None, :TOPK] == expert_ids[:, None, None]
    own_slots = jnp.max(jnp.where(hit, table[None, TOPK:], -1), axis=1)
    gate_slots = jnp.sum(
        jnp.where(
            own_slots[:, None, :] == slot_ids[None, :, None], gate_table[:, None, :], 0.0
        ),
        axis=-1,
    )
    by_device = (F, S, own_experts, capacity)

    def to_devices(values):
        return lanes(values.reshape(by_device).transpose(1, 0, 2, 3).reshape(N, -1), N)

    gate_send = to_devices(gate_slots)

    ffn_rows = mm("brt,btd->brd", select, ffn_all).astype(BF).reshape(grouped)
    x_rows, gate_up_w, gate_got = exchange(
        [ffn_rows, w_gate_up.reshape((S, own_experts) + w_gate_up.shape[1:]), gate_send],
        ((("fsdp",), 1, 0), (("seq",), 0, 0), (EVERY, 0, 0)), sizes, 4,
    )
    gate_up_w = gate_up_w.transpose(1, 0, 2, 3).reshape(own_experts, width, 2 * FF)
    x_rows = x_rows.reshape(shape5)
    row_gate = gate_got.reshape(S, F, -1)[:, :, : own_experts * capacity]
    row_gate = row_gate.transpose(1, 0, 2).reshape(F, S, own_experts, capacity, 1)

    gate_up = mm("asjcd,jdf->asjcf", x_rows, gate_up_w)
    gate_part = gate_up[..., :FF]
    up_part = gate_up[..., FF:]
    hidden_low = (jax.nn.silu(gate_part) * up_part).astype(BF)
    expert_out = mm("asjch,jhd->asjcd", hidden_low, down_w).astype(BF)
    out_wide = expert_out.astype(F32)
    g_wide = g_rows.astype(F32)
    grad_prob_rows = jnp.sum(out_wide * g_wide, axis=-1)
    moe_rows = (row_gate * out_wide).astype(BF)
    grad_eo_low = (row_gate * g_wide).astype(BF)

    grad_hidden_low = mm("asjcd,jhd->asjch", grad_eo_low, down_w).astype(BF)
    grad_hidden = lax.optimization_barrier(grad_hidden_low).astype(F32)
    sigmoid_gate = jax.nn.sigmoid(gate_part)
    grad_gate = grad_hidden * up_part * sigmoid_gate * (1.0 + gate_part * (1.0 - sigmoid_gate))
    grad_up = grad_hidden * gate_part * sigmoid_gate
    grad_gu_low = jnp.concatenate([grad_gate, grad_up], axis=-1).astype(BF)
    grad_rows = mm("asjcf,jdf->asjcd", grad_gu_low, gate_up_w).astype(BF)
    up_term = mm("asjcd,asjcf->jdf", x_rows, grad_gu_low).astype(BF)
    down_term = mm("asjch,asjcd->jhd", hidden_low, grad_eo_low).astype(BF)
    prob_send = grad_prob_rows.reshape(F, S, -1).transpose(1, 0, 2).reshape(N, -1)
    back_layout = grad_rows.reshape(F, S, own_experts * capacity, width)
    up_blocks = up_term.reshape(own_experts, S, part_width, 2 * FF).transpose(1, 0, 2, 3)
    grad_back, up_got, prob_got = exchange(
        [back_layout, up_blocks, lanes(prob_send, N)],
        ((("fsdp",), 0, 1), (("seq",), 0, 0), (EVERY, 0, 0)), sizes, 6,
    )
    grad_gate_up = up_got.reshape(w_gate_up.shape).astype(F32)
    prob_slots = prob_got.reshape(S, F, -1)[:, :, : own_experts * capacity]
    prob_slots = prob_slots.reshape(S, F, own_experts, capacity).transpose(1, 0, 2, 3)
    prob_slots = prob_slots.reshape(expert_count, capacity)

    grad_part = mm("brt,brd->btd", select, grad_back.reshape(S, -1, width)).astype(BF)

    prob_of_route = jnp.einsum(
        "tke,ec->tkc", picked.astype(F32), prob_slots, precision=lax.Precision.HIGHEST
    )
    at_slot = slot_rows[:, :, None] == slot_ids[None, None, :]
    grad_prob = jnp.sum(jnp.where(at_slot, prob_of_route, 0.0), axis=-1)
    grad_selected = gate_prob * (grad_prob - jnp.sum(gate_prob * grad_prob, axis=-1, keepdims=True))
    grad_logits = jnp.sum(jnp.where(picked, grad_selected[:, :, None], 0.0), axis=1).astype(BF)
    grad_ffn_add = mm("te,de->td", grad_logits, full_router)
    grad_router_part = mm("td,te->de", ffn_low, grad_logits)
    valid = (seq_at * tok_count + jnp.arange(tok_count, dtype=jnp.int32)) < lengths[0]
    grad_final = jnp.where(valid[:, None], cotangent[0].astype(F32), 0.0)
    grad_residual, grad_gain_ffn, grad_attn_low, moe_back, down_got = line(
        "grad", sizes, [grad_part], [grad_final, gain_ffn, residual, grad_ffn_add],
        [moe_rows.reshape(F, S, own_experts * capacity, width), down_term],
        ((("fsdp",), 0, 1), (("seq",), "columns", 0)), 7,
    )
    grad_down = down_got.reshape(w_down.shape).astype(F32)
    grad_attn_low = grad_attn_low.reshape(seq_total, width)

    grad_o_low = mm("td,ed->te", grad_attn_low, out_own).astype(BF)
    grad_out_part = mm("te,td->ed", o_low, grad_attn_low).astype(BF)
    grad_proj, grad_gain_heads = attend_back(
        lengths, projected, qkv_low, grad_o_low, cosine, sine, gain_heads, heads
    )
    grad_qkv_part = mm("td,te->de", attn_low, grad_proj).astype(BF).reshape(S, F, w_rows, own_width)
    attn_part = mm("te,de->td", grad_proj, w_proj).astype(BF).reshape(S, tok_count, width)
    moe_part = mm("brt,brd->btd", select, moe_back.reshape(S, -1, width)).astype(BF)
    sums, grad_out_got, grad_qkv_plane = line(
        "sum", sizes, [attn_part, moe_part], [],
        [grad_out_part.reshape(F, -1, width), grad_qkv_part],
        ((("fsdp",), 0, 0), (("fsdp",), 1, 0)), 8,
    )
    grad_attn_norm, moe_out = sums[0], sums[1]
    final = jnp.where(valid[:, None], residual + moe_out, 0.0)
    grad_out = jnp.sum(grad_out_got.astype(F32), axis=0)
    grad_qkv_own = jnp.sum(grad_qkv_plane.astype(F32), axis=0)
    layer_inputs = tokens[0].astype(F32)
    factor = rms_factor(layer_inputs)
    normed = layer_inputs * factor
    scaled = grad_attn_norm * gain_attn
    inner = jnp.mean(scaled * normed, axis=-1, keepdims=True)
    grad_inputs = grad_residual + factor * (scaled - normed * inner)
    grad_gain_attn = jnp.sum(grad_attn_norm * normed, axis=0)

    gain_part = jnp.concatenate([grad_gain_attn, grad_gain_ffn[0], grad_gain_heads.reshape(-1)])
    small_part = jnp.concatenate(
        [grad_router_part.reshape(N, -1), gain_part.reshape(N, -1)], axis=1
    )
    small_got, grad_qkv_got = exchange(
        [lanes(small_part, N), grad_qkv_own], ((EVERY, 0, 0), (("seq",), 0, 0)), sizes, 10
    )
    grad_qkv = whole_columns(grad_qkv_got)
    small_sum = jnp.sum(small_got, axis=0).reshape(-1)
    grad_router = small_sum[:router_size].reshape(w_router.shape)
    grad_gains = small_sum[router_size : router_size + small]
    return (
        final.astype(BF)[None],
        grad_inputs[None],
        grad_qkv,
        grad_out,
        grad_router,
        grad_gains,
        grad_gate_up,
        grad_down,
    )


def solution(mesh):
    in_specs = (
        P("fsdp", "seq", None),
        P("fsdp", "seq", None),
        P("fsdp"),
        P("fsdp", "seq", None),
        P("fsdp", "seq", None),
        P(("seq", "fsdp"), None),
        P(("seq", "fsdp"), None),
        P(("seq", "fsdp"), None),
        P(("seq", "fsdp")),
        P("fsdp", "seq", None),
        P("fsdp", None, "seq"),
    )
    out_specs = (
        P("fsdp", "seq", None),
        P("fsdp", "seq", None),
        P(("seq", "fsdp"), None),
        P(("seq", "fsdp"), None),
        P(("seq", "fsdp"), None),
        P(("seq", "fsdp")),
        P("fsdp", "seq", None),
        P("fsdp", None, "seq"),
    )
    return jax.shard_map(
        per_device, mesh=mesh, in_specs=in_specs, out_specs=out_specs, check_vma=False
    )
```

profile of v0, /device:TPU:0, one launch (start us, length us, event | category | flops | bytes accessed | tf_op | source)
XLA Modules:
  0.0 1398.2 jit_solution(11932625338350173392)
XLA Ops:
  4.2 205.8 %entry.1 = (bf16[4,256,2048]{2,1,0:T(8,128)(2,1)}, bf16[4,256,2048]{2,1,0:T(8,128)(2,1)}, s32[4,16,256]{2,1,0:T(8,128)}, bf16[4,8,64,1280]{3,2,1,0:T(8,128)(2,1)...) custom-call(bf16[256,2048]{1,0:T(8,128)(2,1)} %bitcast.236, bf16[256,2048]{1,0:T(8,128)(2,1)} %bitcast.245, ...), custom_call_target="tpu_custom_call" | custom-call | tf_op jit(solution)/shard_map/entry/pallas_call | solution.py:331
  218.3 7.5 fusion.76.proj_ref
  230.4 30.6 %attend.1 = (bf16[1024,1280]{1,0:T(8,128)(2,1)}, bf16[1024,1024]{1,0:T(8,128)(2,1)}) custom-call(s32[1]{0:T(128)} %copy.112.length_ref, f32[1024,1280]{1,0:T(8,128)} %fusion.76.proj_ref, f32[1024,128]{1,0:T(8,128)} %get-tuple-element.130.cos_ref, f32[1024,128]{1,0:T(8,128)} %get-tuple-element.131.sin_ref, f32[2,128]{1,0:T(2,128)} %slice_convert_fusion.gains_ref), custom_call_target="tpu_custom_call" | custom-call | flops 4294967296 | bytes 10485760 | tf_op jit(solution)/shard_map/attend/pallas_call | solution.py:618
  261.0 7.6 convolution_convert_fusion.8
  269.3 8.1 convolution_convert_fusion.3
  277.4 188.8 %line_ffn.1 = (f32[256,2048]{1,0:T(8,128)}, bf16[4,256,2048]{2,1,0:T(8,128)(2,1)}, bf16[8,4,80,2048]{3,2,1,0:T(8,128)(2,1)}, bf16[1,768,2048]{2,1,0:T(8,128)(2,1)}) custom-call(bf16[4,256,2048]{2,1,0:T(8,128)(2,1)} %bitcast.248, bf16[256,2048]{1,0:T(8,128)(2,1)} %bitcast.237, f32[1,2048]{1,0:T(1,128)} %bitcast.267, bf16[4,8,80,2048]{3,2,1,0:T(8,128)(2,1)} %bitcast.234, ...), custom_call_target="tpu_custom_call" | custom-call | tf_op jit(solution)/shard_map/line_ffn/pallas_call | solution.py:552
  471.3 8.2 convolution_convert_fusion.2
  479.5 146.6 %exchange_4.1 = (bf16[8,4,80,2048]{3,2,1,0:T(8,128)(2,1)}, bf16[4,1,512,1536]{3,2,1,0:T(8,128)(2,1)}, f32[32,16,128]{2,1,0:T(8,128)}) custom-call(bf16[4,8,80,2048]{3,2,1,0:T(8,128)(2,1)} %bitcast.235, bf16[4,1,512,1536]{3,2,1,0:T(8,128)(2,1)} %bitcast.238, f32[32,16,128]{2,1,0:T(8,128)} %bitcast.254), custom_call_target="tpu_custom_call" | custom-call | tf_op jit(solution)/shard_map/exchange_4/pallas_call | solution.py:137
  627.3 12.5 convert_bitcast_fusion.3
  639.8 19.8 %convolution_bitcast_fusion = f32[8,4,1,80,1536]{4,3,1,0,2:T(8,128)S(1)} fusion(bf16[2048,1536,1,1]{1,0,3,2:T(8,128)(2,1)S(1)} %bitcast.292, bf16[8,4,80,2048]{3,2,1,0:T(8,128)(2,1)} %get-tuple-element.52), kind=kOutput, calls=%fused_computation.31 | convolution fusion | flops 16106127360 | bytes 32505856 | tf_op jit(solution)/shard_map/asjcd,jdf->asjcf/dot_general | solution.py:744
  659.6 6.8 fusion.20
  666.4 17.2 %fusion.5 = (bf16[8,4,80,2048]{3,2,1,0:T(8,128)(2,1)}, f32[8,4,80]{2,1,0:T(4,128)S(1)}) fusion(f32[8,4,80]{2,1,0:T(4,128)S(1)} %bitcast.279, bf16[8,4,80,2048]{3,2,1,0:T(8,128)(2,1)} %get-tuple-element.51, bf16[8,4,1,80,768]{4,3,1,0,2:T(8,128)(2,1)S(1)} %get-tuple-element.112, bf16[1,768,2048]{2,1,0:T(8,128)(2,1)} %get-tuple-element.49), kind=kOutput, calls=%fused_computation.9 | convolution fusion | flops 8089761280 | bytes 28069888 | tf_op jit(solution)/shard_map/asjch,jhd->asjcd/dot_general | solution.py:744
  684.4 22.5 %bitcast_convert_fusion = bf16[2048,1536]{1,0:T(8,128)(2,1)} fusion(bf16[8,4,80,2048]{3,2,1,0:T(8,128)(2,1)} %get-tuple-element.52, bf16[8,4,80,768]{3,2,1,0:T(8,128)(2,1)} %get-tuple-element.111, bf16[8,4,80,768]{3,2,1,0:T(8,128)(2,1)} %get-tuple-element.110), kind=kOutput, calls=%fused_computation.8 | convolution fusion | flops 16125001728 | bytes 24641536 | tf_op jit(solution)/shard_map/asjcd,asjcf->jdf/dot_general | solution.py:744
  706.9 21.4 %convert_bitcast_fusion.2.refs_0_ = bf16[8,4,80,2048]{3,2,1,0:T(8,128)(2,1)} fusion(bf16[2048,1536,1,1]{1,0,3,2:T(8,128)(2,1)} %bitcast.289, bf16[8,4,80,768]{3,2,1,0:T(8,128)(2,1)S(1)} %copy-done.12, bf16[8,4,80,768]{3,2,1,0:T(8,128)(2,1)S(1)} %copy-done.11), kind=kOutput, calls=%fused_computation.11 | convolution fusion | flops 16127098880 | bytes 24641536 | tf_op jit(solution)/shard_map/asjcf,jdf->asjcd/dot_general | solution.py:744
  728.4 147.0 %exchange_6.1 = (bf16[4,8,80,2048]{3,2,1,0:T(8,128)(2,1)}, bf16[4,1,512,1536]{3,2,1,0:T(8,128)(2,1)}, f32[32,16,128]{2,1,0:T(8,128)}) custom-call(bf16[8,4,80,2048]{3,2,1,0:T(8,128)(2,1)} %convert_bitcast_fusion.2.refs_0_, bf16[4,1,512,1536]{3,2,1,0:T(8,128)(2,1)} %bitcast.239, f32[32,16,128]{2,1,0:T(8,128)} %bitcast.253), custom_call_target="tpu_custom_call" | custom-call | tf_op jit(solution)/shard_map/exchange_6/pallas_call | solution.py:137
  879.3 13.9 fusion.27.refs_6_
  895.0 9.5 convolution_convert_fusion.5.refs_0_
  906.2 190.8 %line_grad.1 = (f32[256,2048]{1,0:T(8,128)}, f32[1,2048]{1,0:T(1,128)}, bf16[4,256,2048]{2,1,0:T(8,128)(2,1)}, bf16[4,8,80,2048]{3,2,1,0:T(8,128)(2,1)}, bf16[4,1,768,512]{3,2,1,0:T(8,128)(2,1)}) custom-call(bf16[4,256,2048]{2,1,0:T(8,128)(2,1)} %convolution_convert_fusion.5.refs_0_, f32[256,2048]{1,0:T(8,128)} %convert_select_fusion.refs_1_, ...), custom_call_target="tpu_custom_call" | custom-call | tf_op jit(solution)/shard_map/line_grad/pallas_call | solution.py:552
  1097.0 8.1 convolution_convert_fusion.9.grad_ref
  1105.1 37.4 %attend_back.1 = (bf16[1024,1280]{1,0:T(8,128)(2,1)}, f32[2,128]{1,0:T(2,128)}) custom-call(s32[1]{0:T(128)} %copy.112.length_ref, f32[1024,1280]{1,0:T(8,128)} %fusion.76.proj_ref, bf16[1024,1280]{1,0:T(8,128)(2,1)} %get-tuple-element.46.low_ref.kv_ref, bf16[1024,1280]{1,0:T(8,128)(2,1)} %get-tuple-element.46.low_ref.kv_ref, ...), custom_call_target="tpu_custom_call" | custom-call | flops 10737418240 | bytes 13107200 | tf_op jit(solution)/shard_map/attend_back/pallas_call | solution.py:707
  1144.3 7.5 convolution_convert_fusion
  1163.5 7.2 convolution_convert_fusion.6
  1170.7 156.2 %line_sum.1 = (f32[2,256,2048]{2,1,0:T(8,128)}, bf16[8,128,2048]{2,1,0:T(8,128)(2,1)}, bf16[8,4,64,1280]{3,2,1,0:T(8,128)(2,1)}) custom-call(bf16[4,256,2048]{2,1,0:T(8,128)(2,1)} %bitcast.244, bf16[4,256,2048]{2,1,0:T(8,128)(2,1)} %convolution_convert_fusion.4.refs_1_, bf16[8,128,2048]{2,1,0:T(8,128)(2,1)} %bitcast.243, bf16[4,8,64,1280]{3,2,1,0:T(8,128)(2,1)} %bitcast.242), custom_call_target="tpu_custom_call" | custom-call | tf_op jit(solution)/shard_map/line_sum/pallas_call | solution.py:552
  1334.9 39.1 %exchange_10.1 = (f32[32,32,128]{2,1,0:T(8,128)}, f32[4,64,1280]{2,1,0:T(8,128)}) custom-call(f32[32,32,128]{2,1,0:T(8,128)} %bitcast.250, f32[4,64,1280]{2,1,0:T(8,128)} %convert_reduce_fusion.refs_1_), custom_call_target="tpu_custom_call" | custom-call | tf_op jit(solution)/shard_map/exchange_10/pallas_call | solution.py:137
  (180 shorter events, 75.8 us)
Async XLA Ops:
  230.4 30.6 %copy-start.31 = (bf16[8,128,2048]{2,1,0:T(8,128)(2,1)S(1)}, bf16[8,128,2048]{2,1,0:T(8,128)(2,1)}, u32[]{:S(2)}) copy-start(bf16[8,128,2048]{2,1,0:T(8,128)(2,1)} %get-tuple-element.42) | copy-start | bytes 12582916
  269.3 202.0 %copy-start.4 = (pred[4,640,256]{2,1,0:T(32,128)(4,1)}, pred[4,640,256]{2,1,0:T(32,128)(4,1)S(1)}, u32[]{:S(2)}) copy-start(pred[4,640,256]{2,1,0:T(32,128)(4,1)S(1)} %bitcast_compare_fusion) | copy-start | bytes 1966084
  277.4 191.1 %copy-start.18 = (s32[1,256,8]{1,2,0:T(8,128)S(1)}, s32[1,256,8]{1,2,0:T(8,128)}, u32[]{:S(2)}) copy-start(s32[1,256,8]{1,2,0:T(8,128)} %param.14) | copy-start | bytes 24580
  277.4 192.4 %copy-start.21 = (s32[1,256,8]{1,2,0:T(8,128)S(1)}, s32[1,256,8]{1,2,0:T(8,128)}, u32[]{:S(2)}) copy-start(s32[1,256,8]{1,2,0:T(8,128)} %param.15) | copy-start | bytes 24580
  466.6 12.9 copy-start.6
  626.1 13.7 slice-start.5
  666.4 17.2 %copy-start.10 = (bf16[8,4,1,80,768]{4,3,1,0,2:T(8,128)(2,1)}, bf16[8,4,1,80,768]{4,3,1,0,2:T(8,128)(2,1)S(1)}, u32[]{:S(2)}) copy-start(bf16[8,4,1,80,768]{4,3,1,0,2:T(8,128)(2,1)S(1)} %get-tuple-element.112) | copy-start | bytes 11796484
  684.4 22.5 %copy-start.11 = (bf16[8,4,80,768]{3,2,1,0:T(8,128)(2,1)S(1)}, bf16[8,4,80,768]{3,2,1,0:T(8,128)(2,1)}, u32[]{:S(2)}) copy-start(bf16[8,4,80,768]{3,2,1,0:T(8,128)(2,1)} %get-tuple-element.110) | copy-start | bytes 11796484
  684.4 22.5 %copy-start.12 = (bf16[8,4,80,768]{3,2,1,0:T(8,128)(2,1)S(1)}, bf16[8,4,80,768]{3,2,1,0:T(8,128)(2,1)}, u32[]{:S(2)}) copy-start(bf16[8,4,80,768]{3,2,1,0:T(8,128)(2,1)} %get-tuple-element.111) | copy-start | bytes 11796484
  728.4 148.1 %copy-start.19 = (s32[1,256,8]{1,2,0:T(8,128)S(1)}, s32[1,256,8]{1,2,0:T(8,128)}, u32[]{:S(2)}) copy-start(s32[1,256,8]{1,2,0:T(8,128)} %param.14) | copy-start | bytes 24580
  728.4 148.1 %copy-start.22 = (s32[1,256,8]{1,2,0:T(8,128)S(1)}, s32[1,256,8]{1,2,0:T(8,128)}, u32[]{:S(2)}) copy-start(s32[1,256,8]{1,2,0:T(8,128)} %param.15) | copy-start | bytes 24580
  728.4 148.6 %copy-start.15 = (f32[256,8]{0,1:T(8,128)S(1)}, f32[256,8]{0,1:T(8,128)}, u32[]{:S(2)}) copy-start(f32[256,8]{0,1:T(8,128)} %copy-done.14) | copy-start | bytes 24580
  728.4 148.6 %copy-start.24 = (f32[256]{0:T(256)S(1)}, f32[256]{0:T(256)}, u32[]{:S(2)}) copy-start(f32[256]{0:T(256)} %copy-done.23) | copy-start | bytes 3076
  728.4 148.6 %copy-start.26 = (f32[256]{0:T(256)S(1)}, f32[256]{0:T(256)}, u32[]{:S(2)}) copy-start(f32[256]{0:T(256)} %copy-done.25) | copy-start | bytes 3076
  879.3 13.9 copy-start.7
  879.3 15.8 %copy-start.5 = (pred[4,640,256]{2,1,0:T(32,128)(4,1)S(1)}, pred[4,640,256]{2,1,0:T(32,128)(4,1)}, u32[]{:S(2)}) copy-start(pred[4,640,256]{2,1,0:T(32,128)(4,1)} %copy-done.4) | copy-start | bytes 1966084
  906.2 190.8 %copy-start.32 = (bf16[8,128,2048]{2,1,0:T(8,128)(2,1)S(1)}, bf16[8,128,2048]{2,1,0:T(8,128)(2,1)}, u32[]{:S(2)}) copy-start(bf16[8,128,2048]{2,1,0:T(8,128)(2,1)} %get-tuple-element.42) | copy-start | bytes 12582916
  1105.1 37.4 %copy-start.27 = (f32[1,2,4,128]{3,2,1,0:T(4,128)S(1)}, f32[1,2,4,128]{3,2,1,0:T(4,128)}, u32[]{:S(2)}) copy-start(f32[1,2,4,128]{3,2,1,0:T(4,128)} %get-tuple-element.128) | copy-start | bytes 12292
  1105.1 37.4 %copy-start.1 = (bf16[4,256,2048]{2,1,0:T(8,128)(2,1)S(1)}, bf16[4,256,2048]{2,1,0:T(8,128)(2,1)}, u32[]{:S(2)}) copy-start(bf16[4,256,2048]{2,1,0:T(8,128)(2,1)} %get-tuple-element.38) | copy-start | bytes 12582916
  1105.1 37.4 %copy-start.17 = (f32[2048]{0:T(1024)S(1)}, f32[2048]{0:T(1024)}, u32[]{:S(2)}) copy-start(f32[2048]{0:T(1024)} %copy-done.16) | copy-start | bytes 24580
  1142.6 15.8 %slice-start.2 = ((s8[10485760]{0:T(1024)(128)(4,1)}), s8[4194304]{0:T(1024)(128)(4,1)S(1)}, s32[]{:S(2)}) async-start(s8[10485760]{0:T(1024)(128)(4,1)} %bitcast.285), calls=%async_computation.2 | async-start | bytes 8388608
  1144.3 14.1 %slice-start.3 = ((s8[10485760]{0:T(1024)(128)(4,1)}), s8[4194304]{0:T(1024)(128)(4,1)S(1)}, s32[]{:S(2)}) async-start(s8[10485760]{0:T(1024)(128)(4,1)} %bitcast.285), calls=%async_computation.3 | async-start | bytes 8388608
  1144.3 14.1 %slice-start.4 = ((s8[10485760]{0:T(1024)(128)(4,1)}), s8[2097152]{0:T(1024)(128)(4,1)S(1)}, s32[]{:S(2)}) async-start(s8[10485760]{0:T(1024)(128)(4,1)} %bitcast.285), calls=%async_computation.4 | async-start | bytes 4194304
  1170.7 156.2 %copy-start.2 = (bf16[1,256,2048]{2,1,0:T(8,128)(2,1)S(1)}, bf16[1,256,2048]{2,1,0:T(8,128)(2,1)}, u32[]{:S(2)}) copy-start(bf16[1,256,2048]{2,1,0:T(8,128)(2,1)} %param.11) | copy-start | bytes 3145732
  (22 other events, 121.1 us)
where the time goes:
time: 1410 us; the launch traced here: 1400 us
  Pallas kernels  1140 us (81%)
  matrix products  189 us (13%)
  other arithmetic  48.1 us (3%)
  local copies, waits for them, and re-layouts  16.9 us (1%)
    pallas_call x3, Pallas kernels, line(): pl.pallas_call(functools.partial(line_kernel, sizes, chunks, mode, len(pa...  536 us
    pallas_call x3, Pallas kernels, exchange(): pl.pallas_call(functools.partial(exchange_kernel, sizes, specs), out_shap...  333 us
    pallas_call x1, Pallas kernels, entry(): pl.pallas_call(functools.partial(entry_kernel, sizes), out_shape=[line_ou...  206 us
    dot_general x16, matrix products, mm(): return jnp.einsum(form, left, right, preferred_element_type=F32)  171 us
    pallas_call x1, Pallas kernels, attend_back(): pl.pallas_call(functools.partial(attend_back_kernel, heads, blocks), grid...  37.4 us
    pallas_call x1, Pallas kernels, attend(): pl.pallas_call(functools.partial(attend_kernel, heads, blocks), grid=(blo...  30.6 us

commit v1 on v0

--- a/solution.py
+++ b/solution.py
@@ -68,15 +68,16 @@
         self.own, self.away = [], []
         if not specs:
             return
-        send_sem, recv_sem, own_sem = sems
+        send_sem, recv_sem, own_sem, *stages = sems
         for i, (axes, before, after) in enumerate(specs):
             me = index_of(sizes, axes)
             total = count_of(sizes, axes)
+            source = block_of(sources[i], before, me, total)
+            result = block_of(results[i], after, me, total)
             self.own.append(
-                pltpu.make_async_copy(
-                    block_of(sources[i], before, me, total),
-                    block_of(results[i], after, me, total),
-                    own_sem.at[i],
+                (
+                    pltpu.make_async_copy(source, stages[i], own_sem.at[i, 0]),
+                    pltpu.make_async_copy(stages[i], result, own_sem.at[i, 1]),
                 )
             )
             for step in range(1, total):
@@ -93,19 +94,35 @@
                 )
 
     def start(self):
-        for copy in self.own + self.away:
+        for copy in self.away:
             copy.start()
+        for inward, _ in self.own:
+            inward.start()
 
     def wait(self):
-        for copy in self.own + self.away:
+        for inward, outward in self.own:
+            inward.wait()
+            outward.start()
+        for _, outward in self.own:
+            outward.wait()
+        for copy in self.away:
             copy.wait()
 
 
-def block_sems(sizes, specs):
+def block_scratch(sizes, arrays, specs):
     if not specs:
         return []
     total = max(count_of(sizes, axes) for axes, _, _ in specs)
-    return [DMA((len(specs), total)), DMA((len(specs), total)), DMA((len(specs),))]
+    stages = []
+    for array, (axes, before, after) in zip(arrays, specs):
+        shape = list(array.shape)
+        if before == "columns":
+            shape[-1] //= count_of(sizes, axes)
+        else:
+            del shape[before]
+        stages.append(pltpu.VMEM(tuple(shape), array.dtype))
+    count = len(specs)
+    return [DMA((count, total)), DMA((count, total)), DMA((count, 2))] + stages
 
 
 def block_outs(sizes, arrays, specs):
@@ -139,7 +156,7 @@
         out_shape=block_outs(sizes, arrays, specs),
         in_specs=[ANY] * count,
         out_specs=[ANY] * count,
-        scratch_shapes=block_sems(sizes, specs),
+        scratch_shapes=block_scratch(sizes, arrays, specs),
         compiler_params=pltpu.CompilerParams(collective_id=collective_id, has_side_effects=True),
         name=f"exchange_{collective_id}",
     )(*arrays)
@@ -149,7 +166,7 @@
     sizes, tok_ref, cot_ref, table_ref, wqkv_ref, wout_ref, small_ref,
     tok_out, cot_out, table_out, wq_out, wo_out, small_out,
     tok_send, tok_recv, tab_send, tab_recv, wq_zsend, wq_zrecv,
-    pl_send, pl_recv, sib_send, sib_recv, sm_send, sm_recv, own_sem,
+    pl_send, pl_recv, sib_send, sib_recv, sm_send, sm_recv, own_sem, *stages,
 ):
     S, F = sizes["seq"], sizes["fsdp"]
     s = lax.axis_index("seq")
@@ -171,22 +188,25 @@
     def columns(z, p):
         return pl.ds(pl.multiple_of(starts[p] + z * widths[p], 128), widths[p])
 
-    own = [
-        pltpu.make_async_copy(tok_ref, tok_out.at[s], own_sem.at[0]),
-        pltpu.make_async_copy(table_ref, table_out.at[s], own_sem.at[1]),
-        pltpu.make_async_copy(wout_ref, wo_out.at[f], own_sem.at[2]),
-        pltpu.make_async_copy(small_ref, small_out.at[me], own_sem.at[3]),
-        pltpu.make_async_copy(cot_ref, cot_out.at[s], own_sem.at[4]),
+    pairs = [
+        (wqkv_ref.at[:, columns(s, p)], wq_out.at[s, f, :, pl.ds(offsets[p], widths[p])])
+        for p in range(3)
+    ] + [
+        (wout_ref, wo_out.at[f]),
+        (tok_ref, tok_out.at[s]),
+        (cot_ref, cot_out.at[s]),
+        (table_ref, table_out.at[s]),
+        (small_ref, small_out.at[me]),
     ]
-    for p in range(3):
-        own.append(
-            pltpu.make_async_copy(
-                wqkv_ref.at[:, columns(s, p)],
-                wq_out.at[s, f, :, pl.ds(offsets[p], widths[p])],
-                own_sem.at[5 + p],
-            )
-        )
-    for copy in own:
+    inward = [
+        pltpu.make_async_copy(source, stages[i], own_sem.at[i, 0])
+        for i, (source, _) in enumerate(pairs)
+    ]
+    outward = [
+        pltpu.make_async_copy(stages[i], result, own_sem.at[i, 1])
+        for i, (_, result) in enumerate(pairs)
+    ]
+    for copy in inward:
         copy.start()
     met()
 
@@ -285,9 +305,13 @@
                       place_of(sizes, EVERY, target))
         copy.start()
         smalls.append(copy)
-    for copy in own:
+    for i, copy in enumerate(inward):
+        copy.wait()
+        outward[i].start()
+    for copy in outward[:3]:
         copy.wait()
     spread(0)
+    outward[3].wait()
     spread(S)
     relay(0, 1)
     depart(1)
@@ -311,6 +335,8 @@
                 @pl.when((s > 0) & (s <= S - hop))
                 def _():
                     along(a, s, c, 1, hop).wait_send()
+    for copy in outward[4:]:
+        copy.wait()
     for slot in range(S + 1):
         for step in range(1, chips):
             to_chip(slot, step).wait_send()
@@ -328,6 +354,20 @@
     own_width = w_qkv.shape[1] // S
     N = S * F
     line_out = jax.ShapeDtypeStruct((S,) + tokens.shape, tokens.dtype)
+    q_width, kv = QH * HD // S, KH * HD // S
+    stages = [
+        pltpu.VMEM(shape, dtype)
+        for shape, dtype in [
+            ((w_qkv.shape[0], q_width), BF),
+            ((w_qkv.shape[0], kv), BF),
+            ((w_qkv.shape[0], kv), BF),
+            (w_out.shape, BF),
+            (tokens.shape, BF),
+            (cotangent.shape, BF),
+            (table.shape, table.dtype),
+            (small.shape, BF),
+        ]
+    ]
     return pl.pallas_call(
         functools.partial(entry_kernel, sizes),
         out_shape=[
@@ -343,8 +383,8 @@
         scratch_shapes=[
             DMA((2, 2, chunks, S)), DMA((2, 2, chunks, S)), DMA((S,)), DMA((S,)),
             DMA((S, 3)), DMA((S, 3)), DMA((S + 1, F // 2)), DMA((S + 1, F // 2)),
-            DMA((S + 1, F // 2)), DMA((S + 1, F // 2)), DMA((N,)), DMA((N,)), DMA((8,)),
-        ],
+            DMA((S + 1, F // 2)), DMA((S + 1, F // 2)), DMA((N,)), DMA((N,)), DMA((8, 2)),
+        ] + stages,
         compiler_params=pltpu.CompilerParams(collective_id=collective_id, has_side_effects=True),
         name="entry",
     )(tokens, cotangent, table, w_qkv, w_out, small)
@@ -554,7 +594,7 @@
         out_shape=outs + block_outs(sizes, extras, specs),
         in_specs=[VM] * (len(parts) + len(others)) + [ANY] * len(extras),
         out_specs=out_specs + [ANY] * len(extras),
-        scratch_shapes=scratch + sems + block_sems(sizes, specs),
+        scratch_shapes=scratch + sems + block_scratch(sizes, extras, specs),
         compiler_params=pltpu.CompilerParams(
             collective_id=collective_id, has_side_effects=True, vmem_limit_bytes=56 << 20
         ),
@@ -567,7 +607,9 @@
 
 
 def softmax_block(query, keys, first_row, length, scale):
-    scores = lax.dot_general(query, keys, (((1,), (1,)), ((), ())), preferred_element_type=F32) * scale
+    scores = lax.dot_general(
+        query, keys, (((1,), (1,)), ((), ())), preferred_element_type=F32
+    ) * scale
     row = first_row + lax.broadcasted_iota(jnp.int32, scores.shape, 0)
     column = lax.broadcasted_iota(jnp.int32, scores.shape, 1)
     scores = jnp.where((column <= row) & (column < length), scores, MASKED)
@@ -576,72 +618,132 @@
     return weights * (1.0 / jnp.sum(weights, axis=-1, keepdims=True))
 
 
-def attend_kernel(heads, blocks, length_ref, proj_ref, cos_ref, sin_ref, gains_ref, low_ref, out_ref, k_all, v_all):
+def tiles(width, step, body):
+    @pl.loop(0, width // step)
+    def _(n):
+        body(pl.ds(pl.multiple_of(n * step, step), step))
+
+
+def attend_kernel(sizes, heads, blocks, specs, *refs):
+    count = len(specs)
+    length_ref, tok_ref, gain_ref, wq_ref, cos_ref, sin_ref, gains_ref, wo_ref = refs[:8]
+    sources = refs[8 : 8 + count]
+    attn_ref, proj_ref, low_ref, out_ref, part_ref = refs[8 + count : 13 + count]
+    results = refs[13 + count : 13 + 2 * count]
+    k_all, v_all, *sems = refs[13 + 2 * count :]
     step = pl.program_id(0)
-    rows = proj_ref.shape[0]
+
+    @pl.when(step == 0)
+    def _():
+        greet(sizes)()
+        Blocks(sizes, specs, sources, results, sems).start()
+
+    rows, width = proj_ref.shape
     length = length_ref[0]
     cosine = cos_ref[...]
     sine = sin_ref[...]
     q_gain = gains_ref[0:1, :]
     k_gain = gains_ref[1:2, :]
     scale = HD ** (-0.5)
+    value = tok_ref[...].astype(F32)
+    factor = lax.rsqrt(jnp.mean(value * value, axis=-1, keepdims=True) + EPSILON)
+    attn_ref[...] = (value * factor * gain_ref[...]).astype(BF)
+
+    def project(at):
+        proj_ref[:, at] = jnp.dot(attn_ref[...], wq_ref[:, at], preferred_element_type=F32)
+
+    tiles(width, 256, project)
 
     def normed(raw, gain):
         factor = lax.rsqrt(jnp.mean(raw * raw, axis=-1, keepdims=True) + EPSILON)
         return turn(raw * factor * gain, cosine, sine).astype(BF)
 
     key = normed(proj_ref[:, heads * HD : (heads + 1) * HD], k_gain)
-    value = proj_ref[:, (heads + 1) * HD :].astype(BF)
+    value_low = proj_ref[:, (heads + 1) * HD :].astype(BF)
     low_ref[:, heads * HD : (heads + 1) * HD] = key
-    low_ref[:, (heads + 1) * HD :] = value
+    low_ref[:, (heads + 1) * HD :] = value_low
     here = pl.ds(pl.multiple_of(step * rows, rows), rows)
     k_all[here, :] = key
-    v_all[here, :] = value
+    v_all[here, :] = value_low
     for block in range(blocks):
         @pl.when(step == block)
         def _():
-            width = (block + 1) * rows
-
-            @pl.loop(0, heads)
-            def _(h):
-                column = pl.ds(pl.multiple_of(h * HD, HD), HD)
+            reach = (block + 1) * rows
+
+            def one(column):
                 query = normed(proj_ref[:, column], q_gain)
                 low_ref[:, column] = query
-                probs = softmax_block(query, k_all[:width, :], block * rows, length, scale)
-                mixed = jnp.dot(probs.astype(BF), v_all[:width, :], preferred_element_type=F32)
+                probs = softmax_block(query, k_all[:reach, :], block * rows, length, scale)
+                mixed = jnp.dot(probs.astype(BF), v_all[:reach, :], preferred_element_type=F32)
                 out_ref[:, column] = mixed.astype(BF)
 
-
-def attend(length, projected, cosine, sine, gains, heads, blocks=4):
-    total, width = projected.shape
+            tiles(heads * HD, HD, one)
+
+    def leave(at):
+        part_ref[:, at] = jnp.dot(
+            out_ref[...], wo_ref[:, at], preferred_element_type=F32
+        ).astype(BF)
+
+    tiles(part_ref.shape[1], 256, leave)
+
+    @pl.when(step == blocks - 1)
+    def _():
+        Blocks(sizes, specs, sources, results, sems).wait()
+
+
+def attend(
+    length, tokens, gain, w_proj, cosine, sine, gains, w_out, heads, extras, specs, sizes,
+    collective_id, blocks=4,
+):
+    total, width = tokens.shape
+    own_width = w_proj.shape[1]
     rows = total // blocks
+    q_width = heads * HD
+
+    def by_rows(columns):
+        return pl.BlockSpec((rows, columns), lambda i: (i, 0))
+
+    def whole(array):
+        return pl.BlockSpec(array.shape, lambda i: (0, 0), pipeline_mode=pl.Buffered(1))
+
     return pl.pallas_call(
-        functools.partial(attend_kernel, heads, blocks),
+        functools.partial(attend_kernel, sizes, heads, blocks, specs),
         grid=(blocks,),
         out_shape=[
             jax.ShapeDtypeStruct((total, width), BF),
-            jax.ShapeDtypeStruct((total, heads * HD), BF),
-        ],
+            jax.ShapeDtypeStruct((total, own_width), F32),
+            jax.ShapeDtypeStruct((total, own_width), BF),
+            jax.ShapeDtypeStruct((total, q_width), BF),
+            jax.ShapeDtypeStruct((total, width), BF),
+        ] + block_outs(sizes, extras, specs),
         in_specs=[
             pl.BlockSpec(memory_space=pltpu.SMEM),
-            pl.BlockSpec((rows, width), lambda i: (i, 0)),
-            pl.BlockSpec((rows, HD), lambda i: (i, 0)),
-            pl.BlockSpec((rows, HD), lambda i: (i, 0)),
-            pl.BlockSpec((2, HD), lambda i: (0, 0)),
-        ],
-        out_specs=[
-            pl.BlockSpec((rows, width), lambda i: (i, 0)),
-            pl.BlockSpec((rows, heads * HD), lambda i: (i, 0)),
-        ],
-        scratch_shapes=[pltpu.VMEM((total, HD), BF), pltpu.VMEM((total, HD), BF)],
-        compiler_params=pltpu.CompilerParams(vmem_limit_bytes=56 << 20),
-        cost_estimate=pl.CostEstimate(flops=4 * heads * total * total * HD, bytes_accessed=total * width * 8, transcendentals=heads * total * total),
+            by_rows(width),
+            whole(gain),
+            whole(w_proj),
+            by_rows(HD),
+            by_rows(HD),
+            whole(gains),
+            whole(w_out),
+        ] + [ANY] * len(extras),
+        out_specs=[by_rows(width), by_rows(own_width), by_rows(own_width), by_rows(q_width), by_rows(width)]
+        + [ANY] * len(extras),
+        scratch_shapes=[pltpu.VMEM((total, HD), BF), pltpu.VMEM((total, HD), BF)]
+        + block_scratch(sizes, extras, specs),
+        compiler_params=pltpu.CompilerParams(
+            collective_id=collective_id, has_side_effects=True, vmem_limit_bytes=58 << 20
+        ),
         name="attend",
-    )(length, projected, cosine, sine, gains)
-
-
-def attend_back_kernel(heads, blocks, length_ref, proj_ref, low_ref, kv_ref, grad_ref, cos_ref, sin_ref, gains_ref,
-                       out_ref, gains_out, gk_all, gv_all):
+    )(length, tokens, gain, w_proj, cosine, sine, gains, w_out, *extras)
+
+
+def attend_back_kernel(sizes, heads, blocks, specs, *refs):
+    count = len(specs)
+    length_ref, proj_ref, low_ref, kv_ref, grad_ref, wo_ref, wq_ref, cos_ref, sin_ref, gains_ref = refs[:10]
+    sources = refs[10 : 10 + count]
+    out_ref, part_ref, gains_out = refs[10 + count : 13 + count]
+    results = refs[13 + count : 13 + 2 * count]
+    gk_all, gv_all, go_ref, *sems = refs[13 + 2 * count :]
     step = pl.program_id(0)
     rows = proj_ref.shape[0]
     length = length_ref[0]
@@ -662,36 +764,46 @@
 
     @pl.when(step == 0)
     def _():
+        greet(sizes)()
+        Blocks(sizes, specs, sources, results, sems).start()
         gk_all[...] = jnp.zeros_like(gk_all)
         gv_all[...] = jnp.zeros_like(gv_all)
         gains_out[...] = jnp.zeros_like(gains_out)
 
+    def arrive(at):
+        go_ref[:, at] = lax.dot_general(
+            grad_ref[...], wo_ref[at, :], (((1,), (1,)), ((), ())), preferred_element_type=F32
+        ).astype(BF)
+
+    tiles(heads * HD, 256, arrive)
     for block in range(blocks):
         @pl.when(block_at == block)
         def _():
-            width = (block + 1) * rows
-            keys = kv_ref[:width, :HD]
-            values = kv_ref[:width, HD:]
-
-            @pl.loop(0, heads)
-            def _(h):
-                column = pl.ds(pl.multiple_of(h * HD, HD), HD)
+            reach = (block + 1) * rows
+            keys = kv_ref[:reach, :HD]
+            values = kv_ref[:reach, HD:]
+
+            def one(column):
                 query = low_ref[:, column]
-                grad_o = grad_ref[:, column]
+                grad_o = go_ref[:, column]
                 probs = softmax_block(query, keys, block * rows, length, scale)
-                grad_p = lax.dot_general(grad_o, values, (((1,), (1,)), ((), ())), preferred_element_type=F32)
+                grad_p = lax.dot_general(
+                    grad_o, values, (((1,), (1,)), ((), ())), preferred_element_type=F32
+                )
                 inner = jnp.sum(probs * grad_p, axis=-1, keepdims=True)
                 grad_s = (probs * (grad_p - inner)).astype(BF)
                 grad_q = jnp.dot(grad_s, keys, preferred_element_type=F32) * scale
-                gk_all[:width, :] += lax.dot_general(
+                gk_all[:reach, :] += lax.dot_general(
                     grad_s, query, (((0,), (0,)), ((), ())), preferred_element_type=F32
                 )
-                gv_all[:width, :] += lax.dot_general(
+                gv_all[:reach, :] += lax.dot_general(
                     probs.astype(BF), grad_o, (((0,), (0,)), ((), ())), preferred_element_type=F32
                 )
                 grad_raw, gained = back(proj_ref[:, column], q_gain, grad_q.astype(BF).astype(F32))
                 out_ref[:, column] = grad_raw.astype(BF)
                 gains_out[0:1, :] += gained
+
+            tiles(heads * HD, HD, one)
 
     here = pl.ds(pl.multiple_of(block_at * rows, rows), rows)
     grad_k = (gk_all[here, :] * scale).astype(BF).astype(F32)
@@ -700,36 +812,65 @@
     out_ref[:, (heads + 1) * HD :] = gv_all[here, :].astype(BF)
     gains_out[1:2, :] += gained
 
-
-def attend_back(length, projected, low, grad_o, cosine, sine, gains, heads, blocks=4):
-    total, width = projected.shape
+    def leave(at):
+        part_ref[:, at] = lax.dot_general(
+            out_ref[...], wq_ref[at, :], (((1,), (1,)), ((), ())), preferred_element_type=F32
+        ).astype(BF)
+
+    tiles(part_ref.shape[1], 256, leave)
+
+    @pl.when(step == blocks - 1)
+    def _():
+        Blocks(sizes, specs, sources, results, sems).wait()
+
+
+def attend_back(
+    length, projected, low, grad, w_out, w_proj, cosine, sine, gains, heads, extras, specs, sizes,
+    collective_id, blocks=4,
+):
+    total, own_width = projected.shape
+    width = w_out.shape[1]
     rows = total // blocks
+    q_width = heads * HD
+
+    def by_rows(columns):
+        return pl.BlockSpec((rows, columns), lambda i: (blocks - 1 - i, 0))
+
+    def whole(array):
+        return pl.BlockSpec(array.shape, lambda i: (0, 0), pipeline_mode=pl.Buffered(1))
+
     return pl.pallas_call(
-        functools.partial(attend_back_kernel, heads, blocks),
+        functools.partial(attend_back_kernel, sizes, heads, blocks, specs),
         grid=(blocks,),
         out_shape=[
+            jax.ShapeDtypeStruct((total, own_width), BF),
             jax.ShapeDtypeStruct((total, width), BF),
             jax.ShapeDtypeStruct((2, HD), F32),
-        ],
+        ] + block_outs(sizes, extras, specs),
         in_specs=[
             pl.BlockSpec(memory_space=pltpu.SMEM),
-            pl.BlockSpec((rows, width), lambda i: (blocks - 1 - i, 0)),
-            pl.BlockSpec((rows, heads * HD), lambda i: (blocks - 1 - i, 0)),
+            by_rows(own_width),
+            by_rows(q_width),
             pl.BlockSpec((total, 2 * HD), lambda i: (0, heads // 2)),
-            pl.BlockSpec((rows, heads * HD), lambda i: (blocks - 1 - i, 0)),
-            pl.BlockSpec((rows, HD), lambda i: (blocks - 1 - i, 0)),
-            pl.BlockSpec((rows, HD), lambda i: (blocks - 1 - i, 0)),
-            pl.BlockSpec((2, HD), lambda i: (0, 0)),
-        ],
-        out_specs=[
-            pl.BlockSpec((rows, width), lambda i: (blocks - 1 - i, 0)),
-            pl.BlockSpec((2, HD), lambda i: (0, 0)),
-        ],
-        scratch_shapes=[pltpu.VMEM((total, HD), F32), pltpu.VMEM((total, HD), F32)],
-        compiler_params=pltpu.CompilerParams(vmem_limit_bytes=56 << 20),
-        cost_estimate=pl.CostEstimate(flops=10 * heads * total * total * HD, bytes_accessed=total * width * 10, transcendentals=heads * total * total),
+            by_rows(width),
+            whole(w_out),
+            whole(w_proj),
+            by_rows(HD),
+            by_rows(HD),
+            whole(gains),
+        ] + [ANY] * len(extras),
+        out_specs=[by_rows(own_width), by_rows(width), pl.BlockSpec((2, HD), lambda i: (0, 0))]
+        + [ANY] * len(extras),
+        scratch_shapes=[
+            pltpu.VMEM((total, HD), F32),
+            pltpu.VMEM((total, HD), F32),
+            pltpu.VMEM((rows, q_width), BF),
+        ] + block_scratch(sizes, extras, specs),
+        compiler_params=pltpu.CompilerParams(
+            collective_id=collective_id, has_side_effects=True, vmem_limit_bytes=58 << 20
+        ),
         name="attend_back",
-    )(length, projected, low, low, grad_o, cosine, sine, gains)
+    )(length, projected, low, low, grad, w_out, w_proj, cosine, sine, gains, *extras)
 
 
 def rms_factor(values):
@@ -804,16 +945,17 @@
     gain_ffn = gain_values[width : 2 * width][None]
     gain_heads = gain_values[2 * width :].reshape(2, HD)
 
-    inputs_all = tok_all.reshape(seq_total, width).astype(F32)
-    attn_low = (inputs_all * rms_factor(inputs_all) * gain_attn).astype(BF)
-    projected = dot(attn_low, w_proj)
     positions = jnp.arange(seq_total, dtype=jnp.int32)
     frequency = THETA ** (-jnp.arange(HD // 2, dtype=F32) / (HD // 2))
     angles = positions.astype(F32)[:, None] * frequency[None, :]
     cosine = jnp.concatenate([jnp.cos(angles)] * 2, axis=-1)
     sine = jnp.concatenate([-jnp.sin(angles), jnp.sin(angles)], axis=-1)
-    qkv_low, o_low = attend(lengths, projected, cosine, sine, gain_heads, heads)
-    o_part = dot(o_low, out_own).astype(BF).reshape(S, tok_count, width)
+    attn_low, projected, qkv_low, o_low, o_part, down_w = attend(
+        lengths, tok_all.reshape(seq_total, width), gain_attn[None], w_proj, cosine, sine,
+        gain_heads, out_own, heads, [w_down.reshape((S, own_experts) + w_down.shape[1:])],
+        ((("seq",), 0, "columns"),), sizes, 3,
+    )
+    o_part = o_part.reshape(S, tok_count, width)
 
     expert_ids = jnp.arange(expert_count, dtype=jnp.int32)
     slot_ids = jnp.arange(capacity, dtype=jnp.int32)
@@ -830,10 +972,8 @@
     shape5 = (F, S, own_experts, capacity, width)
 
     cot_rows = mm("brt,btd->brd", select, cot_all).astype(BF).reshape(grouped)
-    residual, ffn_all, g_rows, down_w = line(
-        "ffn", sizes, [o_part], [tokens[0], gain_ffn],
-        [cot_rows, w_down.reshape((S, own_experts) + w_down.shape[1:])],
-        ((("fsdp",), 1, 0), (("seq",), 0, "columns")), 2,
+    residual, ffn_all, g_rows = line(
+        "ffn", sizes, [o_part], [tokens[0], gain_ffn], [cot_rows], ((("fsdp",), 1, 0),), 2
     )
     g_rows = g_rows.reshape(shape5)
     ffn_low = lax.dynamic_index_in_dim(ffn_all, seq_at, 0, keepdims=False)
@@ -915,21 +1055,20 @@
     grad_router_part = mm("td,te->de", ffn_low, grad_logits)
     valid = (seq_at * tok_count + jnp.arange(tok_count, dtype=jnp.int32)) < lengths[0]
     grad_final = jnp.where(valid[:, None], cotangent[0].astype(F32), 0.0)
-    grad_residual, grad_gain_ffn, grad_attn_low, moe_back, down_got = line(
+    grad_residual, grad_gain_ffn, grad_attn_low, moe_back = line(
         "grad", sizes, [grad_part], [grad_final, gain_ffn, residual, grad_ffn_add],
-        [moe_rows.reshape(F, S, own_experts * capacity, width), down_term],
-        ((("fsdp",), 0, 1), (("seq",), "columns", 0)), 7,
+        [moe_rows.reshape(F, S, own_experts * capacity, width)], ((("fsdp",), 0, 1),), 7,
+    )
+    grad_attn_low = grad_attn_low.reshape(seq_total, width)
+
+    grad_proj, attn_part, grad_gain_heads, down_got = attend_back(
+        lengths, projected, qkv_low, grad_attn_low, out_own, w_proj, cosine, sine, gain_heads,
+        heads, [down_term], ((("seq",), "columns", 0),), sizes, 9,
     )
     grad_down = down_got.reshape(w_down.shape).astype(F32)
-    grad_attn_low = grad_attn_low.reshape(seq_total, width)
-
-    grad_o_low = mm("td,ed->te", grad_attn_low, out_own).astype(BF)
+    attn_part = attn_part.reshape(S, tok_count, width)
     grad_out_part = mm("te,td->ed", o_low, grad_attn_low).astype(BF)
-    grad_proj, grad_gain_heads = attend_back(
-        lengths, projected, qkv_low, grad_o_low, cosine, sine, gain_heads, heads
-    )
     grad_qkv_part = mm("td,te->de", attn_low, grad_proj).astype(BF).reshape(S, F, w_rows, own_width)
-    attn_part = mm("te,de->td", grad_proj, w_proj).astype(BF).reshape(S, tok_count, width)
     moe_part = mm("brt,brd->btd", select, moe_back.reshape(S, -1, width)).astype(BF)
     sums, grad_out_got, grad_qkv_plane = line(
         "sum", sizes, [attn_part, moe_part], [],
@@ -939,7 +1078,7 @@
     grad_attn_norm, moe_out = sums[0], sums[1]
     final = jnp.where(valid[:, None], residual + moe_out, 0.0)
     grad_out = jnp.sum(grad_out_got.astype(F32), axis=0)
-    grad_qkv_own = jnp.sum(grad_qkv_plane.astype(F32), axis=0)
+    grad_qkv_own = jnp.sum(grad_qkv_plane.astype(F32), axis=0).astype(BF)
     layer_inputs = tokens[0].astype(F32)
     factor = rms_factor(layer_inputs)
     normed = layer_inputs * factor
@@ -955,7 +1094,7 @@
     small_got, grad_qkv_got = exchange(
         [lanes(small_part, N), grad_qkv_own], ((EVERY, 0, 0), (("seq",), 0, 0)), sizes, 10
     )
-    grad_qkv = whole_columns(grad_qkv_got)
+    grad_qkv = whole_columns(grad_qkv_got).astype(F32)
     small_sum = jnp.sum(small_got, axis=0).reshape(-1)
     grad_router = small_sum[:router_size].reshape(w_router.shape)
     grad_gains = small_sum[router_size : router_size + small]

time: 1410 us -> 1300 us (0.922)
  Pallas kernels: 1140 us -> 1070 us
  matrix products: 189 us -> 160 us
    pallas_call x3, Pallas kernels: 536 us -> 462 us  [line(): pl.pallas_call(functools.partial(line_kernel, sizes, chunks, mode, len(pa...]
    pallas_call x2, Pallas kernels: 68 us -> 125 us  [the longest x1 63.4 us: attend_back(): pl.pallas_call(functools.partial(attend_back_kernel, sizes, heads, blocks...]
    pallas_call x1, Pallas kernels: 206 us -> 163 us  [entry(): pl.pallas_call(functools.partial(entry_kernel, sizes), out_shape=[line_ou...]
    dot_general x3 -> x1, matrix products: 17 us -> 1.84 us  [dot(): return jnp.dot(left, right, preferred_element_type=F32)]
    dot_general x16 -> x14, matrix products: 171 us -> 158 us  [mm(): return jnp.einsum(form, left, right, preferred_element_type=F32)]
where the time goes in v1:
time: 1300 us; the launch traced here: 1290 us
  Pallas kernels  1070 us (82%)
  matrix products  160 us (12%)
  other arithmetic  41.8 us (3%)
  local copies, waits for them, and re-layouts  14.2 us (1%)
    pallas_call x3, Pallas kernels, line(): pl.pallas_call(functools.partial(line_kernel, sizes, chunks, mode, len(pa...  462 us
    pallas_call x3, Pallas kernels, exchange(): pl.pallas_call(functools.partial(exchange_kernel, sizes, specs), out_shap...  322 us
    pallas_call x1, Pallas kernels, entry(): pl.pallas_call(functools.partial(entry_kernel, sizes), out_shape=[line_ou...  163 us
    dot_general x14, matrix products, mm(): return jnp.einsum(form, left, right, preferred_element_type=F32)  158 us
    pallas_call x1, Pallas kernels, attend_back(): pl.pallas_call(functools.partial(attend_back_kernel, sizes, heads, blocks...  63.4 us
    pallas_call x1, Pallas kernels, attend(): pl.pallas_call(functools.partial(attend_kernel, sizes, heads, blocks, spe...  61.8 us

profile of v1, /device:TPU:0, one launch (start us, length us, event | category | flops | bytes accessed | tf_op | source)
XLA Modules:
  0.0 1290.2 jit_solution(10973891701670373676)
XLA Ops:
  4.2 162.5 %entry.1 = (bf16[4,256,2048]{2,1,0:T(8,128)(2,1)}, bf16[4,256,2048]{2,1,0:T(8,128)(2,1)}, s32[4,16,256]{2,1,0:T(8,128)}, bf16[4,8,64,1280]{3,2,1,0:T(8,128)(2,1)...) custom-call(bf16[256,2048]{1,0:T(8,128)(2,1)} %bitcast.220, bf16[256,2048]{1,0:T(8,128)(2,1)} %bitcast.237, ...), custom_call_target="tpu_custom_call" | custom-call | tf_op jit(solution)/shard_map/entry/pallas_call | solution.py:371
  173.0 61.8 %attend.1 = (bf16[1024,2048]{1,0:T(8,128)(2,1)}, f32[1024,1280]{1,0:T(8,128)}, bf16[1024,1280]{1,0:T(8,128)(2,1)}, bf16[1024,1024]{1,0:T(8,128)(2,1)}, bf16[1024...) custom-call(s32[1]{0:T(128)} %copy.111.refs_0_, bf16[1024,2048]{1,0:T(8,128)(2,1)} %bitcast.231, f32[1,2048]{1,0:T(1,128)} %bitcast.256, ...), custom_call_target="tpu_custom_call" | custom-call | tf_op jit(solution)/shard_map/attend/pallas_call | solution.py:709
  235.6 8.0 convolution_convert_fusion.3
  243.6 151.1 %line_ffn.1 = (f32[256,2048]{1,0:T(8,128)}, bf16[4,256,2048]{2,1,0:T(8,128)(2,1)}, bf16[8,4,80,2048]{3,2,1,0:T(8,128)(2,1)}) custom-call(bf16[4,256,2048]{2,1,0:T(8,128)(2,1)} %bitcast.232, bf16[256,2048]{1,0:T(8,128)(2,1)} %bitcast.221, f32[1,2048]{1,0:T(1,128)} %bitcast.258, bf16[4,8,80,2048]{3,2,1,0:T(8,128)(2,1)} %bitcast.218), custom_call_target="tpu_custom_call" | custom-call | tf_op jit(solution)/shard_map/line_ffn/pallas_call | solution.py:592
  399.8 7.8 convolution_convert_fusion.2
  407.6 146.6 %exchange_4.1 = (bf16[8,4,80,2048]{3,2,1,0:T(8,128)(2,1)}, bf16[4,1,512,1536]{3,2,1,0:T(8,128)(2,1)}, f32[32,16,128]{2,1,0:T(8,128)}) custom-call(bf16[4,8,80,2048]{3,2,1,0:T(8,128)(2,1)} %bitcast.219, bf16[4,1,512,1536]{3,2,1,0:T(8,128)(2,1)} %bitcast.226, f32[32,16,128]{2,1,0:T(8,128)} %bitcast.242), custom_call_target="tpu_custom_call" | custom-call | tf_op jit(solution)/shard_map/exchange_4/pallas_call | solution.py:154
  555.4 12.5 convert_bitcast_fusion.3
  567.9 19.8 %convolution_bitcast_fusion = f32[8,4,1,80,1536]{4,3,1,0,2:T(8,128)S(1)} fusion(bf16[2048,1536,1,1]{1,0,3,2:T(8,128)(2,1)S(1)} %bitcast.280, bf16[8,4,80,2048]{3,2,1,0:T(8,128)(2,1)} %get-tuple-element.57), kind=kOutput, calls=%fused_computation.25 | convolution fusion | flops 16106127360 | bytes 32505856 | tf_op jit(solution)/shard_map/asjcd,jdf->asjcf/dot_general | solution.py:885
  587.8 6.8 fusion.18
  594.5 17.2 %fusion.5 = (bf16[8,4,80,2048]{3,2,1,0:T(8,128)(2,1)}, f32[8,4,80]{2,1,0:T(4,128)S(1)}) fusion(f32[8,4,80]{2,1,0:T(4,128)S(1)} %bitcast.269, bf16[8,4,80,2048]{3,2,1,0:T(8,128)(2,1)} %get-tuple-element.56, bf16[8,4,1,80,768]{4,3,1,0,2:T(8,128)(2,1)S(1)} %get-tuple-element.120, bf16[1,768,2048]{2,1,0:T(8,128)(2,1)} %get-tuple-element.54), kind=kOutput, calls=%fused_computation.9 | convolution fusion | flops 8089761280 | bytes 28069888 | tf_op jit(solution)/shard_map/asjch,jhd->asjcd/dot_general | solution.py:885
  612.5 22.5 %bitcast_convert_fusion = bf16[2048,1536]{1,0:T(8,128)(2,1)} fusion(bf16[8,4,80,2048]{3,2,1,0:T(8,128)(2,1)} %get-tuple-element.57, bf16[8,4,80,768]{3,2,1,0:T(8,128)(2,1)} %get-tuple-element.119, bf16[8,4,80,768]{3,2,1,0:T(8,128)(2,1)} %get-tuple-element.118), kind=kOutput, calls=%fused_computation.8 | convolution fusion | flops 16125001728 | bytes 24641536 | tf_op jit(solution)/shard_map/asjcd,asjcf->jdf/dot_general | solution.py:885
  635.0 21.4 %convert_bitcast_fusion.2.refs_0_ = bf16[8,4,80,2048]{3,2,1,0:T(8,128)(2,1)} fusion(bf16[2048,1536,1,1]{1,0,3,2:T(8,128)(2,1)} %bitcast.277, bf16[8,4,80,768]{3,2,1,0:T(8,128)(2,1)S(1)} %copy-done.11, bf16[8,4,80,768]{3,2,1,0:T(8,128)(2,1)S(1)} %copy-done.10), kind=kOutput, calls=%fused_computation.10 | convolution fusion | flops 16127098880 | bytes 24641536 | tf_op jit(solution)/shard_map/asjcf,jdf->asjcd/dot_general | solution.py:885
  656.5 147.1 %exchange_6.1 = (bf16[4,8,80,2048]{3,2,1,0:T(8,128)(2,1)}, bf16[4,1,512,1536]{3,2,1,0:T(8,128)(2,1)}, f32[32,16,128]{2,1,0:T(8,128)}) custom-call(bf16[8,4,80,2048]{3,2,1,0:T(8,128)(2,1)} %convert_bitcast_fusion.2.refs_0_, bf16[4,1,512,1536]{3,2,1,0:T(8,128)(2,1)} %bitcast.227, f32[32,16,128]{2,1,0:T(8,128)} %bitcast.241), custom_call_target="tpu_custom_call" | custom-call | tf_op jit(solution)/shard_map/exchange_6/pallas_call | solution.py:154
  807.4 13.9 %fusion.25.refs_10_ = bf16[1,768,2048]{2,1,0:T(8,128)(2,1)} fusion(bf16[8,4,80,2048]{3,2,1,0:T(8,128)(2,1)} %get-tuple-element.56, f32[8,4,80]{2,1,0:T(4,128)S(1)} %bitcast.270, bf16[8,4,1,80,768]{4,3,1,0,2:T(8,128)(2,1)} %copy-done.9), kind=kOutput, calls=%fused_computation.42 | convolution fusion | flops 8070365184 | bytes 17573888 | tf_op jit(solution)/shard_map/asjch,asjcd->jhd/dot_general | solution.py:885
  823.2 9.5 convolution_convert_fusion.5.refs_0_
  834.2 137.1 %line_grad.1 = (f32[256,2048]{1,0:T(8,128)}, f32[1,2048]{1,0:T(1,128)}, bf16[4,256,2048]{2,1,0:T(8,128)(2,1)}, bf16[4,8,80,2048]{3,2,1,0:T(8,128)(2,1)}) custom-call(bf16[4,256,2048]{2,1,0:T(8,128)(2,1)} %convolution_convert_fusion.5.refs_0_, f32[256,2048]{1,0:T(8,128)} %convert_select_fusion.refs_1_, f32[1,2048]{1,0:T(1,128)} %bitcast.259, ...), custom_call_target="tpu_custom_call" | custom-call | tf_op jit(solution)/shard_map/line_grad/pallas_call | solution.py:592
  971.3 63.4 %attend_back.1 = (bf16[1024,1280]{1,0:T(8,128)(2,1)}, bf16[1024,2048]{1,0:T(8,128)(2,1)}, f32[2,128]{1,0:T(2,128)}, bf16[4,1,768,512]{3,2,1,0:T(8,128)(2,1)}) custom-call(s32[1]{0:T(128)} %copy.111.refs_0_, f32[1024,1280]{1,0:T(8,128)} %get-tuple-element.50.refs_1_, bf16[1024,1280]{1,0:T(8,128)(2,1)} %get-tuple-element.51.refs_2_.refs_3_, ...), custom_call_target="tpu_custom_call" | custom-call | tf_op jit(solution)/shard_map/attend_back/pallas_call | solution.py:842
  1034.7 9.9 convolution_convert_fusion
  1044.7 6.3 convolution_convert_fusion.6
  1051.0 5.2 convolution_convert_fusion.4.refs_1_
  1056.2 173.9 %line_sum.1 = (f32[2,256,2048]{2,1,0:T(8,128)}, bf16[8,128,2048]{2,1,0:T(8,128)(2,1)}, bf16[8,4,64,1280]{3,2,1,0:T(8,128)(2,1)}) custom-call(bf16[4,256,2048]{2,1,0:T(8,128)(2,1)} %bitcast.235, bf16[4,256,2048]{2,1,0:T(8,128)(2,1)} %convolution_convert_fusion.4.refs_1_, bf16[8,128,2048]{2,1,0:T(8,128)(2,1)} %bitcast.236, bf16[4,8,64,1280]{3,2,1,0:T(8,128)(2,1)} %bitcast.230), custom_call_target="tpu_custom_call" | custom-call | tf_op jit(solution)/shard_map/line_sum/pallas_call | solution.py:592
  1238.0 28.4 %exchange_10.1 = (f32[32,32,128]{2,1,0:T(8,128)}, bf16[4,64,1280]{2,1,0:T(8,128)(2,1)}) custom-call(f32[32,32,128]{2,1,0:T(8,128)} %bitcast.239, bf16[4,64,1280]{2,1,0:T(8,128)(2,1)} %reduce_sum.140.refs_1_), custom_call_target="tpu_custom_call" | custom-call | tf_op jit(solution)/shard_map/exchange_10/pallas_call | solution.py:154
  1272.1 5.3 fusion.41
  1283.2 6.6 bitcast_convert_fusion.1
  (143 shorter events, 43.2 us)
Async XLA Ops:
  173.0 61.8 %copy-start.18 = (s32[4,16,256]{2,1,0:T(8,128)S(1)}, s32[4,16,256]{2,1,0:T(8,128)}, u32[]{:S(2)}) copy-start(s32[4,16,256]{2,1,0:T(8,128)} %get-tuple-element.47) | copy-start | bytes 196612
  235.6 164.3 %copy-start.2 = (pred[4,640,256]{2,1,0:T(32,128)(4,1)}, pred[4,640,256]{2,1,0:T(32,128)(4,1)S(1)}, u32[]{:S(2)}) copy-start(pred[4,640,256]{2,1,0:T(32,128)(4,1)S(1)} %bitcast_compare_fusion) | copy-start | bytes 1966084
  243.6 153.4 %copy-start.15 = (s32[1,256,8]{1,2,0:T(8,128)S(1)}, s32[1,256,8]{1,2,0:T(8,128)}, u32[]{:S(2)}) copy-start(s32[1,256,8]{1,2,0:T(8,128)} %param.14) | copy-start | bytes 24580
  243.6 154.7 %copy-start.19 = (s32[1,256,8]{1,2,0:T(8,128)S(1)}, s32[1,256,8]{1,2,0:T(8,128)}, u32[]{:S(2)}) copy-start(s32[1,256,8]{1,2,0:T(8,128)} %param.15) | copy-start | bytes 24580
  395.2 12.5 copy-start.4
  397.1 10.5 copy-start.13
  554.2 13.7 %slice-start.2 = ((s8[6291456]{0:T(1024)(128)(4,1)}), s8[2097152]{0:T(1024)(128)(4,1)S(1)}, s32[]{:S(2)}) async-start(s8[6291456]{0:T(1024)(128)(4,1)} %bitcast.278), calls=%async_computation.2 | async-start | bytes 4194304
  555.4 12.5 slice-start.3
  594.5 17.2 %copy-start.9 = (bf16[8,4,1,80,768]{4,3,1,0,2:T(8,128)(2,1)}, bf16[8,4,1,80,768]{4,3,1,0,2:T(8,128)(2,1)S(1)}, u32[]{:S(2)}) copy-start(bf16[8,4,1,80,768]{4,3,1,0,2:T(8,128)(2,1)S(1)} %get-tuple-element.120) | copy-start | bytes 11796484
  612.5 22.5 %copy-start.10 = (bf16[8,4,80,768]{3,2,1,0:T(8,128)(2,1)S(1)}, bf16[8,4,80,768]{3,2,1,0:T(8,128)(2,1)}, u32[]{:S(2)}) copy-start(bf16[8,4,80,768]{3,2,1,0:T(8,128)(2,1)} %get-tuple-element.118) | copy-start | bytes 11796484
  612.5 22.5 %copy-start.11 = (bf16[8,4,80,768]{3,2,1,0:T(8,128)(2,1)S(1)}, bf16[8,4,80,768]{3,2,1,0:T(8,128)(2,1)}, u32[]{:S(2)}) copy-start(bf16[8,4,80,768]{3,2,1,0:T(8,128)(2,1)} %get-tuple-element.119) | copy-start | bytes 11796484
  656.5 148.1 %copy-start.16 = (s32[1,256,8]{1,2,0:T(8,128)S(1)}, s32[1,256,8]{1,2,0:T(8,128)}, u32[]{:S(2)}) copy-start(s32[1,256,8]{1,2,0:T(8,128)} %param.14) | copy-start | bytes 24580
  656.5 148.1 %copy-start.20 = (s32[1,256,8]{1,2,0:T(8,128)S(1)}, s32[1,256,8]{1,2,0:T(8,128)}, u32[]{:S(2)}) copy-start(s32[1,256,8]{1,2,0:T(8,128)} %param.15) | copy-start | bytes 24580
  656.5 148.6 %copy-start.14 = (f32[256,8]{0,1:T(8,128)S(1)}, f32[256,8]{0,1:T(8,128)}, u32[]{:S(2)}) copy-start(f32[256,8]{0,1:T(8,128)} %copy-done.13) | copy-start | bytes 24580
  656.5 148.6 %copy-start.22 = (f32[256]{0:T(256)S(1)}, f32[256]{0:T(256)}, u32[]{:S(2)}) copy-start(f32[256]{0:T(256)} %copy-done.21) | copy-start | bytes 3076
  656.5 148.7 %copy-start.24 = (f32[256]{0:T(256)S(1)}, f32[256]{0:T(256)}, u32[]{:S(2)}) copy-start(f32[256]{0:T(256)} %copy-done.23) | copy-start | bytes 3076
  807.4 13.9 %copy-start.5 = (bf16[2048,32]{1,0:T(8,128)(2,1)S(1)}, bf16[2048,32]{1,0:T(8,128)(2,1)}, u32[]{:S(2)}) copy-start(bf16[2048,32]{1,0:T(8,128)(2,1)} %copy-done.4) | copy-start | bytes 393220
  807.4 15.7 %copy-start.3 = (pred[4,640,256]{2,1,0:T(32,128)(4,1)S(1)}, pred[4,640,256]{2,1,0:T(32,128)(4,1)}, u32[]{:S(2)}) copy-start(pred[4,640,256]{2,1,0:T(32,128)(4,1)} %copy-done.2) | copy-start | bytes 1966084
  823.2 9.5 copy-start.8
  1034.7 9.9 copy-start.6
  1034.7 9.9 copy-start.28
  1056.2 174.0 %copy-start = (bf16[1,256,2048]{2,1,0:T(8,128)(2,1)S(1)}, bf16[1,256,2048]{2,1,0:T(8,128)(2,1)}, u32[]{:S(2)}) copy-start(bf16[1,256,2048]{2,1,0:T(8,128)(2,1)} %param.11) | copy-start | bytes 3145732
  1056.2 174.3 %copy-start.17 = (f32[2048]{0:T(1024)S(1)}, f32[2048]{0:T(1024)}, u32[]{:S(2)}) copy-start(f32[2048]{0:T(1024)} %get-tuple-element.132) | copy-start | bytes 24580
  1238.0 34.1 %copy-start.1 = (f32[256,2048]{1,0:T(8,128)S(1)}, f32[256,2048]{1,0:T(8,128)}, u32[]{:S(2)}) copy-start(f32[256,2048]{1,0:T(8,128)} %get-tuple-element.49.refs_3_) | copy-start | bytes 6291460
  (9 other events, 29.6 us)

commit v2 on v1

--- a/solution.py
+++ b/solution.py
@@ -57,6 +57,8 @@
 
 
 def block_of(ref, dim, at, total):
+    if dim is None:
+        return ref
     if dim == "columns":
         width = ref.shape[-1] // total
         return ref.at[:, :, pl.ds(pl.multiple_of(at * width, 128), width)]
@@ -118,7 +120,7 @@
         shape = list(array.shape)
         if before == "columns":
             shape[-1] //= count_of(sizes, axes)
-        else:
+        elif before is not None:
             del shape[before]
         stages.append(pltpu.VMEM(tuple(shape), array.dtype))
     count = len(specs)
@@ -130,7 +132,9 @@
     for array, (axes, before, after) in zip(arrays, specs):
         shape = list(array.shape)
         total = count_of(sizes, axes)
-        if before == "columns":
+        if before is None:
+            shape = [total] + shape
+        elif before == "columns":
             shape = [total, shape[0], shape[1], shape[2] // total]
         elif after == "columns":
             shape = [shape[1], shape[2], shape[3] * total]
@@ -390,13 +394,156 @@
     )(tokens, cotangent, table, w_qkv, w_out, small)
 
 
-def line_kernel(sizes, chunks, mode, parts, extra, *refs):
+class Widen:
+    def __init__(self, pairs, sems, buffers):
+        self.jobs = []
+        for i, (source, result) in enumerate(pairs):
+            narrow, wide = buffers[2 * i], buffers[2 * i + 1]
+            for j in range(source.shape[0]):
+                self.jobs.append(
+                    (
+                        pltpu.make_async_copy(source.at[j], narrow.at[j % 2], sems.at[i, 0, j % 2]),
+                        pltpu.make_async_copy(wide.at[j % 2], result.at[j], sems.at[i, 1, j % 2]),
+                        narrow.at[j % 2],
+                        wide.at[j % 2],
+                        j,
+                        source.shape[0],
+                    )
+                )
+        self.done = 0
+
+    def start(self):
+        for inward, _, _, _, j, _ in self.jobs:
+            if j < 2:
+                inward.start()
+
+    def turn(self):
+        if self.done == len(self.jobs):
+            return
+        at = self.done
+        inward, outward, narrow, wide, j, number = self.jobs[at]
+        inward.wait()
+        if j >= 2:
+            self.jobs[at - 2][1].wait()
+        wide[...] = narrow[...].astype(F32)
+        outward.start()
+        if j + 2 < number:
+            self.jobs[at + 2][0].start()
+        self.done += 1
+
+    def wait(self):
+        while self.done < len(self.jobs):
+            self.turn()
+        for _, outward, _, _, j, number in self.jobs:
+            if j >= number - 2:
+                outward.wait()
+
+
+def widen_scratch(arrays):
+    if not arrays:
+        return []
+    scratch = [DMA((len(arrays), 2, 2))]
+    for array in arrays:
+        shape = (2,) + array.shape[1:]
+        scratch += [pltpu.VMEM(shape, BF), pltpu.VMEM(shape, F32)]
+    return scratch
+
+
+def grads_kernel(sizes, specs, *refs):
     S = sizes["seq"]
+    count = len(specs)
+    sources, (x_any, gu_any, ph_any, g_any) = refs[:count], refs[count : count + 4]
+    results, (up_out, down_out) = refs[count + 4 : 2 * count + 4], refs[2 * count + 4 : 2 * count + 6]
+    x_ref, gu_ref, ph_ref, g_ref, up_stage, down_stage, in_sem, up_send, up_recv, out_sem, *sems = refs[2 * count + 6 :]
+    s = lax.axis_index("seq")
+    inward = [
+        pltpu.make_async_copy(source, target, in_sem.at[i])
+        for i, (source, target) in enumerate(
+            ((x_any, x_ref), (gu_any, gu_ref), (ph_any, ph_ref), (g_any, g_ref))
+        )
+    ]
+    met = greet(sizes)
+    for copy in inward:
+        copy.start()
+    blocks = Blocks(sizes, specs, sources, results, sems)
+    met()
+    blocks.start()
+    inward[0].wait()
+    inward[1].wait()
+    part = up_stage.shape[1]
+    over_rows = (((0,), (0,)), ((), ()))
+    sent = []
+    for turn_at in range(1, S + 1):
+        target = lax.rem(s + turn_at, S)
+        mine = pl.ds(pl.multiple_of(target * part, 128), part)
+        block = up_stage.at[turn_at - 1]
+
+        def one(at):
+            block[:, at] = lax.dot_general(
+                x_ref[:, mine], gu_ref[:, at], over_rows, preferred_element_type=F32
+            ).astype(BF)
+
+        tiles(gu_ref.shape[1], 256, one)
+        if turn_at < S:
+            copy = pltpu.make_async_remote_copy(
+                src_ref=block, dst_ref=up_out.at[s],
+                send_sem=up_send.at[turn_at], recv_sem=up_recv.at[turn_at],
+                device_id={"seq": target}, device_id_type=MESH,
+            )
+        else:
+            copy = pltpu.make_async_copy(block, up_out.at[s], out_sem.at[0])
+        copy.start()
+        sent.append(copy)
+    inward[2].wait()
+    inward[3].wait()
+
+    def one_down(at):
+        down_stage[:, at] = lax.dot_general(
+            ph_ref[...], g_ref[:, at], over_rows, preferred_element_type=F32
+        ).astype(BF)
+
+    tiles(g_ref.shape[1], 256, one_down)
+    copy = pltpu.make_async_copy(down_stage, down_out, out_sem.at[1])
+    copy.start()
+    sent.append(copy)
+    blocks.wait()
+    for copy in sent:
+        copy.wait()
+
+
+def grads(arrays, specs, rows, grad_gu, hidden, grad_out, sizes, collective_id):
+    S = sizes["seq"]
+    part = rows.shape[1] // S
+    up_block = (part, grad_gu.shape[1])
+    down = (hidden.shape[1], grad_out.shape[1])
+    inner = [rows, grad_gu, hidden, grad_out]
+    return pl.pallas_call(
+        functools.partial(grads_kernel, sizes, specs),
+        out_shape=block_outs(sizes, arrays, specs)
+        + [jax.ShapeDtypeStruct((S,) + up_block, BF), jax.ShapeDtypeStruct(down, BF)],
+        in_specs=[ANY] * (len(arrays) + 4),
+        out_specs=[ANY] * (len(arrays) + 2),
+        scratch_shapes=[pltpu.VMEM(array.shape, BF) for array in inner]
+        + [pltpu.VMEM((S,) + up_block, BF), pltpu.VMEM(down, BF)]
+        + [DMA((4,)), DMA((S,)), DMA((S,)), DMA((2,))]
+        + block_scratch(sizes, arrays, specs),
+        compiler_params=pltpu.CompilerParams(
+            collective_id=collective_id, has_side_effects=True, vmem_limit_bytes=60 << 20
+        ),
+        name="grads",
+    )(*arrays, *inner)
+
+
+def line_kernel(sizes, chunks, mode, parts, extra, widened, *refs):
+    S, F = sizes["seq"], sizes["fsdp"]
     count = len(extra)
     names = {
         "ffn": (["base", "gain"], ["resid_out", "all_out"]),
         "grad": (["base", "gain", "resid", "add"], ["grad_out", "gain_out", "all_out"]),
-        "sum": ([], ["sum_out"]),
+        "last": (
+            ["base", "gain", "resid", "inputs", "length", "gout", "gqkv"],
+            ["grad_out", "low_out", "gains_all", "gout_out", "gqkv_out"],
+        ),
     }[mode]
     refs = list(refs)
 
@@ -407,21 +554,32 @@
     part_refs = take(parts)
     given = dict(zip(names[0], take(len(names[0]))))
     sources = take(count)
+    narrow = take(widened)
     given.update(zip(names[1], take(len(names[1]))))
     results = take(count)
+    wide = take(widened)
     from_left, from_right = take(2)
-    gather = mode != "sum"
+    gather = mode != "last"
     if gather:
-        (stage,) = take(1)
-    rs_send, rs_recv = take(2)
-    if gather:
-        ag_send, ag_recv, own_sem = take(3)
+        stage, rs_send, rs_recv, ag_send, ag_recv, own_sem = take(6)
         all_out = given["all_out"]
+    else:
+        gain_sum, gain_stage, gain_send, gain_recv, gain_own = take(5)
+        plane_gout, plane_gqkv, gqkv_stage, gqkv_line, line_send, line_recv = take(6)
+        plane_sems = take(5)
+        rs_send, rs_recv = take(2)
     s = lax.axis_index("seq")
+    f = lax.axis_index("fsdp")
+    me = s * F + f
+    N = S * F
     rows = part_refs[0].shape[1]
     span = rows // chunks
     met = greet(sizes)
+    widen = Widen(list(zip(narrow, wide)), refs[0], refs[1:]) if widened else None
+    del refs[: (1 + 2 * widened) if widened else 0]
     blocks = Blocks(sizes, extra, sources, results, refs)
+    if widen:
+        widen.start()
     met()
 
     def at(c):
@@ -484,8 +642,22 @@
         total = mine(s, c)[...].astype(F32)
         total = total + jnp.where(s > 0, landed(0, s, c)[...].astype(F32), 0.0)
         total = total + jnp.where(s < S - 1, landed(1, s, c)[...].astype(F32), 0.0)
-        if mode == "sum":
-            given["sum_out"][c // chunks, at(c), :] = total
+        if mode == "last":
+            if c >= chunks:
+                row = s * rows + (c % chunks) * span + lax.broadcasted_iota(jnp.int32, total.shape, 0)
+                value = given["resid"][at(c), :] + total
+                given["low_out"][at(c), :] = jnp.where(row < given["length"][0], value, 0.0).astype(BF)
+                return
+            value = given["inputs"][at(c), :].astype(F32)
+            factor = lax.rsqrt(jnp.mean(value * value, axis=-1, keepdims=True) + EPSILON)
+            normed = value * factor
+            scaled = total * given["gain"][...]
+            inner = jnp.mean(scaled * normed, axis=-1, keepdims=True)
+            given["grad_out"][at(c), :] = given["base"][at(c), :] + factor * (scaled - normed * inner)
+            gained = jnp.sum(total * normed, axis=0, keepdims=True)
+            gain_sum[...] = gained if c == 0 else gain_sum[...] + gained
+            if c == chunks - 1:
+                send_gains()
             return
         if mode == "ffn":
             value = given["base"][at(c), :].astype(F32) + total
@@ -516,6 +688,68 @@
         def _():
             ag_copy(s, c, 1, 1).start()
 
+    def gain_copy(step):
+        return pltpu.make_async_remote_copy(
+            src_ref=gain_stage, dst_ref=given["gains_all"].at[me],
+            send_sem=gain_send.at[step], recv_sem=gain_recv.at[step],
+            device_id=place_of(sizes, EVERY, lax.rem(me + step, N)), device_id_type=MESH,
+        )
+
+    def own_gains():
+        return pltpu.make_async_copy(gain_stage, given["gains_all"].at[me], gain_own.at[0])
+
+    def send_gains():
+        for j in range(gain_stage.shape[0]):
+            gain_stage[j : j + 1, :] = gain_sum[:, j * 128 : (j + 1) * 128]
+        own_gains().start()
+        for step in range(1, N):
+            gain_copy(step).start()
+
+    plane = None
+    if mode == "last":
+        plane = Blocks(
+            sizes, ((("fsdp",), 0, 0), (("fsdp",), 1, 0)), [given["gout"], given["gqkv"]],
+            [plane_gout, plane_gqkv], plane_sems,
+        )
+
+    def line_copy(step):
+        return pltpu.make_async_remote_copy(
+            src_ref=gqkv_stage.at[lax.rem(s + step, S)], dst_ref=gqkv_line.at[s],
+            send_sem=line_send.at[step], recv_sem=line_recv.at[step],
+            device_id={"seq": lax.rem(s + step, S)}, device_id_type=MESH,
+        )
+
+    def plane_step():
+        plane.wait()
+        for z in range(S):
+            total = plane_gqkv[0, z].astype(F32)
+            for owner in range(1, F):
+                total = total + plane_gqkv[owner, z].astype(F32)
+            gqkv_stage[z] = total.astype(BF)
+        for step in range(1, S):
+            line_copy(step).start()
+        gqkv_line[s] = gqkv_stage[s]
+        half = plane_gout.shape[1] // 2
+        for part_at in range(2):
+            own = pl.ds(part_at * half, half)
+            total = plane_gout[0, own].astype(F32)
+            for owner in range(1, F):
+                total = total + plane_gout[owner, own].astype(F32)
+            given["gout_out"][own, :] = total
+
+    def columns_step():
+        for step in range(1, S):
+            line_copy(step).wait()
+        result = given["gqkv_out"]
+        q_width, kv = QH * HD // S, KH * HD // S
+        for z in range(S):
+            block = gqkv_line[z].astype(F32)
+            result[:, z * q_width : (z + 1) * q_width] = block[:, :q_width]
+            key_at = S * q_width + z * kv
+            result[:, key_at : key_at + kv] = block[:, q_width : q_width + kv]
+            value_at = S * (q_width + kv) + z * kv
+            result[:, value_at : value_at + kv] = block[:, q_width + kv :]
+
     def relay_step(c, hop):
         @pl.when(s >= hop)
         def _():
@@ -538,7 +772,10 @@
     for c in range(ahead):
         end_step(c)
     blocks.start()
+    if plane:
+        plane.start()
     hops = S - 1 if gather else 0
+    plane_at = steps - 3
     for t in range(steps + 1 + hops):
         if t < steps:
             middle_step(t)
@@ -549,6 +786,10 @@
         for hop in range(1, hops + 1):
             if 0 <= t - 1 - hop < steps:
                 relay_step(t - 1 - hop, hop)
+        if widen:
+            widen.turn()
+        if plane and t == plane_at:
+            plane_step()
 
     for c in range(steps):
         for d in range(S - 1, 0, -1):
@@ -569,37 +810,70 @@
                 @pl.when((s > 0) & (s <= S - hop))
                 def _():
                     ag_copy(s, c, 1, hop).wait_send()
+    if mode == "last":
+        columns_step()
+        own_gains().wait()
+        for step in range(1, N):
+            gain_copy(step).wait()
+    if widen:
+        widen.wait()
     blocks.wait()
 
 
-def line(mode, sizes, parts, others, extras, specs, collective_id, chunks=8):
+def line(mode, sizes, parts, others, extras, specs, collective_id, chunks=8, widened=()):
     S = sizes["seq"]
     _, rows, width = parts[0].shape
     full = jax.ShapeDtypeStruct((rows, width), F32)
     everyone = jax.ShapeDtypeStruct((S, rows, width), BF)
     steps = chunks * len(parts)
     scratch = [pltpu.VMEM((len(parts), S, rows, width), BF)] * 2
+    in_specs = [VM] * (len(parts) + len(others))
     sems = [DMA((2, S, steps)), DMA((2, S, steps))]
     if mode == "ffn":
         outs, out_specs = [full, everyone], [VM, ANY]
     elif mode == "grad":
         outs, out_specs = [full, jax.ShapeDtypeStruct((1, width), F32), everyone], [VM, VM, ANY]
     else:
-        outs, out_specs = [jax.ShapeDtypeStruct((len(parts), rows, width), F32)], [VM]
-    if mode != "sum":
+        gout, gqkv = others[-2:]
+        owned = gqkv.shape[2:]
+        outs = [
+            full,
+            jax.ShapeDtypeStruct((rows, width), BF),
+            jax.ShapeDtypeStruct((S * sizes["fsdp"], width // 128, 128), F32),
+            jax.ShapeDtypeStruct(gout.shape[1:], F32),
+            jax.ShapeDtypeStruct((owned[0], owned[1] * S), F32),
+        ]
+        out_specs = [VM, VM, ANY, VM, VM]
+        N = S * sizes["fsdp"]
+        scratch += [pltpu.VMEM((1, width), F32), pltpu.VMEM((width // 128, 128), F32)]
+        scratch += [DMA((N,)), DMA((N,)), DMA((1,))]
+        scratch += [
+            pltpu.VMEM(gout.shape, BF),
+            pltpu.VMEM((sizes["fsdp"], S) + owned, BF),
+            pltpu.VMEM((S,) + owned, BF),
+            pltpu.VMEM((S,) + owned, BF),
+            DMA((S,)),
+            DMA((S,)),
+        ]
+        scratch += block_scratch(sizes, [gout, gqkv], ((("fsdp",), 0, 0), (("fsdp",), 1, 0)))
+        in_specs[-2:] = [ANY, ANY]
+        in_specs[-3] = pl.BlockSpec(memory_space=pltpu.SMEM)
+    if mode != "last":
         scratch.append(pltpu.VMEM((rows, width), BF))
         sems += [DMA((2, chunks, S)), DMA((2, chunks, S)), DMA((chunks,))]
     return pl.pallas_call(
-        functools.partial(line_kernel, sizes, chunks, mode, len(parts), specs),
-        out_shape=outs + block_outs(sizes, extras, specs),
-        in_specs=[VM] * (len(parts) + len(others)) + [ANY] * len(extras),
-        out_specs=out_specs + [ANY] * len(extras),
-        scratch_shapes=scratch + sems + block_scratch(sizes, extras, specs),
+        functools.partial(line_kernel, sizes, chunks, mode, len(parts), specs, len(widened)),
+        out_shape=outs
+        + block_outs(sizes, extras, specs)
+        + [jax.ShapeDtypeStruct(array.shape, F32) for array in widened],
+        in_specs=in_specs + [ANY] * (len(extras) + len(widened)),
+        out_specs=out_specs + [ANY] * (len(extras) + len(widened)),
+        scratch_shapes=scratch + sems + widen_scratch(widened) + block_scratch(sizes, extras, specs),
         compiler_params=pltpu.CompilerParams(
             collective_id=collective_id, has_side_effects=True, vmem_limit_bytes=56 << 20
         ),
         name=f"line_{mode}",
-    )(*parts, *others, *extras)
+    )(*parts, *others, *extras, *widened)
 
 
 def turn(values, cosine, sine):
@@ -1016,28 +1290,35 @@
     hidden_low = (jax.nn.silu(gate_part) * up_part).astype(BF)
     expert_out = mm("asjch,jhd->asjcd", hidden_low, down_w).astype(BF)
     out_wide = expert_out.astype(F32)
-    g_wide = g_rows.astype(F32)
-    grad_prob_rows = jnp.sum(out_wide * g_wide, axis=-1)
+    grad_prob_rows = jnp.sum(out_wide * g_rows.astype(F32), axis=-1)
     moe_rows = (row_gate * out_wide).astype(BF)
-    grad_eo_low = (row_gate * g_wide).astype(BF)
-
-    grad_hidden_low = mm("asjcd,jhd->asjch", grad_eo_low, down_w).astype(BF)
-    grad_hidden = lax.optimization_barrier(grad_hidden_low).astype(F32)
+
+    through_down = mm("asjcd,jhd->asjch", g_rows, down_w)
+    grad_hidden = lax.optimization_barrier((row_gate * through_down).astype(BF)).astype(F32)
+    gated_hidden = (row_gate * hidden_low.astype(F32)).astype(BF)
     sigmoid_gate = jax.nn.sigmoid(gate_part)
     grad_gate = grad_hidden * up_part * sigmoid_gate * (1.0 + gate_part * (1.0 - sigmoid_gate))
     grad_up = grad_hidden * gate_part * sigmoid_gate
     grad_gu_low = jnp.concatenate([grad_gate, grad_up], axis=-1).astype(BF)
     grad_rows = mm("asjcf,jdf->asjcd", grad_gu_low, gate_up_w).astype(BF)
-    up_term = mm("asjcd,asjcf->jdf", x_rows, grad_gu_low).astype(BF)
-    down_term = mm("asjch,asjcd->jhd", hidden_low, grad_eo_low).astype(BF)
     prob_send = grad_prob_rows.reshape(F, S, -1).transpose(1, 0, 2).reshape(N, -1)
     back_layout = grad_rows.reshape(F, S, own_experts * capacity, width)
-    up_blocks = up_term.reshape(own_experts, S, part_width, 2 * FF).transpose(1, 0, 2, 3)
-    grad_back, up_got, prob_got = exchange(
-        [back_layout, up_blocks, lanes(prob_send, N)],
-        ((("fsdp",), 0, 1), (("seq",), 0, 0), (EVERY, 0, 0)), sizes, 6,
-    )
-    grad_gate_up = up_got.reshape(w_gate_up.shape).astype(F32)
+    back_blocks = [back_layout, lanes(prob_send, N)]
+    back_specs = ((("fsdp",), 0, 1), (EVERY, 0, 0))
+    if own_experts == 1:
+        grad_back, prob_got, up_got, down_term = grads(
+            back_blocks, back_specs, x_rows.reshape(-1, width), grad_gu_low.reshape(-1, 2 * FF),
+            gated_hidden.reshape(-1, FF), g_rows.reshape(-1, width), sizes, 6,
+        )
+        down_term = down_term[None]
+    else:
+        up_term = mm("asjcd,asjcf->jdf", x_rows, grad_gu_low).astype(BF)
+        down_term = mm("asjch,asjcd->jhd", gated_hidden, g_rows).astype(BF)
+        up_blocks = up_term.reshape(own_experts, S, part_width, 2 * FF).transpose(1, 0, 2, 3)
+        grad_back, prob_got, up_got = exchange(
+            back_blocks + [up_blocks], back_specs + ((("seq",), 0, 0),), sizes, 6
+        )
+    up_got = up_got.reshape(w_gate_up.shape)
     prob_slots = prob_got.reshape(S, F, -1)[:, :, : own_experts * capacity]
     prob_slots = prob_slots.reshape(S, F, own_experts, capacity).transpose(1, 0, 2, 3)
     prob_slots = prob_slots.reshape(expert_count, capacity)
@@ -1055,9 +1336,10 @@
     grad_router_part = mm("td,te->de", ffn_low, grad_logits)
     valid = (seq_at * tok_count + jnp.arange(tok_count, dtype=jnp.int32)) < lengths[0]
     grad_final = jnp.where(valid[:, None], cotangent[0].astype(F32), 0.0)
-    grad_residual, grad_gain_ffn, grad_attn_low, moe_back = line(
+    grad_residual, grad_gain_ffn, grad_attn_low, moe_back, grad_gate_up = line(
         "grad", sizes, [grad_part], [grad_final, gain_ffn, residual, grad_ffn_add],
         [moe_rows.reshape(F, S, own_experts * capacity, width)], ((("fsdp",), 0, 1),), 7,
+        widened=(up_got,),
     )
     grad_attn_low = grad_attn_low.reshape(seq_total, width)
 
@@ -1065,41 +1347,34 @@
         lengths, projected, qkv_low, grad_attn_low, out_own, w_proj, cosine, sine, gain_heads,
         heads, [down_term], ((("seq",), "columns", 0),), sizes, 9,
     )
-    grad_down = down_got.reshape(w_down.shape).astype(F32)
     attn_part = attn_part.reshape(S, tok_count, width)
     grad_out_part = mm("te,td->ed", o_low, grad_attn_low).astype(BF)
     grad_qkv_part = mm("td,te->de", attn_low, grad_proj).astype(BF).reshape(S, F, w_rows, own_width)
     moe_part = mm("brt,brd->btd", select, moe_back.reshape(S, -1, width)).astype(BF)
-    sums, grad_out_got, grad_qkv_plane = line(
-        "sum", sizes, [attn_part, moe_part], [],
-        [grad_out_part.reshape(F, -1, width), grad_qkv_part],
-        ((("fsdp",), 0, 0), (("fsdp",), 1, 0)), 8,
+    router_blocks = lanes(grad_router_part.reshape(N, -1), N)
+    early_gains = lanes(jnp.concatenate([grad_gain_ffn[0], grad_gain_heads.reshape(-1)])[None], 1)[0]
+    (
+        grad_inputs, final, late_gains, grad_out, grad_qkv, router_got, gains_got, grad_down
+    ) = line(
+        "last", sizes, [attn_part, moe_part],
+        [
+            grad_residual, gain_attn[None], residual, tokens[0], lengths,
+            grad_out_part.reshape(F, -1, width), grad_qkv_part,
+        ],
+        [router_blocks, early_gains], ((EVERY, 0, 0), (EVERY, None, 0)), 8,
+        widened=(down_got.reshape(w_down.shape),),
     )
-    grad_attn_norm, moe_out = sums[0], sums[1]
-    final = jnp.where(valid[:, None], residual + moe_out, 0.0)
-    grad_out = jnp.sum(grad_out_got.astype(F32), axis=0)
-    grad_qkv_own = jnp.sum(grad_qkv_plane.astype(F32), axis=0).astype(BF)
-    layer_inputs = tokens[0].astype(F32)
-    factor = rms_factor(layer_inputs)
-    normed = layer_inputs * factor
-    scaled = grad_attn_norm * gain_attn
-    inner = jnp.mean(scaled * normed, axis=-1, keepdims=True)
-    grad_inputs = grad_residual + factor * (scaled - normed * inner)
-    grad_gain_attn = jnp.sum(grad_attn_norm * normed, axis=0)
-
-    gain_part = jnp.concatenate([grad_gain_attn, grad_gain_ffn[0], grad_gain_heads.reshape(-1)])
-    small_part = jnp.concatenate(
-        [grad_router_part.reshape(N, -1), gain_part.reshape(N, -1)], axis=1
+    grad_router = jnp.sum(router_got, axis=0).reshape(-1)[:router_size].reshape(w_router.shape)
+    gain_sum = jnp.concatenate(
+        [
+            jnp.sum(late_gains, axis=0).reshape(-1),
+            jnp.sum(gains_got, axis=0).reshape(-1)[: width + 2 * HD],
+        ]
     )
-    small_got, grad_qkv_got = exchange(
-        [lanes(small_part, N), grad_qkv_own], ((EVERY, 0, 0), (("seq",), 0, 0)), sizes, 10
-    )
-    grad_qkv = whole_columns(grad_qkv_got).astype(F32)
-    small_sum = jnp.sum(small_got, axis=0).reshape(-1)
-    grad_router = small_sum[:router_size].reshape(w_router.shape)
-    grad_gains = small_sum[router_size : router_size + small]
+    device_at = seq_at * F + lax.axis_index("fsdp")
+    grad_gains = lax.dynamic_slice_in_dim(gain_sum, device_at * small, small, 0)
     return (
-        final.astype(BF)[None],
+        final[None],
         grad_inputs[None],
         grad_qkv,
         grad_out,

time: 1300 us -> 1280 us (0.985)
  matrix products: 160 us -> 129 us
  local copies, waits for them, and re-layouts: 14.2 us -> 32.4 us
    pallas_call x3 -> x1, Pallas kernels: 322 us -> 147 us  [exchange(): pl.pallas_call(functools.partial(exchange_kernel, sizes, specs), out_shap...]
    pallas_call x0 -> x1, Pallas kernels: none -> 123 us  [grads(): pl.pallas_call(functools.partial(grads_kernel, sizes, specs), out_shape=b...]
    pallas_call x3, Pallas kernels: 462 us -> 513 us  [line(): pl.pallas_call(functools.partial(line_kernel, sizes, chunks, mode, len(pa...]
    dot_general x14 -> x12, matrix products: 158 us -> 127 us  [mm(): return jnp.einsum(form, left, right, preferred_element_type=F32)]
    unnamed x77 -> x64, local copies, waits for them, and re-layouts: 8.69 us -> 26.7 us
where the time goes in v2:
time: 1280 us; the launch traced here: 1270 us
  Pallas kernels  1070 us (84%)
  matrix products  129 us (10%)
  other arithmetic  32.4 us (3%)
  local copies, waits for them, and re-layouts  32.4 us (3%)
    pallas_call x3, Pallas kernels, line(): pl.pallas_call(functools.partial(line_kernel, sizes, chunks, mode, len(pa...  513 us
    pallas_call x1, Pallas kernels, entry(): pl.pallas_call(functools.partial(entry_kernel, sizes), out_shape=[line_ou...  163 us
    pallas_call x1, Pallas kernels, exchange(): pl.pallas_call(functools.partial(exchange_kernel, sizes, specs), out_shap...  147 us
    dot_general x12, matrix products, mm(): return jnp.einsum(form, left, right, preferred_element_type=F32)  127 us
    pallas_call x1, Pallas kernels, grads(): pl.pallas_call(functools.partial(grads_kernel, sizes, specs), out_shape=b...  123 us
    pallas_call x1, Pallas kernels, attend_back(): pl.pallas_call(functools.partial(attend_back_kernel, sizes, heads, blocks...  63.7 us
    pallas_call x1, Pallas kernels, attend(): pl.pallas_call(functools.partial(attend_kernel, sizes, heads, blocks, spe...  61.8 us
    unnamed x64, local copies, waits for them, and re-layouts  26.7 us

profile of v2, /device:TPU:0, one launch (start us, length us, event | category | flops | bytes accessed | tf_op | source)
XLA Modules:
  0.0 1266.9 jit_solution(17649439605000560004)
XLA Ops:
  4.2 162.5 %entry.1 = (bf16[4,256,2048]{2,1,0:T(8,128)(2,1)}, bf16[4,256,2048]{2,1,0:T(8,128)(2,1)}, s32[4,16,256]{2,1,0:T(8,128)}, bf16[4,8,64,1280]{3,2,1,0:T(8,128)(2,1)...) custom-call(bf16[256,2048]{1,0:T(8,128)(2,1)} %bitcast.177, bf16[256,2048]{1,0:T(8,128)(2,1)} %bitcast.188, ...), custom_call_target="tpu_custom_call" | custom-call | tf_op jit(solution)/shard_map/entry/pallas_call | solution.py:375
  173.0 61.8 %attend.1 = (bf16[1024,2048]{1,0:T(8,128)(2,1)}, f32[1024,1280]{1,0:T(8,128)}, bf16[1024,1280]{1,0:T(8,128)(2,1)}, bf16[1024,1024]{1,0:T(8,128)(2,1)}, bf16[1024...) custom-call(s32[1]{0:T(128)} %copy.93.refs_0_.refs_6_, bf16[1024,2048]{1,0:T(8,128)(2,1)} %bitcast.184, ...), custom_call_target="tpu_custom_call" | custom-call | tf_op jit(solution)/shard_map/attend/pallas_call | solution.py:983
  235.7 8.1 convolution_convert_fusion.3
  243.7 151.1 %line_ffn.1 = (f32[256,2048]{1,0:T(8,128)}, bf16[4,256,2048]{2,1,0:T(8,128)(2,1)}, bf16[8,4,80,2048]{3,2,1,0:T(8,128)(2,1)}) custom-call(bf16[4,256,2048]{2,1,0:T(8,128)(2,1)} %bitcast.187, bf16[256,2048]{1,0:T(8,128)(2,1)} %bitcast.178, f32[1,2048]{1,0:T(1,128)} %bitcast.208, bf16[4,8,80,2048]{3,2,1,0:T(8,128)(2,1)} %bitcast.164), custom_call_target="tpu_custom_call" | custom-call | tf_op jit(solution)/shard_map/line_ffn/pallas_call | solution.py:864
  399.9 7.8 convolution_convert_fusion.2
  407.7 146.6 %exchange_4.1 = (bf16[8,4,80,2048]{3,2,1,0:T(8,128)(2,1)}, bf16[4,1,512,1536]{3,2,1,0:T(8,128)(2,1)}, f32[32,16,128]{2,1,0:T(8,128)}) custom-call(bf16[4,8,80,2048]{3,2,1,0:T(8,128)(2,1)} %bitcast.165, bf16[4,1,512,1536]{3,2,1,0:T(8,128)(2,1)} %bitcast.180, f32[32,16,128]{2,1,0:T(8,128)} %bitcast.196), custom_call_target="tpu_custom_call" | custom-call | tf_op jit(solution)/shard_map/exchange_4/pallas_call | solution.py:158
  555.3 13.6 %fusion.16 = bf16[8,4,1,80,768]{4,3,1,0,2:T(8,128)(2,1)} fusion(f32[8,4,80]{2,1,0:T(4,128)S(1)} %bitcast.213, bf16[8,4,80,2048]{3,2,1,0:T(8,128)(2,1)} %get-tuple-element.60, bf16[1,768,2048]{2,1,0:T(8,128)(2,1)} %get-tuple-element.59), kind=kOutput, calls=%fused_computation.29 | convolution fusion | flops 8056995840 | bytes 17573888 | tf_op jit(solution)/shard_map/asjcd,jhd->asjch/dot_general | solution.py:1159
  569.0 20.6 %convolution_bitcast_fusion = f32[8,4,1,80,1536]{4,3,1,0,2:T(8,128)S(1)} fusion(bf16[2048,1536,1,1]{1,0,3,2:T(8,128)(2,1)} %bitcast.230, bf16[8,4,80,2048]{3,2,1,0:T(8,128)(2,1)S(1)} %copy-done.1), kind=kOutput, calls=%fused_computation.25 | convolution fusion | flops 16106127360 | bytes 32505856 | tf_op jit(solution)/shard_map/asjcd,jdf->asjcf/dot_general | solution.py:1159
  589.6 11.9 multiply_convert_fusion
  601.5 7.0 pad_maximum_fusion.refs_3_
  608.5 16.6 %fusion.3 = (bf16[8,4,80,2048]{3,2,1,0:T(8,128)(2,1)}, f32[8,4,80]{2,1,0:T(4,128)S(1)}) fusion(f32[8,4,80]{2,1,0:T(4,128)S(1)} %bitcast.215, bf16[8,4,80,2048]{3,2,1,0:T(8,128)(2,1)} %get-tuple-element.60, bf16[8,4,1,80,768]{4,3,1,0,2:T(8,128)(2,1)} %get-tuple-element.127, bf16[1,768,2048]{2,1,0:T(8,128)(2,1)} %get-tuple-element.59), kind=kOutput, calls=%fused_computation.5 | convolution fusion | flops 8089761280 | bytes 28069888 | tf_op jit(solution)/shard_map/asjch,jhd->asjcd/dot_general | solution.py:1159
  625.9 22.0 %convert_bitcast_fusion.1.refs_0_ = bf16[8,4,80,2048]{3,2,1,0:T(8,128)(2,1)} fusion(bf16[2048,1536,1,1]{1,0,3,2:T(8,128)(2,1)} %bitcast.231, bf16[8,4,80,768]{3,2,1,0:T(8,128)(2,1)S(1)} %bitcast.171, bf16[8,4,80,768]{3,2,1,0:T(8,128)(2,1)} %bitcast.173), kind=kOutput, calls=%fused_computation.6 | convolution fusion | flops 16127098880 | bytes 24641536 | tf_op jit(solution)/shard_map/asjcf,jdf->asjcd/dot_general | solution.py:1159
  648.0 122.8 %grads.1 = (bf16[4,8,80,2048]{3,2,1,0:T(8,128)(2,1)}, f32[32,16,128]{2,1,0:T(8,128)}, bf16[4,512,1536]{2,1,0:T(8,128)(2,1)}, bf16[768,2048]{1,0:T(8,128)(2,1)}) custom-call(bf16[8,4,80,2048]{3,2,1,0:T(8,128)(2,1)} %convert_bitcast_fusion.1.refs_0_, f32[32,16,128]{2,1,0:T(8,128)} %bitcast.195, bf16[2560,2048]{1,0:T(8,128)(2,1)} %bitcast.176, ...), custom_call_target="tpu_custom_call" | custom-call | tf_op jit(solution)/shard_map/grads/pallas_call | solution.py:520
  774.3 9.2 convolution_convert_fusion.5.refs_0_
  785.0 164.7 %line_grad.1 = (f32[256,2048]{1,0:T(8,128)}, f32[1,2048]{1,0:T(1,128)}, bf16[4,256,2048]{2,1,0:T(8,128)(2,1)}, bf16[4,8,80,2048]{3,2,1,0:T(8,128)(2,1)}, f32[4,512,1536]{2,1,0:T(8,128)}) custom-call(bf16[4,256,2048]{2,1,0:T(8,128)(2,1)} %convolution_convert_fusion.5.refs_0_, f32[256,2048]{1,0:T(8,128)} %convert_select_fusion.refs_1_, f32[1,2048]{1,0:T(1,128)} %bitcast.209, ...), custom_call_target="tpu_custom_call" | custom-call | tf_op jit(solution)/shard_map/line_grad/pallas_call | solution.py:864
  949.7 63.7 %attend_back.1 = (bf16[1024,1280]{1,0:T(8,128)(2,1)}, bf16[1024,2048]{1,0:T(8,128)(2,1)}, f32[2,128]{1,0:T(2,128)}, bf16[4,1,768,512]{3,2,1,0:T(8,128)(2,1)}) custom-call(s32[1]{0:T(128)} %copy.93.refs_0_.refs_6_, f32[1024,1280]{1,0:T(8,128)} %get-tuple-element.51.refs_1_, bf16[1024,1280]{1,0:T(8,128)(2,1)} %get-tuple-element.52.refs_2_.refs_3_, ...), custom_call_target="tpu_custom_call" | custom-call | tf_op jit(solution)/shard_map/attend_back/pallas_call | solution.py:1116
  1017.5 9.9 convolution_convert_fusion
  1027.4 6.3 convolution_convert_fusion.6
  1033.7 9.3 convolution_convert_fusion.4.refs_1_
  1043.0 197.3 %line_last.1 = (f32[256,2048]{1,0:T(8,128)}, bf16[256,2048]{1,0:T(8,128)(2,1)}, f32[32,16,128]{2,1,0:T(8,128)}, f32[128,2048]{1,0:T(8,128)}, f32[64,5120]{1,0:T(...) custom-call(bf16[4,256,2048]{2,1,0:T(8,128)(2,1)} %bitcast.189, ...), custom_call_target="tpu_custom_call" | custom-call | tf_op jit(solution)/shard_map/line_last/pallas_call | solution.py:864
  1245.0 2.3 copy.94
  1247.3 3.1 copy.95
  1252.4 11.3 copy.98
  1263.7 2.7 copy.99
  (116 shorter events, 32.3 us)
Async XLA Ops:
  173.0 61.9 %copy-start.14 = (s32[4,16,256]{2,1,0:T(8,128)S(1)}, s32[4,16,256]{2,1,0:T(8,128)}, u32[]{:S(2)}) copy-start(s32[4,16,256]{2,1,0:T(8,128)} %get-tuple-element.53) | copy-start | bytes 196612
  235.6 164.2 %copy-start.2 = (pred[4,640,256]{2,1,0:T(32,128)(4,1)}, pred[4,640,256]{2,1,0:T(32,128)(4,1)S(1)}, u32[]{:S(2)}) copy-start(pred[4,640,256]{2,1,0:T(32,128)(4,1)S(1)} %bitcast_compare_fusion) | copy-start | bytes 1966084
  243.7 153.4 %copy-start.12 = (s32[1,256,8]{1,2,0:T(8,128)S(1)}, s32[1,256,8]{1,2,0:T(8,128)}, u32[]{:S(2)}) copy-start(s32[1,256,8]{1,2,0:T(8,128)} %param.14) | copy-start | bytes 24580
  243.7 154.6 %copy-start.15 = (s32[1,256,8]{1,2,0:T(8,128)S(1)}, s32[1,256,8]{1,2,0:T(8,128)}, u32[]{:S(2)}) copy-start(s32[1,256,8]{1,2,0:T(8,128)} %param.15) | copy-start | bytes 24580
  395.2 12.5 copy-start.4
  397.2 10.5 copy-start.10
  397.2 0.6 copy-start.17
  555.3 13.6 %copy-start.1 = (bf16[8,4,80,2048]{3,2,1,0:T(8,128)(2,1)S(1)}, bf16[8,4,80,2048]{3,2,1,0:T(8,128)(2,1)}, u32[]{:S(2)}) copy-start(bf16[8,4,80,2048]{3,2,1,0:T(8,128)(2,1)} %get-tuple-element.61) | copy-start | bytes 31457284
  608.5 17.4 %copy-start = (bf16[8,4,1,80,768]{4,3,1,0,2:T(8,128)(2,1)S(1)}, bf16[8,4,1,80,768]{4,3,1,0,2:T(8,128)(2,1)}, u32[]{:S(2)}) copy-start(bf16[8,4,1,80,768]{4,3,1,0,2:T(8,128)(2,1)} %get-tuple-element.130) | copy-start | bytes 11796484
  648.0 123.9 %copy-start.13 = (s32[1,256,8]{1,2,0:T(8,128)S(1)}, s32[1,256,8]{1,2,0:T(8,128)}, u32[]{:S(2)}) copy-start(s32[1,256,8]{1,2,0:T(8,128)} %param.14) | copy-start | bytes 24580
  648.0 123.9 %copy-start.16 = (s32[1,256,8]{1,2,0:T(8,128)S(1)}, s32[1,256,8]{1,2,0:T(8,128)}, u32[]{:S(2)}) copy-start(s32[1,256,8]{1,2,0:T(8,128)} %param.15) | copy-start | bytes 24580
  648.0 124.4 %copy-start.11 = (f32[256,8]{0,1:T(8,128)S(1)}, f32[256,8]{0,1:T(8,128)}, u32[]{:S(2)}) copy-start(f32[256,8]{0,1:T(8,128)} %copy-done.10) | copy-start | bytes 24580
  648.0 124.4 %copy-start.18 = (f32[256]{0:T(256)S(1)}, f32[256]{0:T(256)}, u32[]{:S(2)}) copy-start(f32[256]{0:T(256)} %copy-done.17) | copy-start | bytes 3076
  648.0 124.4 %copy-start.20 = (f32[256]{0:T(256)S(1)}, f32[256]{0:T(256)}, u32[]{:S(2)}) copy-start(f32[256]{0:T(256)} %copy-done.19) | copy-start | bytes 3076
  648.0 124.5 %copy-start.5 = (bf16[2048,32]{1,0:T(8,128)(2,1)S(1)}, bf16[2048,32]{1,0:T(8,128)(2,1)}, u32[]{:S(2)}) copy-start(bf16[2048,32]{1,0:T(8,128)(2,1)} %copy-done.4) | copy-start | bytes 393220
  648.0 126.3 %copy-start.3 = (pred[4,640,256]{2,1,0:T(32,128)(4,1)S(1)}, pred[4,640,256]{2,1,0:T(32,128)(4,1)}, u32[]{:S(2)}) copy-start(pred[4,640,256]{2,1,0:T(32,128)(4,1)} %copy-done.2) | copy-start | bytes 1966084
  774.3 9.2 copy-start.7
  949.7 63.7 %copy-start.21 = (f32[1,2048]{1,0:T(1,128)S(1)}, f32[1,2048]{1,0:T(1,128)}, u32[]{:S(2)}) copy-start(f32[1,2048]{1,0:T(1,128)} %get-tuple-element.74) | copy-start | bytes 24580
  1017.5 9.9 copy-start.6
  1017.5 9.9 copy-start.22
  1240.3 10.1 copy-start.8
  1240.3 11.1 copy-start.9
  1251.5 12.2 slice-start
  1252.4 11.3 slice-start.1
  (1 other events, 0.5 us)

commit v3 on v2

--- a/solution.py
+++ b/solution.py
@@ -15,7 +15,7 @@
 EPSILON = 1e-06
 THETA = 1000000.0
 MASKED = -1e30
-AHEAD = 2
+AHEAD = 1
 BF = jnp.bfloat16
 F32 = jnp.float32
 MESH = pl.DeviceIdType.MESH
@@ -67,7 +67,7 @@
 
 class Blocks:
     def __init__(self, sizes, specs, sources, results, sems):
-        self.own, self.away = [], []
+        self.own, self.parted = [], []
         if not specs:
             return
         send_sem, recv_sem, own_sem, *stages = sems
@@ -82,9 +82,10 @@
                     pltpu.make_async_copy(stages[i], result, own_sem.at[i, 1]),
                 )
             )
+            self.parted.append([])
             for step in range(1, total):
                 target = lax.rem(me + step, total)
-                self.away.append(
+                self.parted[-1].append(
                     pltpu.make_async_remote_copy(
                         src_ref=block_of(sources[i], before, target, total),
                         dst_ref=block_of(results[i], after, me, total),
@@ -96,18 +97,22 @@
                 )
 
     def start(self):
-        for copy in self.away:
-            copy.start()
+        for copies in self.parted:
+            for copy in copies:
+                copy.start()
         for inward, _ in self.own:
             inward.start()
 
     def wait(self):
-        for inward, outward in self.own:
-            inward.wait()
-            outward.start()
-        for _, outward in self.own:
-            outward.wait()
-        for copy in self.away:
+        for i in range(len(self.own)):
+            self.wait_one(i)
+
+    def wait_one(self, i):
+        inward, outward = self.own[i]
+        inward.wait()
+        outward.start()
+        outward.wait()
+        for copy in self.parted[i]:
             copy.wait()
 
 
@@ -449,12 +454,21 @@
     return scratch
 
 
-def grads_kernel(sizes, specs, *refs):
+def grads_kernel(sizes, specs, combined, *refs):
     S = sizes["seq"]
     count = len(specs)
-    sources, (x_any, gu_any, ph_any, g_any) = refs[:count], refs[count : count + 4]
-    results, (up_out, down_out) = refs[count + 4 : 2 * count + 4], refs[2 * count + 4 : 2 * count + 6]
-    x_ref, gu_ref, ph_ref, g_ref, up_stage, down_stage, in_sem, up_send, up_recv, out_sem, *sems = refs[2 * count + 6 :]
+    refs = list(refs)
+
+    def take(number):
+        taken, refs[:number] = refs[:number], []
+        return taken
+
+    sources, (x_any, gu_any, ph_any, g_any) = take(count), take(4)
+    combine = take(1) if combined else None
+    results, (up_out, down_out) = take(count), take(2)
+    part_out = take(1) if combined else None
+    x_ref, gu_ref, ph_ref, g_ref, up_stage, down_stage = take(6)
+    in_sem, up_send, up_recv, out_sem, back_sem, *sems = refs
     s = lax.axis_index("seq")
     inward = [
         pltpu.make_async_copy(source, target, in_sem.at[i])
@@ -506,32 +520,230 @@
     copy = pltpu.make_async_copy(down_stage, down_out, out_sem.at[1])
     copy.start()
     sent.append(copy)
-    blocks.wait()
+    blocks.wait_one(0)
+    if combined:
+        back = results[0]
+        groups, slots = back.shape[1], back.shape[2]
+        pieces = []
+        for block_at in range(S):
+            for group in range(groups):
+                row = pl.ds((block_at * groups + group) * slots, slots)
+                pieces.append(
+                    pltpu.make_async_copy(
+                        back.at[block_at, group], x_ref.at[row], back_sem.at[block_at, group]
+                    )
+                )
+                pieces[-1].start()
+        for copy in pieces:
+            copy.wait()
+        reach = groups * slots
+        for block_at in range(S):
+
+            def one_part(at):
+                part_out[0][block_at, :, at] = lax.dot_general(
+                    combine[0][block_at], x_ref[block_at * reach : (block_at + 1) * reach, at],
+                    over_rows, preferred_element_type=F32,
+                ).astype(BF)
+
+            tiles(part_out[0].shape[2], 512, one_part)
+    for i in range(1, count):
+        blocks.wait_one(i)
     for copy in sent:
         copy.wait()
 
 
-def grads(arrays, specs, rows, grad_gu, hidden, grad_out, sizes, collective_id):
+def grads(arrays, specs, rows, grad_gu, hidden, grad_out, select, sizes, collective_id):
     S = sizes["seq"]
+    combined = select is not None
+    groups = arrays[0].shape[0]
     part = rows.shape[1] // S
     up_block = (part, grad_gu.shape[1])
     down = (hidden.shape[1], grad_out.shape[1])
     inner = [rows, grad_gu, hidden, grad_out]
     return pl.pallas_call(
-        functools.partial(grads_kernel, sizes, specs),
+        functools.partial(grads_kernel, sizes, specs, combined),
         out_shape=block_outs(sizes, arrays, specs)
-        + [jax.ShapeDtypeStruct((S,) + up_block, BF), jax.ShapeDtypeStruct(down, BF)],
-        in_specs=[ANY] * (len(arrays) + 4),
-        out_specs=[ANY] * (len(arrays) + 2),
+        + [jax.ShapeDtypeStruct((S,) + up_block, BF), jax.ShapeDtypeStruct(down, BF)]
+        + ([jax.ShapeDtypeStruct((S, select.shape[2], rows.shape[1]), BF)] if combined else []),
+        in_specs=[ANY] * (len(arrays) + 4) + [VM] * combined,
+        out_specs=[ANY] * (len(arrays) + 2) + [VM] * combined,
         scratch_shapes=[pltpu.VMEM(array.shape, BF) for array in inner]
         + [pltpu.VMEM((S,) + up_block, BF), pltpu.VMEM(down, BF)]
-        + [DMA((4,)), DMA((S,)), DMA((S,)), DMA((2,))]
+        + [DMA((4,)), DMA((S,)), DMA((S,)), DMA((2,)), DMA((S, groups))]
         + block_scratch(sizes, arrays, specs),
         compiler_params=pltpu.CompilerParams(
             collective_id=collective_id, has_side_effects=True, vmem_limit_bytes=60 << 20
         ),
         name="grads",
-    )(*arrays, *inner)
+    )(*arrays, *inner, *([select] if combined else []))
+
+
+def dispatch_kernel(sizes, specs, *refs):
+    S, F = sizes["seq"], sizes["fsdp"]
+    count = len(specs)
+    refs = list(refs)
+
+    def take(number):
+        taken, refs[:number] = refs[:number], []
+        return taken
+
+    sources = take(count)
+    tok_any, g_any, down_any, select_ref = take(4)
+    results = take(count)
+    rows_out, through_out = take(2)
+    tok_ref, rows_ref, g_ref, down_ref, through_ref, row_send, row_recv, own_sem, in_sem, out_sem, *sems = refs
+    f = lax.axis_index("fsdp")
+    slots = rows_out.shape[2]
+    met = greet(sizes)
+    inward = [pltpu.make_async_copy(tok_any.at[b], tok_ref.at[b], in_sem.at[b]) for b in range(S)]
+    inward.append(pltpu.make_async_copy(down_any, down_ref, in_sem.at[S]))
+    inward.append(pltpu.make_async_copy(g_any, g_ref, in_sem.at[S + 1]))
+    for copy in inward:
+        copy.start()
+    blocks = Blocks(sizes, specs, sources, results, sems)
+    met()
+    sent = []
+    for b in range(S):
+        inward[b].wait()
+
+        def one(at):
+            rows_ref[b, :, at] = jnp.dot(
+                select_ref[b], tok_ref[b, :, at], preferred_element_type=F32
+            ).astype(BF)
+
+        tiles(rows_ref.shape[2], 512, one)
+        for step in range(1, F):
+            target = lax.rem(f + step, F)
+            copy = pltpu.make_async_remote_copy(
+                src_ref=rows_ref.at[b, pl.ds(pl.multiple_of(target * slots, 16), slots)],
+                dst_ref=rows_out.at[f, b],
+                send_sem=row_send.at[b, step], recv_sem=row_recv.at[b, step],
+                device_id={"fsdp": target}, device_id_type=MESH,
+            )
+            copy.start()
+            sent.append(copy)
+        copy = pltpu.make_async_copy(
+            rows_ref.at[b, pl.ds(pl.multiple_of(f * slots, 16), slots)], rows_out.at[f, b], own_sem.at[b]
+        )
+        copy.start()
+        sent.append(copy)
+        if b == 0:
+            blocks.start()
+    inward[S].wait()
+    inward[S + 1].wait()
+    span = through_ref.shape[1]
+    outward = []
+    for n in range(g_ref.shape[0] // span):
+        if n >= 2:
+            outward[n - 2].wait()
+        own = pl.ds(n * span, span)
+
+        def one_through(at):
+            through_ref[n % 2, :, at] = lax.dot_general(
+                g_ref[own, :], down_ref[at, :], (((1,), (1,)), ((), ())), preferred_element_type=F32
+            )
+
+        tiles(through_ref.shape[2], 256, one_through)
+        outward.append(pltpu.make_async_copy(through_ref.at[n % 2], through_out.at[own], out_sem.at[n % 2]))
+        outward[-1].start()
+    for copy in outward[-2:]:
+        copy.wait()
+    blocks.wait()
+    for copy in sent:
+        copy.wait()
+
+
+def dispatch(arrays, specs, tokens, grads_in, w_down, select, sizes, collective_id):
+    S, F = sizes["seq"], sizes["fsdp"]
+    slots = select.shape[1] // F
+    width = tokens.shape[2]
+    count = grads_in.shape[0]
+    hidden = w_down.shape[0]
+    span = 512
+    return pl.pallas_call(
+        functools.partial(dispatch_kernel, sizes, specs),
+        out_shape=block_outs(sizes, arrays, specs)
+        + [
+            jax.ShapeDtypeStruct((F, S, slots, width), BF),
+            jax.ShapeDtypeStruct((count, hidden), F32),
+        ],
+        in_specs=[ANY] * (len(arrays) + 3) + [VM],
+        out_specs=[ANY] * (len(arrays) + 2),
+        scratch_shapes=[
+            pltpu.VMEM(tokens.shape, BF),
+            pltpu.VMEM((S, select.shape[1], width), BF),
+            pltpu.VMEM(grads_in.shape, BF),
+            pltpu.VMEM(w_down.shape, BF),
+            pltpu.VMEM((2, span, hidden), F32),
+            DMA((S, F)), DMA((S, F)), DMA((S,)), DMA((S + 2,)), DMA((2,)),
+        ] + block_scratch(sizes, arrays, specs),
+        compiler_params=pltpu.CompilerParams(
+            collective_id=collective_id, has_side_effects=True, vmem_limit_bytes=58 << 20
+        ),
+        name="dispatch",
+    )(*arrays, tokens, grads_in, w_down, select)
+
+
+def expert_kernel(
+    x_ref, gate_ref, through_ref, g_ref, up_w, down_w,
+    moe_ref, back_ref, gu_ref, gated_ref, prob_ref, hidden_ref,
+):
+    hidden = hidden_ref.shape[1]
+    width = x_ref.shape[1]
+    row_gate = gate_ref[...]
+    for at in range(0, hidden, 256):
+        low = slice(at, at + 256)
+        high = slice(hidden + at, hidden + at + 256)
+        gate = jnp.dot(x_ref[...], up_w[:, low], preferred_element_type=F32)
+        up = jnp.dot(x_ref[...], up_w[:, high], preferred_element_type=F32)
+        sigmoid = jax.nn.sigmoid(gate)
+        silu = gate * sigmoid
+        value = (silu * up).astype(BF)
+        hidden_ref[:, low] = value
+        gated_ref[:, low] = (row_gate * value.astype(F32)).astype(BF)
+        grad = (row_gate * through_ref[:, low]).astype(BF).astype(F32)
+        gu_ref[:, low] = (grad * up * sigmoid * (1.0 + gate * (1.0 - sigmoid))).astype(BF)
+        gu_ref[:, high] = (grad * silu).astype(BF)
+    prob = jnp.zeros_like(row_gate)
+    for at in range(0, width, 256):
+        here = slice(at, at + 256)
+        out = jnp.dot(hidden_ref[...], down_w[:, here], preferred_element_type=F32)
+        out = out.astype(BF).astype(F32)
+        moe_ref[:, here] = (row_gate * out).astype(BF)
+        prob = prob + jnp.sum(out * g_ref[:, here].astype(F32), axis=-1, keepdims=True)
+        back_ref[:, here] = lax.dot_general(
+            gu_ref[...], up_w[here, :], (((1,), (1,)), ((), ())), preferred_element_type=F32
+        ).astype(BF)
+    prob_ref[...] = prob
+
+
+def expert(x, row_gate, through, g, up_w, down_w, steps):
+    count, width = x.shape
+    hidden = down_w.shape[0]
+    rows = count // steps
+
+    def by_rows(columns):
+        return pl.BlockSpec((rows, columns), lambda i: (i, 0))
+
+    def whole(array):
+        return pl.BlockSpec(array.shape, lambda i: (0, 0), pipeline_mode=pl.Buffered(1))
+
+    return pl.pallas_call(
+        expert_kernel,
+        grid=(steps,),
+        out_shape=[
+            jax.ShapeDtypeStruct((count, width), BF),
+            jax.ShapeDtypeStruct((count, width), BF),
+            jax.ShapeDtypeStruct((count, 2 * hidden), BF),
+            jax.ShapeDtypeStruct((count, hidden), BF),
+            jax.ShapeDtypeStruct((count, 1), F32),
+        ],
+        in_specs=[by_rows(width), by_rows(1), by_rows(hidden), by_rows(width), whole(up_w), whole(down_w)],
+        out_specs=[by_rows(width), by_rows(width), by_rows(2 * hidden), by_rows(hidden), by_rows(1)],
+        scratch_shapes=[pltpu.VMEM((rows, hidden), BF)],
+        compiler_params=pltpu.CompilerParams(vmem_limit_bytes=60 << 20),
+        name="expert",
+    )(x, row_gate, through, g, up_w, down_w)
 
 
 def line_kernel(sizes, chunks, mode, parts, extra, widened, *refs):
@@ -1203,7 +1415,7 @@
     router_size = w_router.size
     part_width = w_gate_up.shape[1]
     down_width = w_down.shape[2]
-    assert KH == S and local_experts % S == 0
+    assert KH == S and own_experts == 1
 
     small_send = lanes(jnp.concatenate([w_router.reshape(-1), norm_gains])[None], 1)[0]
     table = jnp.concatenate([routes[0].T, slots[0].T])
@@ -1243,13 +1455,11 @@
     one_hot = plane_slots[:, :, None, :] == slot_ids[None, None, :, None]
     select = one_hot.astype(BF).reshape(S, F * own_experts * capacity, tok_count)
     grouped = (S, F, own_experts * capacity, width)
-    shape5 = (F, S, own_experts, capacity, width)
 
     cot_rows = mm("brt,btd->brd", select, cot_all).astype(BF).reshape(grouped)
     residual, ffn_all, g_rows = line(
         "ffn", sizes, [o_part], [tokens[0], gain_ffn], [cot_rows], ((("fsdp",), 1, 0),), 2
     )
-    g_rows = g_rows.reshape(shape5)
     ffn_low = lax.dynamic_index_in_dim(ffn_all, seq_at, 0, keepdims=False)
 
     route_rows = routes[0]
@@ -1274,56 +1484,39 @@
 
     gate_send = to_devices(gate_slots)
 
-    ffn_rows = mm("brt,btd->brd", select, ffn_all).astype(BF).reshape(grouped)
-    x_rows, gate_up_w, gate_got = exchange(
-        [ffn_rows, w_gate_up.reshape((S, own_experts) + w_gate_up.shape[1:]), gate_send],
-        ((("fsdp",), 1, 0), (("seq",), 0, 0), (EVERY, 0, 0)), sizes, 4,
-    )
-    gate_up_w = gate_up_w.transpose(1, 0, 2, 3).reshape(own_experts, width, 2 * FF)
-    x_rows = x_rows.reshape(shape5)
-    row_gate = gate_got.reshape(S, F, -1)[:, :, : own_experts * capacity]
-    row_gate = row_gate.transpose(1, 0, 2).reshape(F, S, own_experts, capacity, 1)
-
-    gate_up = mm("asjcd,jdf->asjcf", x_rows, gate_up_w)
-    gate_part = gate_up[..., :FF]
-    up_part = gate_up[..., FF:]
-    hidden_low = (jax.nn.silu(gate_part) * up_part).astype(BF)
-    expert_out = mm("asjch,jhd->asjcd", hidden_low, down_w).astype(BF)
-    out_wide = expert_out.astype(F32)
-    grad_prob_rows = jnp.sum(out_wide * g_rows.astype(F32), axis=-1)
-    moe_rows = (row_gate * out_wide).astype(BF)
-
-    through_down = mm("asjcd,jhd->asjch", g_rows, down_w)
-    grad_hidden = lax.optimization_barrier((row_gate * through_down).astype(BF)).astype(F32)
-    gated_hidden = (row_gate * hidden_low.astype(F32)).astype(BF)
-    sigmoid_gate = jax.nn.sigmoid(gate_part)
-    grad_gate = grad_hidden * up_part * sigmoid_gate * (1.0 + gate_part * (1.0 - sigmoid_gate))
-    grad_up = grad_hidden * gate_part * sigmoid_gate
-    grad_gu_low = jnp.concatenate([grad_gate, grad_up], axis=-1).astype(BF)
-    grad_rows = mm("asjcf,jdf->asjcd", grad_gu_low, gate_up_w).astype(BF)
-    prob_send = grad_prob_rows.reshape(F, S, -1).transpose(1, 0, 2).reshape(N, -1)
-    back_layout = grad_rows.reshape(F, S, own_experts * capacity, width)
-    back_blocks = [back_layout, lanes(prob_send, N)]
-    back_specs = ((("fsdp",), 0, 1), (EVERY, 0, 0))
-    if own_experts == 1:
-        grad_back, prob_got, up_got, down_term = grads(
-            back_blocks, back_specs, x_rows.reshape(-1, width), grad_gu_low.reshape(-1, 2 * FF),
-            gated_hidden.reshape(-1, FF), g_rows.reshape(-1, width), sizes, 6,
+    up_blocks = w_gate_up.reshape((S, own_experts) + w_gate_up.shape[1:])
+    side_specs = ((("seq",), 0, 0), (EVERY, 0, 0))
+    g_flat = g_rows.reshape(-1, width)
+    fused = capacity % 16 == 0
+    if fused:
+        gate_up_w, gate_got, x_rows, through = dispatch(
+            [up_blocks, gate_send], side_specs, ffn_all, g_flat, down_w[0], select, sizes, 4
         )
-        down_term = down_term[None]
     else:
-        up_term = mm("asjcd,asjcf->jdf", x_rows, grad_gu_low).astype(BF)
-        down_term = mm("asjch,asjcd->jhd", gated_hidden, g_rows).astype(BF)
-        up_blocks = up_term.reshape(own_experts, S, part_width, 2 * FF).transpose(1, 0, 2, 3)
-        grad_back, prob_got, up_got = exchange(
-            back_blocks + [up_blocks], back_specs + ((("seq",), 0, 0),), sizes, 6
+        ffn_rows = mm("brt,btd->brd", select, ffn_all).astype(BF).reshape(grouped)
+        gate_up_w, gate_got, x_rows = exchange(
+            [up_blocks, gate_send, ffn_rows], side_specs + ((("fsdp",), 1, 0),), sizes, 4
         )
-    up_got = up_got.reshape(w_gate_up.shape)
-    prob_slots = prob_got.reshape(S, F, -1)[:, :, : own_experts * capacity]
-    prob_slots = prob_slots.reshape(S, F, own_experts, capacity).transpose(1, 0, 2, 3)
+        through = mm("rd,hd->rh", g_flat, down_w[0])
+    row_gate = gate_got.reshape(S, F, -1)[:, :, :capacity].transpose(1, 0, 2).reshape(-1, 1)
+    x_flat = x_rows.reshape(-1, width)
+    moe_rows, grad_rows, grad_gu_low, gated_hidden, prob_rows = expert(
+        x_flat, row_gate, through, g_flat, gate_up_w.reshape(width, 2 * FF), down_w[0], 5
+    )
+    prob_send = prob_rows.reshape(F, S, -1).transpose(1, 0, 2).reshape(N, -1)
+    back_blocks = [grad_rows.reshape(F, S, capacity, width), lanes(prob_send, N)]
+    grad_back, prob_got, up_got, down_term, *grad_part = grads(
+        back_blocks, ((("fsdp",), 0, 1), (EVERY, 0, 0)), x_flat, grad_gu_low, gated_hidden, g_flat,
+        select if fused else None, sizes, 6,
+    )
+    if fused:
+        (grad_part,) = grad_part
+    else:
+        grad_part = mm("brt,brd->btd", select, grad_back.reshape(S, -1, width)).astype(BF)
+    grad_gate_up = up_got.reshape(w_gate_up.shape).astype(F32)
+    prob_slots = prob_got.reshape(S, F, -1)[:, :, :capacity].transpose(1, 0, 2)
     prob_slots = prob_slots.reshape(expert_count, capacity)
 
-    grad_part = mm("brt,brd->btd", select, grad_back.reshape(S, -1, width)).astype(BF)
 
     prob_of_route = jnp.einsum(
         "tke,ec->tkc", picked.astype(F32), prob_slots, precision=lax.Precision.HIGHEST
@@ -1336,43 +1529,49 @@
     grad_router_part = mm("td,te->de", ffn_low, grad_logits)
     valid = (seq_at * tok_count + jnp.arange(tok_count, dtype=jnp.int32)) < lengths[0]
     grad_final = jnp.where(valid[:, None], cotangent[0].astype(F32), 0.0)
-    grad_residual, grad_gain_ffn, grad_attn_low, moe_back, grad_gate_up = line(
+    grad_residual, grad_gain_ffn, grad_attn_low, moe_back = line(
         "grad", sizes, [grad_part], [grad_final, gain_ffn, residual, grad_ffn_add],
-        [moe_rows.reshape(F, S, own_experts * capacity, width)], ((("fsdp",), 0, 1),), 7,
-        widened=(up_got,),
+        [moe_rows.reshape(F, S, capacity, width)], ((("fsdp",), 0, 1),), 7,
     )
     grad_attn_low = grad_attn_low.reshape(seq_total, width)
 
     grad_proj, attn_part, grad_gain_heads, down_got = attend_back(
         lengths, projected, qkv_low, grad_attn_low, out_own, w_proj, cosine, sine, gain_heads,
-        heads, [down_term], ((("seq",), "columns", 0),), sizes, 9,
+        heads, [down_term[None]], ((("seq",), "columns", 0),), sizes, 9,
     )
     attn_part = attn_part.reshape(S, tok_count, width)
     grad_out_part = mm("te,td->ed", o_low, grad_attn_low).astype(BF)
     grad_qkv_part = mm("td,te->de", attn_low, grad_proj).astype(BF).reshape(S, F, w_rows, own_width)
     moe_part = mm("brt,brd->btd", select, moe_back.reshape(S, -1, width)).astype(BF)
-    router_blocks = lanes(grad_router_part.reshape(N, -1), N)
-    early_gains = lanes(jnp.concatenate([grad_gain_ffn[0], grad_gain_heads.reshape(-1)])[None], 1)[0]
+    early_gains = jnp.concatenate(
+        [jnp.zeros((width,), F32), grad_gain_ffn[0], grad_gain_heads.reshape(-1)]
+    )
+    small_blocks = jnp.concatenate(
+        [grad_router_part.reshape(N, -1), early_gains.reshape(N, -1)], axis=1
+    )
+    small_rows = -(-small_blocks.shape[1] // 1024) * 8
+    small_blocks = jnp.pad(small_blocks, ((0, 0), (0, small_rows * 128 - small_blocks.shape[1])))
+    small_blocks = small_blocks.reshape(N, small_rows, 128)
     (
-        grad_inputs, final, late_gains, grad_out, grad_qkv, router_got, gains_got, grad_down
+        grad_inputs, final, late_gains, grad_out, grad_qkv, small_got
     ) = line(
         "last", sizes, [attn_part, moe_part],
         [
             grad_residual, gain_attn[None], residual, tokens[0], lengths,
             grad_out_part.reshape(F, -1, width), grad_qkv_part,
         ],
-        [router_blocks, early_gains], ((EVERY, 0, 0), (EVERY, None, 0)), 8,
-        widened=(down_got.reshape(w_down.shape),),
-    )
-    grad_router = jnp.sum(router_got, axis=0).reshape(-1)[:router_size].reshape(w_router.shape)
-    gain_sum = jnp.concatenate(
-        [
-            jnp.sum(late_gains, axis=0).reshape(-1),
-            jnp.sum(gains_got, axis=0).reshape(-1)[: width + 2 * HD],
-        ]
+        [small_blocks], ((EVERY, 0, 0),), 8,
+    )
+    grad_down = down_got.reshape(w_down.shape).astype(F32)
+    small_sum = jnp.sum(small_got, axis=0).reshape(-1)
+    grad_router = small_sum[:router_size].reshape(w_router.shape)
+    late_sum = jnp.concatenate(
+        [jnp.sum(late_gains, axis=0).reshape(-1), jnp.zeros((width + 2 * HD,), F32)]
     )
     device_at = seq_at * F + lax.axis_index("fsdp")
-    grad_gains = lax.dynamic_slice_in_dim(gain_sum, device_at * small, small, 0)
+    grad_gains = small_sum[router_size : router_size + small] + lax.dynamic_slice_in_dim(
+        late_sum, device_at * small, small, 0
+    )
     return (
         final[None],
         grad_inputs[None],

time: 1280 us -> 1200 us (0.938)
  matrix products: 129 us -> 35.7 us
  Pallas kernels: 1070 us -> 1110 us
  local copies, waits for them, and re-layouts: 32.4 us -> 15.8 us
    dot_general x12 -> x6, matrix products: 127 us -> 33.6 us  [mm(): return jnp.einsum(form, left, right, preferred_element_type=F32)]
    pallas_call x2 -> x3, Pallas kernels: 269 us -> 338 us  [the longest x1 149 us: dispatch(): pl.pallas_call(functools.partial(dispatch_kernel, sizes, specs), out_shap...]
    pallas_call x3, Pallas kernels: 513 us -> 486 us  [line(): pl.pallas_call(functools.partial(line_kernel, sizes, chunks, mode, len(pa...]
    unnamed x64 -> x43, local copies, waits for them, and re-layouts: 26.7 us -> 9.27 us
where the time goes in v3:
time: 1200 us; the launch traced here: 1190 us
  Pallas kernels  1110 us (92%)
  matrix products  35.7 us (3%)
  other arithmetic  28.2 us (2%)
  local copies, waits for them, and re-layouts  15.8 us (1%)
    pallas_call x3, Pallas kernels, line(): pl.pallas_call(functools.partial(line_kernel, sizes, chunks, mode, len(pa...  486 us
    pallas_call x1, Pallas kernels, entry(): pl.pallas_call(functools.partial(entry_kernel, sizes), out_shape=[line_ou...  163 us
    pallas_call x1, Pallas kernels, dispatch(): pl.pallas_call(functools.partial(dispatch_kernel, sizes, specs), out_shap...  149 us
    pallas_call x1, Pallas kernels, grads(): pl.pallas_call(functools.partial(grads_kernel, sizes, specs, combined), o...  135 us
    pallas_call x1, Pallas kernels, attend_back(): pl.pallas_call(functools.partial(attend_back_kernel, sizes, heads, blocks...  63.7 us
    pallas_call x1, Pallas kernels, attend(): pl.pallas_call(functools.partial(attend_kernel, sizes, heads, blocks, spe...  61.9 us
    pallas_call x1, Pallas kernels, expert(): pl.pallas_call(expert_kernel, grid=(steps,), out_shape=[jax.ShapeDtypeStr...  53.5 us
    dot_general x6, matrix products, mm(): return jnp.einsum(form, left, right, preferred_element_type=F32)  33.6 us

profile of v3, /device:TPU:0, one launch (start us, length us, event | category | flops | bytes accessed | tf_op | source)
XLA Modules:
  0.0 1194.0 jit_solution(7469413732872251944)
XLA Ops:
  0.6 1.3 pad_add_fusion.table_ref
  4.2 162.5 %entry.1 = (bf16[4,256,2048]{2,1,0:T(8,128)(2,1)}, bf16[4,256,2048]{2,1,0:T(8,128)(2,1)}, s32[4,16,256]{2,1,0:T(8,128)}, bf16[4,8,64,1280]{3,2,1,0:T(8,128)(2,1)...) custom-call(bf16[256,2048]{1,0:T(8,128)(2,1)} %bitcast.110, bf16[256,2048]{1,0:T(8,128)(2,1)} %bitcast.120, ...), custom_call_target="tpu_custom_call" | custom-call | tf_op jit(solution)/shard_map/entry/pallas_call | solution.py:380
  169.1 1.9 fusion.8
  173.0 61.9 %attend.1 = (bf16[1024,2048]{1,0:T(8,128)(2,1)}, f32[1024,1280]{1,0:T(8,128)}, bf16[1024,1280]{1,0:T(8,128)(2,1)}, bf16[1024,1024]{1,0:T(8,128)(2,1)}, bf16[1024...) custom-call(s32[1]{0:T(128)} %copy.79.refs_0_.refs_6_, bf16[1024,2048]{1,0:T(8,128)(2,1)} %bitcast.116, ...), custom_call_target="tpu_custom_call" | custom-call | tf_op jit(solution)/shard_map/attend/pallas_call | solution.py:1195
  235.2 1.6 fusion.18
  236.8 7.8 convolution_convert_fusion.1
  244.6 144.4 %line_ffn.1 = (f32[256,2048]{1,0:T(8,128)}, bf16[4,256,2048]{2,1,0:T(8,128)(2,1)}, bf16[8,4,80,2048]{3,2,1,0:T(8,128)(2,1)}) custom-call(bf16[4,256,2048]{2,1,0:T(8,128)(2,1)} %bitcast.117, bf16[256,2048]{1,0:T(8,128)(2,1)} %bitcast.111, f32[1,2048]{1,0:T(1,128)} %bitcast.142, bf16[4,8,80,2048]{3,2,1,0:T(8,128)(2,1)} %bitcast.99), custom_call_target="tpu_custom_call" | custom-call | tf_op jit(solution)/shard_map/line_ffn/pallas_call | solution.py:1076
  389.4 1.6 fusion.3
  392.8 149.3 %dispatch.1 = (bf16[4,1,512,1536]{3,2,1,0:T(8,128)(2,1)}, f32[32,16,128]{2,1,0:T(8,128)}, bf16[8,4,80,2048]{3,2,1,0:T(8,128)(2,1)}, f32[2560,768]{1,0:T(8,128)}) custom-call(bf16[4,1,512,1536]{3,2,1,0:T(8,128)(2,1)} %bitcast.114, f32[32,16,128]{2,1,0:T(8,128)} %bitcast.128, bf16[4,256,2048]{2,1,0:T(8,128)(2,1)} %get-tuple-element.59.refs_2_, ...), custom_call_target="tpu_custom_call" | custom-call | tf_op jit(solution)/shard_map/dispatch/pallas_call | solution.py:663
  543.1 1.7 reshape.300.gate_ref
  544.8 53.5 %expert.1 = (bf16[2560,2048]{1,0:T(8,128)(2,1)}, bf16[2560,2048]{1,0:T(8,128)(2,1)}, bf16[2560,1536]{1,0:T(8,128)(2,1)}, bf16[2560,768]{1,0:T(8,128)(2,1)}, f32[2560,1]{1,0:T(8,128)}) custom-call(bf16[2560,2048]{1,0:T(8,128)(2,1)} %bitcast.100, f32[2560,1]{1,0:T(8,128)} %reshape.300.gate_ref, f32[2560,768]{1,0:T(8,128)} %get-tuple-element.64.through_ref, ...), custom_call_target="tpu_custom_call" | custom-call | tf_op jit(solution)/shard_map/expert/pallas_call | solution.py:731
  598.3 1.7 reduce.1
  600.9 135.0 %grads.1 = (bf16[4,8,80,2048]{3,2,1,0:T(8,128)(2,1)}, f32[32,16,128]{2,1,0:T(8,128)}, bf16[4,512,1536]{2,1,0:T(8,128)(2,1)}, bf16[768,2048]{1,0:T(8,128)(2,1)}, bf16[4,256,2048]{2,1,0:T(8,128)(2,1)}) custom-call(bf16[8,4,80,2048]{3,2,1,0:T(8,128)(2,1)} %bitcast.109, f32[32,16,128]{2,1,0:T(8,128)} %bitcast.127, bf16[2560,2048]{1,0:T(8,128)(2,1)} %bitcast.101, ...), custom_call_target="tpu_custom_call" | custom-call | tf_op jit(solution)/shard_map/grads/pallas_call | solution.py:563
  737.7 1.7 fusion.1
  739.9 1.8 fusion.22.refs_4_
  741.7 1.5 convert_select_fusion.refs_1_
  743.2 149.4 %line_grad.1 = (f32[256,2048]{1,0:T(8,128)}, f32[1,2048]{1,0:T(1,128)}, bf16[4,256,2048]{2,1,0:T(8,128)(2,1)}, bf16[4,8,80,2048]{3,2,1,0:T(8,128)(2,1)}) custom-call(bf16[4,256,2048]{2,1,0:T(8,128)(2,1)} %get-tuple-element.70.refs_0_, f32[256,2048]{1,0:T(8,128)} %convert_select_fusion.refs_1_, f32[1,2048]{1,0:T(1,128)} %bitcast.143, ...), custom_call_target="tpu_custom_call" | custom-call | tf_op jit(solution)/shard_map/line_grad/pallas_call | solution.py:1076
  892.6 63.7 %attend_back.1 = (bf16[1024,1280]{1,0:T(8,128)(2,1)}, bf16[1024,2048]{1,0:T(8,128)(2,1)}, f32[2,128]{1,0:T(2,128)}, bf16[4,1,768,512]{3,2,1,0:T(8,128)(2,1)}) custom-call(s32[1]{0:T(128)} %copy.79.refs_0_.refs_6_, f32[1024,1280]{1,0:T(8,128)} %get-tuple-element.54.refs_1_, bf16[1024,1280]{1,0:T(8,128)(2,1)} %get-tuple-element.55.refs_2_.refs_3_, ...), custom_call_target="tpu_custom_call" | custom-call | tf_op jit(solution)/shard_map/attend_back/pallas_call | solution.py:1328
  958.0 10.7 convolution_convert_fusion
  968.7 6.3 convolution_convert_fusion.3
  975.0 5.3 convolution_convert_fusion.2.refs_1_
  980.3 192.3 %line_last.1 = (f32[256,2048]{1,0:T(8,128)}, bf16[256,2048]{1,0:T(8,128)(2,1)}, f32[32,16,128]{2,1,0:T(8,128)}, f32[128,2048]{1,0:T(8,128)}, f32[64,5120]{1,0:T(8,128)}, /*index=5*/f32[32,24,128]{2,1,0:T(8,128)}) custom-call(bf16[4,256,2048]{2,1,0:T(8,128)(2,1)} %bitcast.121, bf16[4,256,2048]{2,1,0:T(8,128)(2,1)} %convolution_convert_fusion.2.refs_1_, ...), custom_call_target="tpu_custom_call" | custom-call | tf_op jit(solution)/shard_map/line_last/pallas_call | solution.py:1076
  1176.1 3.6 bitcast_convert_fusion
  1179.7 9.5 convert_element_type.73
  (93 shorter events, 21.7 us)
Async XLA Ops:
  173.0 61.9 %copy-start.8 = (s32[4,16,256]{2,1,0:T(8,128)S(1)}, s32[4,16,256]{2,1,0:T(8,128)}, u32[]{:S(2)}) copy-start(s32[4,16,256]{2,1,0:T(8,128)} %get-tuple-element.57) | copy-start | bytes 196612
  244.6 146.5 %copy-start.7 = (s32[1,256,8]{1,2,0:T(8,128)S(1)}, s32[1,256,8]{1,2,0:T(8,128)}, u32[]{:S(2)}) copy-start(s32[1,256,8]{1,2,0:T(8,128)} %param.14) | copy-start | bytes 24580
  244.6 146.7 %copy-start.9 = (s32[1,256,8]{1,2,0:T(8,128)S(1)}, s32[1,256,8]{1,2,0:T(8,128)}, u32[]{:S(2)}) copy-start(s32[1,256,8]{1,2,0:T(8,128)} %param.15) | copy-start | bytes 24580
  736.0 5.7 copy-start.1
  892.6 63.8 %copy-start.10 = (f32[1,2048]{1,0:T(1,128)S(1)}, f32[1,2048]{1,0:T(1,128)}, u32[]{:S(2)}) copy-start(f32[1,2048]{1,0:T(1,128)} %get-tuple-element.82) | copy-start | bytes 24580
  957.1 17.9 %slice-start = ((s8[10485760]{0:T(1024)(128)(4,1)}), s8[4194304]{0:T(1024)(128)(4,1)S(1)}, s32[]{:S(2)}) async-start(s8[10485760]{0:T(1024)(128)(4,1)} %bitcast.158), calls=%async_computation | async-start | bytes 8388608
  958.0 10.7 copy-start
  958.0 10.7 copy-start.11
  958.0 17.0 %slice-start.1 = ((s8[10485760]{0:T(1024)(128)(4,1)}), s8[4194304]{0:T(1024)(128)(4,1)S(1)}, s32[]{:S(2)}) async-start(s8[10485760]{0:T(1024)(128)(4,1)} %bitcast.158), calls=%async_computation.1 | async-start | bytes 8388608
  958.0 17.0 %slice-start.2 = ((s8[10485760]{0:T(1024)(128)(4,1)}), s8[2097152]{0:T(1024)(128)(4,1)S(1)}, s32[]{:S(2)}) async-start(s8[10485760]{0:T(1024)(128)(4,1)} %bitcast.158), calls=%async_computation.2 | async-start | bytes 4194304
  980.3 195.8 %copy-start.2 = (bf16[4,1,768,512]{3,2,1,0:T(8,128)(2,1)S(1)}, bf16[4,1,768,512]{3,2,1,0:T(8,128)(2,1)}, u32[]{:S(2)}) copy-start(bf16[4,1,768,512]{3,2,1,0:T(8,128)(2,1)} %get-tuple-element.91) | copy-start | bytes 9437188
  1179.7 9.5 copy-start.6
  1179.7 10.5 copy-start.3
  1189.2 2.3 copy-start.4
  1189.2 3.4 copy-start.5

commit v4 on v3

--- a/solution.py
+++ b/solution.py
@@ -16,6 +16,7 @@
 THETA = 1000000.0
 MASKED = -1e30
 AHEAD = 1
+CHUNKS = 16
 BF = jnp.bfloat16
 F32 = jnp.float32
 MESH = pl.DeviceIdType.MESH
@@ -399,61 +400,6 @@
     )(tokens, cotangent, table, w_qkv, w_out, small)
 
 
-class Widen:
-    def __init__(self, pairs, sems, buffers):
-        self.jobs = []
-        for i, (source, result) in enumerate(pairs):
-            narrow, wide = buffers[2 * i], buffers[2 * i + 1]
-            for j in range(source.shape[0]):
-                self.jobs.append(
-                    (
-                        pltpu.make_async_copy(source.at[j], narrow.at[j % 2], sems.at[i, 0, j % 2]),
-                        pltpu.make_async_copy(wide.at[j % 2], result.at[j], sems.at[i, 1, j % 2]),
-                        narrow.at[j % 2],
-                        wide.at[j % 2],
-                        j,
-                        source.shape[0],
-                    )
-                )
-        self.done = 0
-
-    def start(self):
-        for inward, _, _, _, j, _ in self.jobs:
-            if j < 2:
-                inward.start()
-
-    def turn(self):
-        if self.done == len(self.jobs):
-            return
-        at = self.done
-        inward, outward, narrow, wide, j, number = self.jobs[at]
-        inward.wait()
-        if j >= 2:
-            self.jobs[at - 2][1].wait()
-        wide[...] = narrow[...].astype(F32)
-        outward.start()
-        if j + 2 < number:
-            self.jobs[at + 2][0].start()
-        self.done += 1
-
-    def wait(self):
-        while self.done < len(self.jobs):
-            self.turn()
-        for _, outward, _, _, j, number in self.jobs:
-            if j >= number - 2:
-                outward.wait()
-
-
-def widen_scratch(arrays):
-    if not arrays:
-        return []
-    scratch = [DMA((len(arrays), 2, 2))]
-    for array in arrays:
-        shape = (2,) + array.shape[1:]
-        scratch += [pltpu.VMEM(shape, BF), pltpu.VMEM(shape, F32)]
-    return scratch
-
-
 def grads_kernel(sizes, specs, combined, *refs):
     S = sizes["seq"]
     count = len(specs)
@@ -746,7 +692,7 @@
     )(x, row_gate, through, g, up_w, down_w)
 
 
-def line_kernel(sizes, chunks, mode, parts, extra, widened, *refs):
+def line_kernel(sizes, chunks, mode, extra, *refs):
     S, F = sizes["seq"], sizes["fsdp"]
     count = len(extra)
     names = {
@@ -763,14 +709,12 @@
         taken, refs[:number] = refs[:number], []
         return taken
 
-    part_refs = take(parts)
+    (part,) = take(1)
     given = dict(zip(names[0], take(len(names[0]))))
     sources = take(count)
-    narrow = take(widened)
     given.update(zip(names[1], take(len(names[1]))))
     results = take(count)
-    wide = take(widened)
-    from_left, from_right = take(2)
+    landings = take(2)
     gather = mode != "last"
     if gather:
         stage, rs_send, rs_recv, ag_send, ag_recv, own_sem = take(6)
@@ -784,24 +728,25 @@
     f = lax.axis_index("fsdp")
     me = s * F + f
     N = S * F
-    rows = part_refs[0].shape[1]
+    steps = chunks * part.shape[0]
+    rows = part.shape[2]
     span = rows // chunks
     met = greet(sizes)
-    widen = Widen(list(zip(narrow, wide)), refs[0], refs[1:]) if widened else None
-    del refs[: (1 + 2 * widened) if widened else 0]
     blocks = Blocks(sizes, extra, sources, results, refs)
-    if widen:
-        widen.start()
     met()
+    if mode == "grad":
+        given["gain_out"][...] = jnp.zeros_like(given["gain_out"])
+    if mode == "last":
+        gain_sum[...] = jnp.zeros_like(gain_sum)
 
     def at(c):
-        return pl.ds((c % chunks) * span, span)
+        return pl.ds(pl.multiple_of((c % chunks) * span, span), span)
 
     def mine(d, c):
-        return part_refs[c // chunks].at[d, at(c)]
+        return part.at[c // chunks, d, at(c)]
 
     def landed(way, d, c):
-        return (from_left, from_right)[way].at[c // chunks, d, at(c)]
+        return landings[way].at[c // chunks, d, at(c)]
 
     def rs_copy(d, c, way, src):
         return pltpu.make_async_remote_copy(
@@ -819,28 +764,25 @@
         )
 
     def end_step(c):
-        for d in range(S - 1, 0, -1):
-            @pl.when((s == 0) & (d > s))
+        @pl.when(s == 0)
+        def _():
+            for d in range(S - 1, 0, -1):
+                rs_copy(d, c, 0, mine(d, c)).start()
+
+        @pl.when(s == S - 1)
+        def _():
+            for d in range(S - 1):
+                rs_copy(d, c, 1, mine(d, c)).start()
+
+    def middle_step(way, c):
+        for d in range(S - 1, 0, -1) if way == 0 else range(S - 1):
+            @pl.when(d > s if way == 0 else d < s)
             def _():
-                rs_copy(d, c, 0, mine(d, c)).start()
-        for d in range(S - 1):
-            @pl.when((s == S - 1) & (d < s))
-            def _():
-                rs_copy(d, c, 1, mine(d, c)).start()
-
-    def middle_step(c):
-        for way in range(2):
-            order = range(S - 1, 0, -1) if way == 0 else range(S - 1)
-            for d in order:
-                inside = (s > 0) & (d > s) if way == 0 else (s < S - 1) & (d < s)
-
-                @pl.when(inside)
-                def _():
-                    buffer = landed(way, d, c)
-                    rs_copy(d, c, way, buffer).wait_recv()
-                    total = buffer[...].astype(F32) + mine(d, c)[...].astype(F32)
-                    buffer[...] = total.astype(BF)
-                    rs_copy(d, c, way, buffer).start()
+                buffer = landed(way, d, c)
+                rs_copy(d, c, way, buffer).wait_recv()
+                total = buffer[...].astype(F32) + mine(d, c)[...].astype(F32)
+                buffer[...] = total.astype(BF)
+                rs_copy(d, c, way, buffer).start()
 
     def final_step(c):
         @pl.when(s > 0)
@@ -855,21 +797,27 @@
         total = total + jnp.where(s > 0, landed(0, s, c)[...].astype(F32), 0.0)
         total = total + jnp.where(s < S - 1, landed(1, s, c)[...].astype(F32), 0.0)
         if mode == "last":
-            if c >= chunks:
-                row = s * rows + (c % chunks) * span + lax.broadcasted_iota(jnp.int32, total.shape, 0)
+            @pl.when(c >= chunks)
+            def _():
+                row = s * rows + (c % chunks) * span
+                row = row + lax.broadcasted_iota(jnp.int32, total.shape, 0)
                 value = given["resid"][at(c), :] + total
                 given["low_out"][at(c), :] = jnp.where(row < given["length"][0], value, 0.0).astype(BF)
-                return
-            value = given["inputs"][at(c), :].astype(F32)
-            factor = lax.rsqrt(jnp.mean(value * value, axis=-1, keepdims=True) + EPSILON)
-            normed = value * factor
-            scaled = total * given["gain"][...]
-            inner = jnp.mean(scaled * normed, axis=-1, keepdims=True)
-            given["grad_out"][at(c), :] = given["base"][at(c), :] + factor * (scaled - normed * inner)
-            gained = jnp.sum(total * normed, axis=0, keepdims=True)
-            gain_sum[...] = gained if c == 0 else gain_sum[...] + gained
-            if c == chunks - 1:
+
+            @pl.when(c < chunks)
+            def _():
+                value = given["inputs"][at(c), :].astype(F32)
+                factor = lax.rsqrt(jnp.mean(value * value, axis=-1, keepdims=True) + EPSILON)
+                normed = value * factor
+                scaled = total * given["gain"][...]
+                inner = jnp.mean(scaled * normed, axis=-1, keepdims=True)
+                given["grad_out"][at(c), :] = given["base"][at(c), :] + factor * (scaled - normed * inner)
+                gain_sum[...] += jnp.sum(total * normed, axis=0, keepdims=True)
+
+            @pl.when(c == chunks - 1)
+            def _():
                 send_gains()
+
             return
         if mode == "ffn":
             value = given["base"][at(c), :].astype(F32) + total
@@ -885,9 +833,7 @@
             inner = jnp.mean(scaled * normed, axis=-1, keepdims=True)
             result = given["base"][at(c), :] + factor * (scaled - normed * inner)
             given["grad_out"][at(c), :] = result
-            gained = jnp.sum(upstream * normed, axis=0, keepdims=True)
-            gain_out = given["gain_out"]
-            gain_out[...] = gained if c == 0 else gain_out[...] + gained
+            given["gain_out"][...] += jnp.sum(upstream * normed, axis=0, keepdims=True)
             low = result.astype(BF)
         stage[at(c), :] = low
         pltpu.make_async_copy(stage.at[at(c)], all_out.at[s, at(c)], own_sem.at[c]).start()
@@ -932,7 +878,7 @@
         )
 
     def plane_step():
-        plane.wait()
+        plane.wait_one(1)
         for z in range(S):
             total = plane_gqkv[0, z].astype(F32)
             for owner in range(1, F):
@@ -941,6 +887,9 @@
         for step in range(1, S):
             line_copy(step).start()
         gqkv_line[s] = gqkv_stage[s]
+
+    def rows_step():
+        plane.wait_one(0)
         half = plane_gout.shape[1] // 2
         for part_at in range(2):
             own = pl.ds(part_at * half, half)
@@ -962,48 +911,66 @@
             value_at = S * (q_width + kv) + z * kv
             result[:, value_at : value_at + kv] = block[:, q_width + kv :]
 
-    def relay_step(c, hop):
-        @pl.when(s >= hop)
-        def _():
-            ag_copy(s - hop, c, 0, hop).wait_recv()
-            if hop < S - 1:
-                @pl.when(s < S - 1)
-                def _():
-                    ag_copy(s - hop, c, 0, hop + 1).start()
-
-        @pl.when(s < S - hop)
-        def _():
-            ag_copy(s + hop, c, 1, hop).wait_recv()
-            if hop < S - 1:
-                @pl.when(s > 0)
-                def _():
-                    ag_copy(s + hop, c, 1, hop + 1).start()
-
-    steps = chunks * parts
-    ahead = min(steps, AHEAD if gather else steps)
+    def relay_step(way, hop, c):
+        block = s - hop if way == 0 else s + hop
+        ag_copy(block, c, way, hop).wait_recv()
+        if hop < S - 1:
+            @pl.when(s < S - 1 if way == 0 else s > 0)
+            def _():
+                ag_copy(block, c, way, hop + 1).start()
+
+    def final_lag(z):
+        return 1 + jnp.maximum(jnp.maximum(z - 2, S - 3 - z), 0)
+
+    ahead = min(steps, AHEAD if gather else 4)
     for c in range(ahead):
         end_step(c)
-    blocks.start()
     if plane:
         plane.start()
-    hops = S - 1 if gather else 0
-    plane_at = steps - 3
-    for t in range(steps + 1 + hops):
-        if t < steps:
-            middle_step(t)
-        if t + ahead < steps:
+    blocks.start()
+    turns = steps + (2 * S - 2 if gather else S)
+
+    def inside(c):
+        return (c >= 0) & (c < steps)
+
+    @pl.loop(0, turns)
+    def _(t):
+        for way in range(2):
+            come = t - (s - 1 if way == 0 else S - 2 - s)
+
+            @pl.when(inside(come) & ((s > 0) & (s < S - 1)))
+            def _():
+                middle_step(way, come)
+
+        @pl.when(inside(t + ahead) & ((s == 0) | (s == S - 1)))
+        def _():
             end_step(t + ahead)
-        if 0 <= t - 1 < steps:
-            final_step(t - 1)
-        for hop in range(1, hops + 1):
-            if 0 <= t - 1 - hop < steps:
-                relay_step(t - 1 - hop, hop)
-        if widen:
-            widen.turn()
-        if plane and t == plane_at:
-            plane_step()
-
-    for c in range(steps):
+
+        done = t - final_lag(s)
+
+        @pl.when(inside(done))
+        def _():
+            final_step(done)
+
+        if gather:
+            for hop in range(1, S):
+                for way in range(2):
+                    block = s - hop if way == 0 else s + hop
+                    passed = t - final_lag(block) - hop
+
+                    @pl.when(inside(passed) & ((block >= 0) & (block < S)))
+                    def _():
+                        relay_step(way, hop, passed)
+        else:
+            @pl.when(t == steps * 13 // 16)
+            def _():
+                plane_step()
+
+    if plane:
+        rows_step()
+
+    @pl.loop(0, steps)
+    def _(c):
         for d in range(S - 1, 0, -1):
             @pl.when(d > s)
             def _():
@@ -1022,24 +989,23 @@
                 @pl.when((s > 0) & (s <= S - hop))
                 def _():
                     ag_copy(s, c, 1, hop).wait_send()
+
     if mode == "last":
         columns_step()
         own_gains().wait()
         for step in range(1, N):
             gain_copy(step).wait()
-    if widen:
-        widen.wait()
     blocks.wait()
 
 
-def line(mode, sizes, parts, others, extras, specs, collective_id, chunks=8, widened=()):
-    S = sizes["seq"]
-    _, rows, width = parts[0].shape
+def line(mode, sizes, part, others, extras, specs, collective_id, chunks=CHUNKS):
+    S, F = sizes["seq"], sizes["fsdp"]
+    parts, _, rows, width = part.shape
     full = jax.ShapeDtypeStruct((rows, width), F32)
     everyone = jax.ShapeDtypeStruct((S, rows, width), BF)
-    steps = chunks * len(parts)
-    scratch = [pltpu.VMEM((len(parts), S, rows, width), BF)] * 2
-    in_specs = [VM] * (len(parts) + len(others))
+    steps = chunks * parts
+    scratch = [pltpu.VMEM((parts, S, rows, width), BF)] * 2
+    in_specs = [VM] * (1 + len(others))
     sems = [DMA((2, S, steps)), DMA((2, S, steps))]
     if mode == "ffn":
         outs, out_specs = [full, everyone], [VM, ANY]
@@ -1051,17 +1017,17 @@
         outs = [
             full,
             jax.ShapeDtypeStruct((rows, width), BF),
-            jax.ShapeDtypeStruct((S * sizes["fsdp"], width // 128, 128), F32),
+            jax.ShapeDtypeStruct((S * F, width // 128, 128), F32),
             jax.ShapeDtypeStruct(gout.shape[1:], F32),
             jax.ShapeDtypeStruct((owned[0], owned[1] * S), F32),
         ]
         out_specs = [VM, VM, ANY, VM, VM]
-        N = S * sizes["fsdp"]
+        N = S * F
         scratch += [pltpu.VMEM((1, width), F32), pltpu.VMEM((width // 128, 128), F32)]
         scratch += [DMA((N,)), DMA((N,)), DMA((1,))]
         scratch += [
             pltpu.VMEM(gout.shape, BF),
-            pltpu.VMEM((sizes["fsdp"], S) + owned, BF),
+            pltpu.VMEM((F, S) + owned, BF),
             pltpu.VMEM((S,) + owned, BF),
             pltpu.VMEM((S,) + owned, BF),
             DMA((S,)),
@@ -1074,18 +1040,16 @@
         scratch.append(pltpu.VMEM((rows, width), BF))
         sems += [DMA((2, chunks, S)), DMA((2, chunks, S)), DMA((chunks,))]
     return pl.pallas_call(
-        functools.partial(line_kernel, sizes, chunks, mode, len(parts), specs, len(widened)),
-        out_shape=outs
-        + block_outs(sizes, extras, specs)
-        + [jax.ShapeDtypeStruct(array.shape, F32) for array in widened],
-        in_specs=in_specs + [ANY] * (len(extras) + len(widened)),
-        out_specs=out_specs + [ANY] * (len(extras) + len(widened)),
-        scratch_shapes=scratch + sems + widen_scratch(widened) + block_scratch(sizes, extras, specs),
+        functools.partial(line_kernel, sizes, chunks, mode, specs),
+        out_shape=outs + block_outs(sizes, extras, specs),
+        in_specs=in_specs + [ANY] * len(extras),
+        out_specs=out_specs + [ANY] * len(extras),
+        scratch_shapes=scratch + sems + block_scratch(sizes, extras, specs),
         compiler_params=pltpu.CompilerParams(
-            collective_id=collective_id, has_side_effects=True, vmem_limit_bytes=56 << 20
+            collective_id=collective_id, has_side_effects=True, vmem_limit_bytes=58 << 20
         ),
         name=f"line_{mode}",
-    )(*parts, *others, *extras, *widened)
+    )(part, *others, *extras)
 
 
 def turn(values, cosine, sine):
@@ -1113,10 +1077,11 @@
 def attend_kernel(sizes, heads, blocks, specs, *refs):
     count = len(specs)
     length_ref, tok_ref, gain_ref, wq_ref, cos_ref, sin_ref, gains_ref, wo_ref = refs[:8]
-    sources = refs[8 : 8 + count]
-    attn_ref, proj_ref, low_ref, out_ref, part_ref = refs[8 + count : 13 + count]
-    results = refs[13 + count : 13 + 2 * count]
-    k_all, v_all, *sems = refs[13 + 2 * count :]
+    select_ref, cot_ref = refs[8:10]
+    sources = refs[10 : 10 + count]
+    attn_ref, proj_ref, low_ref, out_ref, part_ref, rows_ref = refs[10 + count : 16 + count]
+    results = refs[16 + count : 16 + 2 * count]
+    k_all, v_all, *sems = refs[16 + 2 * count :]
     step = pl.program_id(0)
 
     @pl.when(step == 0)
@@ -1172,22 +1137,33 @@
 
     tiles(part_ref.shape[1], 256, leave)
 
+    def pick(at):
+        rows_ref[0, :, at] = jnp.dot(
+            select_ref[0], cot_ref[0, :, at], preferred_element_type=F32
+        ).astype(BF)
+
+    tiles(rows_ref.shape[2], 512, pick)
+
     @pl.when(step == blocks - 1)
     def _():
         Blocks(sizes, specs, sources, results, sems).wait()
 
 
 def attend(
-    length, tokens, gain, w_proj, cosine, sine, gains, w_out, heads, extras, specs, sizes,
-    collective_id, blocks=4,
+    length, tokens, gain, w_proj, cosine, sine, gains, w_out, select, cot, heads, extras, specs,
+    sizes, collective_id,
 ):
     total, width = tokens.shape
+    blocks = select.shape[0]
     own_width = w_proj.shape[1]
     rows = total // blocks
     q_width = heads * HD
 
     def by_rows(columns):
         return pl.BlockSpec((rows, columns), lambda i: (i, 0))
+
+    def by_block(array):
+        return pl.BlockSpec((1,) + array.shape[1:], lambda i: (i, 0, 0))
 
     def whole(array):
         return pl.BlockSpec(array.shape, lambda i: (0, 0), pipeline_mode=pl.Buffered(1))
@@ -1201,6 +1177,7 @@
             jax.ShapeDtypeStruct((total, own_width), BF),
             jax.ShapeDtypeStruct((total, q_width), BF),
             jax.ShapeDtypeStruct((total, width), BF),
+            jax.ShapeDtypeStruct(select.shape[:2] + (width,), BF),
         ] + block_outs(sizes, extras, specs),
         in_specs=[
             pl.BlockSpec(memory_space=pltpu.SMEM),
@@ -1211,25 +1188,36 @@
             by_rows(HD),
             whole(gains),
             whole(w_out),
+            by_block(select),
+            by_block(cot),
         ] + [ANY] * len(extras),
-        out_specs=[by_rows(width), by_rows(own_width), by_rows(own_width), by_rows(q_width), by_rows(width)]
-        + [ANY] * len(extras),
+        out_specs=[
+            by_rows(width), by_rows(own_width), by_rows(own_width), by_rows(q_width), by_rows(width),
+            pl.BlockSpec((1, select.shape[1], width), lambda i: (i, 0, 0)),
+        ] + [ANY] * len(extras),
         scratch_shapes=[pltpu.VMEM((total, HD), BF), pltpu.VMEM((total, HD), BF)]
         + block_scratch(sizes, extras, specs),
         compiler_params=pltpu.CompilerParams(
             collective_id=collective_id, has_side_effects=True, vmem_limit_bytes=58 << 20
         ),
         name="attend",
-    )(length, tokens, gain, w_proj, cosine, sine, gains, w_out, *extras)
+    )(length, tokens, gain, w_proj, cosine, sine, gains, w_out, select, cot, *extras)
 
 
 def attend_back_kernel(sizes, heads, blocks, specs, *refs):
     count = len(specs)
     length_ref, proj_ref, low_ref, kv_ref, grad_ref, wo_ref, wq_ref, cos_ref, sin_ref, gains_ref = refs[:10]
-    sources = refs[10 : 10 + count]
-    out_ref, part_ref, gains_out = refs[10 + count : 13 + count]
-    results = refs[13 + count : 13 + 2 * count]
-    gk_all, gv_all, go_ref, *sems = refs[13 + 2 * count :]
+    select_ref, back_ref, attn_any, o_any, ga_any = refs[10:15]
+    sources = refs[15 : 15 + count]
+    part_ref, gains_out, gqkv_out, gout_out = refs[15 + count : 19 + count]
+    results = refs[19 + count : 19 + 2 * count]
+    gk_all, gv_all, go_ref, out_all, attn_all, o_all, ga_all, gqkv_stage, gout_stage, all_sem, out_sem, *sems = refs[
+        19 + 2 * count :
+    ]
+    inward = [
+        pltpu.make_async_copy(source, target, all_sem.at[i])
+        for i, (source, target) in enumerate(((attn_any, attn_all), (o_any, o_all), (ga_any, ga_all)))
+    ]
     step = pl.program_id(0)
     rows = proj_ref.shape[0]
     length = length_ref[0]
@@ -1239,6 +1227,7 @@
     k_gain = gains_ref[1:2, :]
     scale = HD ** (-0.5)
     block_at = blocks - 1 - step
+    here = pl.ds(pl.multiple_of(block_at * rows, rows), rows)
 
     def back(raw, gain, grad):
         grad = turn(grad, cosine, -sine)
@@ -1252,6 +1241,8 @@
     def _():
         greet(sizes)()
         Blocks(sizes, specs, sources, results, sems).start()
+        for copy in inward:
+            copy.start()
         gk_all[...] = jnp.zeros_like(gk_all)
         gv_all[...] = jnp.zeros_like(gv_all)
         gains_out[...] = jnp.zeros_like(gains_out)
@@ -1286,41 +1277,75 @@
                     probs.astype(BF), grad_o, (((0,), (0,)), ((), ())), preferred_element_type=F32
                 )
                 grad_raw, gained = back(proj_ref[:, column], q_gain, grad_q.astype(BF).astype(F32))
-                out_ref[:, column] = grad_raw.astype(BF)
+                out_all[here, column] = grad_raw.astype(BF)
                 gains_out[0:1, :] += gained
 
             tiles(heads * HD, HD, one)
 
-    here = pl.ds(pl.multiple_of(block_at * rows, rows), rows)
     grad_k = (gk_all[here, :] * scale).astype(BF).astype(F32)
     grad_raw, gained = back(proj_ref[:, heads * HD : (heads + 1) * HD], k_gain, grad_k)
-    out_ref[:, heads * HD : (heads + 1) * HD] = grad_raw.astype(BF)
-    out_ref[:, (heads + 1) * HD :] = gv_all[here, :].astype(BF)
+    out_all[here, heads * HD : (heads + 1) * HD] = grad_raw.astype(BF)
+    out_all[here, (heads + 1) * HD :] = gv_all[here, :].astype(BF)
     gains_out[1:2, :] += gained
 
     def leave(at):
-        part_ref[:, at] = lax.dot_general(
-            out_ref[...], wq_ref[at, :], (((1,), (1,)), ((), ())), preferred_element_type=F32
+        part_ref[0, :, at] = lax.dot_general(
+            out_all[here, :], wq_ref[at, :], (((1,), (1,)), ((), ())), preferred_element_type=F32
         ).astype(BF)
 
-    tiles(part_ref.shape[1], 256, leave)
+    tiles(part_ref.shape[2], 256, leave)
+    over_rows = (((0,), (0,)), ((), ()))
+
+    def combine(at):
+        part_ref[1, :, at] = lax.dot_general(
+            select_ref[0], back_ref[0, :, at], over_rows, preferred_element_type=F32
+        ).astype(BF)
+
+    tiles(part_ref.shape[2], 512, combine)
 
     @pl.when(step == blocks - 1)
     def _():
+        for copy in inward:
+            copy.wait()
+        for i, (left, right, stage, result) in enumerate(
+            ((attn_all, out_all, gqkv_stage, gqkv_out), (o_all, ga_all, gout_stage, gout_out))
+        ):
+            span = stage.shape[1]
+            sent = []
+            for n in range(left.shape[1] // span):
+                if n >= 2:
+                    sent[n - 2].wait()
+                stage[n % 2] = lax.dot_general(
+                    left[:, n * span : (n + 1) * span], right[...], over_rows,
+                    preferred_element_type=F32,
+                ).astype(BF)
+                sent.append(
+                    pltpu.make_async_copy(
+                        stage.at[n % 2], result.at[pl.ds(n * span, span)], out_sem.at[i, n % 2]
+                    )
+                )
+                sent[-1].start()
+            for copy in sent[-2:]:
+                copy.wait()
         Blocks(sizes, specs, sources, results, sems).wait()
 
 
 def attend_back(
-    length, projected, low, grad, w_out, w_proj, cosine, sine, gains, heads, extras, specs, sizes,
-    collective_id, blocks=4,
+    length, projected, low, grad, w_out, w_proj, cosine, sine, gains, select, back, attn_low, o_low,
+    heads, extras, specs, sizes, collective_id,
 ):
     total, own_width = projected.shape
     width = w_out.shape[1]
+    blocks = select.shape[0]
+    span = 256
     rows = total // blocks
     q_width = heads * HD
 
     def by_rows(columns):
         return pl.BlockSpec((rows, columns), lambda i: (blocks - 1 - i, 0))
+
+    def by_block(array):
+        return pl.BlockSpec((1,) + array.shape[1:], lambda i: (blocks - 1 - i, 0, 0))
 
     def whole(array):
         return pl.BlockSpec(array.shape, lambda i: (0, 0), pipeline_mode=pl.Buffered(1))
@@ -1329,9 +1354,10 @@
         functools.partial(attend_back_kernel, sizes, heads, blocks, specs),
         grid=(blocks,),
         out_shape=[
-            jax.ShapeDtypeStruct((total, own_width), BF),
-            jax.ShapeDtypeStruct((total, width), BF),
+            jax.ShapeDtypeStruct((2, total, width), BF),
             jax.ShapeDtypeStruct((2, HD), F32),
+            jax.ShapeDtypeStruct((width, own_width), BF),
+            jax.ShapeDtypeStruct((q_width, width), BF),
         ] + block_outs(sizes, extras, specs),
         in_specs=[
             pl.BlockSpec(memory_space=pltpu.SMEM),
@@ -1344,19 +1370,34 @@
             by_rows(HD),
             by_rows(HD),
             whole(gains),
-        ] + [ANY] * len(extras),
-        out_specs=[by_rows(own_width), by_rows(width), pl.BlockSpec((2, HD), lambda i: (0, 0))]
-        + [ANY] * len(extras),
+            by_block(select),
+            by_block(back),
+        ] + [ANY] * (3 + len(extras)),
+        out_specs=[
+            pl.BlockSpec((2, rows, width), lambda i: (0, blocks - 1 - i, 0)),
+            pl.BlockSpec((2, HD), lambda i: (0, 0)),
+        ] + [ANY] * (2 + len(extras)),
         scratch_shapes=[
             pltpu.VMEM((total, HD), F32),
             pltpu.VMEM((total, HD), F32),
             pltpu.VMEM((rows, q_width), BF),
+            pltpu.VMEM((total, own_width), BF),
+            pltpu.VMEM((total, width), BF),
+            pltpu.VMEM((total, q_width), BF),
+            pltpu.VMEM((total, width), BF),
+            pltpu.VMEM((2, span, own_width), BF),
+            pltpu.VMEM((2, span, width), BF),
+            DMA((3,)),
+            DMA((2, 2)),
         ] + block_scratch(sizes, extras, specs),
         compiler_params=pltpu.CompilerParams(
             collective_id=collective_id, has_side_effects=True, vmem_limit_bytes=58 << 20
         ),
         name="attend_back",
-    )(length, projected, low, low, grad, w_out, w_proj, cosine, sine, gains, *extras)
+    )(
+        length, projected, low, low, grad, w_out, w_proj, cosine, sine, gains, select, back,
+        attn_low, o_low, grad, *extras,
+    )
 
 
 def rms_factor(values):
@@ -1436,13 +1477,6 @@
     angles = positions.astype(F32)[:, None] * frequency[None, :]
     cosine = jnp.concatenate([jnp.cos(angles)] * 2, axis=-1)
     sine = jnp.concatenate([-jnp.sin(angles), jnp.sin(angles)], axis=-1)
-    attn_low, projected, qkv_low, o_low, o_part, down_w = attend(
-        lengths, tok_all.reshape(seq_total, width), gain_attn[None], w_proj, cosine, sine,
-        gain_heads, out_own, heads, [w_down.reshape((S, own_experts) + w_down.shape[1:])],
-        ((("seq",), 0, "columns"),), sizes, 3,
-    )
-    o_part = o_part.reshape(S, tok_count, width)
-
     expert_ids = jnp.arange(expert_count, dtype=jnp.int32)
     slot_ids = jnp.arange(capacity, dtype=jnp.int32)
     plane = (
@@ -1456,9 +1490,16 @@
     select = one_hot.astype(BF).reshape(S, F * own_experts * capacity, tok_count)
     grouped = (S, F, own_experts * capacity, width)
 
-    cot_rows = mm("brt,btd->brd", select, cot_all).astype(BF).reshape(grouped)
+    attn_low, projected, qkv_low, o_low, o_part, cot_rows, down_w = attend(
+        lengths, tok_all.reshape(seq_total, width), gain_attn[None], w_proj, cosine, sine,
+        gain_heads, out_own, select, cot_all, heads, [w_down.reshape((S, own_experts) + w_down.shape[1:])],
+        ((("seq",), 0, "columns"),), sizes, 3,
+    )
+    o_part = o_part.reshape(1, S, tok_count, width)
+    cot_rows = cot_rows.reshape(grouped)
+
     residual, ffn_all, g_rows = line(
-        "ffn", sizes, [o_part], [tokens[0], gain_ffn], [cot_rows], ((("fsdp",), 1, 0),), 2
+        "ffn", sizes, o_part, [tokens[0], gain_ffn], [cot_rows], ((("fsdp",), 1, 0),), 2
     )
     ffn_low = lax.dynamic_index_in_dim(ffn_all, seq_at, 0, keepdims=False)
 
@@ -1530,19 +1571,17 @@
     valid = (seq_at * tok_count + jnp.arange(tok_count, dtype=jnp.int32)) < lengths[0]
     grad_final = jnp.where(valid[:, None], cotangent[0].astype(F32), 0.0)
     grad_residual, grad_gain_ffn, grad_attn_low, moe_back = line(
-        "grad", sizes, [grad_part], [grad_final, gain_ffn, residual, grad_ffn_add],
+        "grad", sizes, grad_part[None], [grad_final, gain_ffn, residual, grad_ffn_add],
         [moe_rows.reshape(F, S, capacity, width)], ((("fsdp",), 0, 1),), 7,
     )
     grad_attn_low = grad_attn_low.reshape(seq_total, width)
 
-    grad_proj, attn_part, grad_gain_heads, down_got = attend_back(
+    last_parts, grad_gain_heads, grad_qkv_part, grad_out_part, down_got = attend_back(
         lengths, projected, qkv_low, grad_attn_low, out_own, w_proj, cosine, sine, gain_heads,
-        heads, [down_term[None]], ((("seq",), "columns", 0),), sizes, 9,
-    )
-    attn_part = attn_part.reshape(S, tok_count, width)
-    grad_out_part = mm("te,td->ed", o_low, grad_attn_low).astype(BF)
-    grad_qkv_part = mm("td,te->de", attn_low, grad_proj).astype(BF).reshape(S, F, w_rows, own_width)
-    moe_part = mm("brt,brd->btd", select, moe_back.reshape(S, -1, width)).astype(BF)
+        select, moe_back.reshape(S, -1, width), attn_low, o_low, heads, [down_term[None]],
+        ((("seq",), "columns", 0),), sizes, 9,
+    )
+    grad_qkv_part = grad_qkv_part.reshape(S, F, w_rows, own_width)
     early_gains = jnp.concatenate(
         [jnp.zeros((width,), F32), grad_gain_ffn[0], grad_gain_heads.reshape(-1)]
     )
@@ -1555,7 +1594,7 @@
     (
         grad_inputs, final, late_gains, grad_out, grad_qkv, small_got
     ) = line(
-        "last", sizes, [attn_part, moe_part],
+        "last", sizes, last_parts.reshape(2, S, tok_count, width),
         [
             grad_residual, gain_attn[None], residual, tokens[0], lengths,
             grad_out_part.reshape(F, -1, width), grad_qkv_part,

time: 1200 us -> 1180 us (0.983)
  matrix products: 35.7 us -> 5.66 us
    dot_general x6 -> x2, matrix products: 33.6 us -> 3.51 us  [mm(): return jnp.einsum(form, left, right, preferred_element_type=F32)]
    pallas_call x1, Pallas kernels: 63.7 us -> 87.4 us  [attend_back(): pl.pallas_call(functools.partial(attend_back_kernel, sizes, heads, blocks...]
    pallas_call x3, Pallas kernels: 486 us -> 467 us  [line(): pl.pallas_call(functools.partial(line_kernel, sizes, chunks, mode, specs)...]
where the time goes in v4:
time: 1180 us; the launch traced here: 1170 us
  Pallas kernels  1120 us (95%)
  other arithmetic  27.9 us (2%)
  local copies, waits for them, and re-layouts  16.6 us (1%)
    pallas_call x3, Pallas kernels, line(): pl.pallas_call(functools.partial(line_kernel, sizes, chunks, mode, specs)...  467 us
    pallas_call x1, Pallas kernels, entry(): pl.pallas_call(functools.partial(entry_kernel, sizes), out_shape=[line_ou...  163 us
    pallas_call x1, Pallas kernels, dispatch(): pl.pallas_call(functools.partial(dispatch_kernel, sizes, specs), out_shap...  150 us
    pallas_call x1, Pallas kernels, grads(): pl.pallas_call(functools.partial(grads_kernel, sizes, specs, combined), o...  137 us
    pallas_call x1, Pallas kernels, attend_back(): pl.pallas_call(functools.partial(attend_back_kernel, sizes, heads, blocks...  87.4 us
    pallas_call x1, Pallas kernels, attend(): pl.pallas_call(functools.partial(attend_kernel, sizes, heads, blocks, spe...  65 us
    pallas_call x1, Pallas kernels, expert(): pl.pallas_call(expert_kernel, grid=(steps,), out_shape=[jax.ShapeDtypeStr...  53.1 us

profile of v4, /device:TPU:0, one launch (start us, length us, event | category | flops | bytes accessed | tf_op | source)
XLA Modules:
  0.0 1173.4 jit_solution(6310440041421539577)
XLA Ops:
  0.6 1.3 pad_add_fusion.table_ref
  4.2 162.5 %entry.1 = (bf16[4,256,2048]{2,1,0:T(8,128)(2,1)}, bf16[4,256,2048]{2,1,0:T(8,128)(2,1)}, s32[4,16,256]{2,1,0:T(8,128)}, bf16[4,8,64,1280]{3,2,1,0:T(8,128)(2,1)...) custom-call(bf16[256,2048]{1,0:T(8,128)(2,1)} %bitcast.106, bf16[256,2048]{1,0:T(8,128)(2,1)} %bitcast.116, ...), custom_call_target="tpu_custom_call" | custom-call | tf_op jit(solution)/shard_map/entry/pallas_call | solution.py:381
  167.7 1.3 fusion.refs_8_.refs_5_.refs_6_.refs_10_
  171.5 1.9 fusion.9
  173.5 1.3 pad_maximum_fusion
  175.4 65.0 %attend.1 = (bf16[1024,2048]{1,0:T(8,128)(2,1)}, f32[1024,1280]{1,0:T(8,128)}, bf16[1024,1280]{1,0:T(8,128)(2,1)}, bf16[1024,1024]{1,0:T(8,128)(2,1)}, bf16[1024...) custom-call(s32[1]{0:T(128)} %copy.70.refs_0_.refs_5_, ...), custom_call_target="tpu_custom_call" | custom-call | tf_op jit(solution)/shard_map/attend/pallas_call | solution.py:1171
  240.5 139.8 %line_ffn.1 = (f32[256,2048]{1,0:T(8,128)}, bf16[4,256,2048]{2,1,0:T(8,128)(2,1)}, bf16[8,4,80,2048]{3,2,1,0:T(8,128)(2,1)}) custom-call(bf16[1,4,256,2048]{3,2,1,0:T(8,128)(2,1)} %bitcast.115, bf16[256,2048]{1,0:T(8,128)(2,1)} %bitcast.107, f32[1,2048]{1,0:T(1,128)} %bitcast.135, bf16[4,8,80,2048]{3,2,1,0:T(8,128)(2,1)} %bitcast.103), custom_call_target="tpu_custom_call" | custom-call | tf_op jit(solution)/shard_map/line_ffn/pallas_call | solution.py:1042
  380.7 1.6 fusion.4
  384.1 149.8 %dispatch.1 = (bf16[4,1,512,1536]{3,2,1,0:T(8,128)(2,1)}, f32[32,16,128]{2,1,0:T(8,128)}, bf16[8,4,80,2048]{3,2,1,0:T(8,128)(2,1)}, f32[2560,768]{1,0:T(8,128)}) custom-call(bf16[4,1,512,1536]{3,2,1,0:T(8,128)(2,1)} %bitcast.111, f32[32,16,128]{2,1,0:T(8,128)} %bitcast.123, bf16[4,256,2048]{2,1,0:T(8,128)(2,1)} %get-tuple-element.62.refs_2_, ...), custom_call_target="tpu_custom_call" | custom-call | tf_op jit(solution)/shard_map/dispatch/pallas_call | solution.py:609
  534.9 1.7 reshape.298.gate_ref
  536.5 53.1 %expert.1 = (bf16[2560,2048]{1,0:T(8,128)(2,1)}, bf16[2560,2048]{1,0:T(8,128)(2,1)}, bf16[2560,1536]{1,0:T(8,128)(2,1)}, bf16[2560,768]{1,0:T(8,128)(2,1)}, f32[2560,1]{1,0:T(8,128)}) custom-call(bf16[2560,2048]{1,0:T(8,128)(2,1)} %bitcast.92, f32[2560,1]{1,0:T(8,128)} %reshape.298.gate_ref, f32[2560,768]{1,0:T(8,128)} %get-tuple-element.67.through_ref, ...), custom_call_target="tpu_custom_call" | custom-call | tf_op jit(solution)/shard_map/expert/pallas_call | solution.py:677
  589.7 1.7 reduce.1
  592.3 136.6 %grads.1 = (bf16[4,8,80,2048]{3,2,1,0:T(8,128)(2,1)}, f32[32,16,128]{2,1,0:T(8,128)}, bf16[4,512,1536]{2,1,0:T(8,128)(2,1)}, bf16[768,2048]{1,0:T(8,128)(2,1)}, bf16[4,256,2048]{2,1,0:T(8,128)(2,1)}) custom-call(bf16[8,4,80,2048]{3,2,1,0:T(8,128)(2,1)} %bitcast.104, f32[32,16,128]{2,1,0:T(8,128)} %bitcast.122, bf16[2560,2048]{1,0:T(8,128)(2,1)} %bitcast.93, ...), custom_call_target="tpu_custom_call" | custom-call | tf_op jit(solution)/shard_map/grads/pallas_call | solution.py:509
  728.9 1.1 reshape.280
  730.6 1.7 fusion.2
  732.8 1.8 fusion.22.refs_4_
  734.6 1.5 convert_select_fusion.refs_1_
  736.2 146.4 %line_grad.1 = (f32[256,2048]{1,0:T(8,128)}, f32[1,2048]{1,0:T(1,128)}, bf16[4,256,2048]{2,1,0:T(8,128)(2,1)}, bf16[4,8,80,2048]{3,2,1,0:T(8,128)(2,1)}) custom-call(bf16[1,4,256,2048]{3,2,1,0:T(8,128)(2,1)} %bitcast.114, f32[256,2048]{1,0:T(8,128)} %convert_select_fusion.refs_1_, f32[1,2048]{1,0:T(1,128)} %bitcast.136, ...), custom_call_target="tpu_custom_call" | custom-call | tf_op jit(solution)/shard_map/line_grad/pallas_call | solution.py:1042
  882.6 87.4 %attend_back.1 = (bf16[2,1024,2048]{2,1,0:T(8,128)(2,1)}, f32[2,128]{1,0:T(2,128)}, bf16[2048,1280]{1,0:T(8,128)(2,1)}, bf16[1024,2048]{1,0:T(8,128)(2,1)}, bf16[4,1,768,512]{3,2,1,0:T(8,128)(2,1)}) custom-call(s32[1]{0:T(128)} %copy.70.refs_0_.refs_5_, f32[1024,1280]{1,0:T(8,128)} %get-tuple-element.58.refs_1_, ...), custom_call_target="tpu_custom_call" | custom-call | tf_op jit(solution)/shard_map/attend_back/pallas_call | solution.py:1353
  971.7 180.7 %line_last.1 = (f32[256,2048]{1,0:T(8,128)}, bf16[256,2048]{1,0:T(8,128)(2,1)}, f32[32,16,128]{2,1,0:T(8,128)}, f32[128,2048]{1,0:T(8,128)}, f32[64,5120]{1,0:T(8,128)}, /*index=5*/f32[32,24,128]{2,1,0:T(8,128)}) custom-call(bf16[2,4,256,2048]{3,2,1,0:T(8,128)(2,1)} %bitcast.109, f32[256,2048]{1,0:T(8,128)} %get-tuple-element.83.refs_1_, ...), custom_call_target="tpu_custom_call" | custom-call | tf_op jit(solution)/shard_map/line_last/pallas_call | solution.py:1042
  1155.8 3.6 bitcast_convert_fusion
  1159.4 9.5 convert_element_type.57
  1169.9 1.3 copy.72
  1171.2 1.1 copy.73
  (76 shorter events, 17.7 us)
Async XLA Ops:
  240.4 141.9 %copy-start.6 = (s32[1,256,8]{1,2,0:T(8,128)S(1)}, s32[1,256,8]{1,2,0:T(8,128)}, u32[]{:S(2)}) copy-start(s32[1,256,8]{1,2,0:T(8,128)} %param.14) | copy-start | bytes 24580
  240.5 142.1 %copy-start.7 = (s32[1,256,8]{1,2,0:T(8,128)S(1)}, s32[1,256,8]{1,2,0:T(8,128)}, u32[]{:S(2)}) copy-start(s32[1,256,8]{1,2,0:T(8,128)} %param.15) | copy-start | bytes 24580
  728.9 5.7 copy-start
  882.6 87.5 %copy-start.8 = (f32[1,2048]{1,0:T(1,128)S(1)}, f32[1,2048]{1,0:T(1,128)}, u32[]{:S(2)}) copy-start(f32[1,2048]{1,0:T(1,128)} %get-tuple-element.86) | copy-start | bytes 24580
  971.7 184.1 %copy-start.1 = (bf16[4,1,768,512]{3,2,1,0:T(8,128)(2,1)S(1)}, bf16[4,1,768,512]{3,2,1,0:T(8,128)(2,1)}, u32[]{:S(2)}) copy-start(bf16[4,1,768,512]{3,2,1,0:T(8,128)(2,1)} %get-tuple-element.95) | copy-start | bytes 9437188
  1159.4 9.5 copy-start.5
  1159.4 10.5 copy-start.2
  1168.9 2.3 copy-start.3
  1168.9 3.4 copy-start.4

commit v5 on v4

--- a/solution.py
+++ b/solution.py
@@ -58,8 +58,8 @@
 
 
 def block_of(ref, dim, at, total):
-    if dim is None:
-        return ref
+    if isinstance(dim, tuple):
+        return ref.at[at, pl.ds(*dim)]
     if dim == "columns":
         width = ref.shape[-1] // total
         return ref.at[:, :, pl.ds(pl.multiple_of(at * width, 128), width)]
@@ -126,7 +126,9 @@
         shape = list(array.shape)
         if before == "columns":
             shape[-1] //= count_of(sizes, axes)
-        elif before is not None:
+        elif isinstance(before, tuple):
+            shape = [before[1]] + shape[2:]
+        else:
             del shape[before]
         stages.append(pltpu.VMEM(tuple(shape), array.dtype))
     count = len(specs)
@@ -138,8 +140,8 @@
     for array, (axes, before, after) in zip(arrays, specs):
         shape = list(array.shape)
         total = count_of(sizes, axes)
-        if before is None:
-            shape = [total] + shape
+        if isinstance(before, tuple):
+            shape = [before[1], shape[0]] + shape[2:]
         elif before == "columns":
             shape = [total, shape[0], shape[1], shape[2] // total]
         elif after == "columns":
@@ -524,7 +526,7 @@
     )(*arrays, *inner, *([select] if combined else []))
 
 
-def dispatch_kernel(sizes, specs, *refs):
+def dispatch_kernel(sizes, specs, parts, *refs):
     S, F = sizes["seq"], sizes["fsdp"]
     count = len(specs)
     refs = list(refs)
@@ -534,16 +536,26 @@
         return taken
 
     sources = take(count)
-    tok_any, g_any, down_any, select_ref = take(4)
+    tok_any, down_any, select_ref = take(3)
+    g_parts = take(parts)
     results = take(count)
-    rows_out, through_out = take(2)
-    tok_ref, rows_ref, g_ref, down_ref, through_ref, row_send, row_recv, own_sem, in_sem, out_sem, *sems = refs
+    rows_out, through_out, g_out = take(3)
+    tok_ref, rows_ref, g_ref, down_ref, through_ref, row_send, row_recv, own_sem, in_sem, out_sem, g_sem, *sems = refs
     f = lax.axis_index("fsdp")
     slots = rows_out.shape[2]
     met = greet(sizes)
     inward = [pltpu.make_async_copy(tok_any.at[b], tok_ref.at[b], in_sem.at[b]) for b in range(S)]
     inward.append(pltpu.make_async_copy(down_any, down_ref, in_sem.at[S]))
-    inward.append(pltpu.make_async_copy(g_any, g_ref, in_sem.at[S + 1]))
+    b = 0
+    for g_any in g_parts:
+        for j in range(g_any.shape[1]):
+            for group in range(F):
+                row = pl.ds((group * S + b) * slots, slots)
+                inward.append(
+                    pltpu.make_async_copy(g_any.at[group, j], g_ref.at[row], g_sem.at[b, group])
+                )
+            b += 1
+    whole_g = pltpu.make_async_copy(g_ref, g_out, in_sem.at[S + 1])
     for copy in inward:
         copy.start()
     blocks = Blocks(sizes, specs, sources, results, sems)
@@ -575,8 +587,9 @@
         sent.append(copy)
         if b == 0:
             blocks.start()
-    inward[S].wait()
-    inward[S + 1].wait()
+    for copy in inward[S:]:
+        copy.wait()
+    whole_g.start()
     span = through_ref.shape[1]
     outward = []
     for n in range(g_ref.shape[0] // span):
@@ -594,40 +607,42 @@
         outward[-1].start()
     for copy in outward[-2:]:
         copy.wait()
+    whole_g.wait()
     blocks.wait()
     for copy in sent:
         copy.wait()
 
 
-def dispatch(arrays, specs, tokens, grads_in, w_down, select, sizes, collective_id):
+def dispatch(arrays, specs, tokens, g_parts, w_down, select, sizes, collective_id):
     S, F = sizes["seq"], sizes["fsdp"]
     slots = select.shape[1] // F
     width = tokens.shape[2]
-    count = grads_in.shape[0]
+    count = F * S * slots
     hidden = w_down.shape[0]
     span = 512
     return pl.pallas_call(
-        functools.partial(dispatch_kernel, sizes, specs),
+        functools.partial(dispatch_kernel, sizes, specs, len(g_parts)),
         out_shape=block_outs(sizes, arrays, specs)
         + [
             jax.ShapeDtypeStruct((F, S, slots, width), BF),
             jax.ShapeDtypeStruct((count, hidden), F32),
+            jax.ShapeDtypeStruct((count, width), BF),
         ],
-        in_specs=[ANY] * (len(arrays) + 3) + [VM],
-        out_specs=[ANY] * (len(arrays) + 2),
+        in_specs=[ANY] * (len(arrays) + 2) + [VM] + [ANY] * len(g_parts),
+        out_specs=[ANY] * (len(arrays) + 3),
         scratch_shapes=[
             pltpu.VMEM(tokens.shape, BF),
             pltpu.VMEM((S, select.shape[1], width), BF),
-            pltpu.VMEM(grads_in.shape, BF),
+            pltpu.VMEM((count, width), BF),
             pltpu.VMEM(w_down.shape, BF),
             pltpu.VMEM((2, span, hidden), F32),
-            DMA((S, F)), DMA((S, F)), DMA((S,)), DMA((S + 2,)), DMA((2,)),
+            DMA((S, F)), DMA((S, F)), DMA((S,)), DMA((S + 2,)), DMA((2,)), DMA((S, F)),
         ] + block_scratch(sizes, arrays, specs),
         compiler_params=pltpu.CompilerParams(
             collective_id=collective_id, has_side_effects=True, vmem_limit_bytes=58 << 20
         ),
         name="dispatch",
-    )(*arrays, tokens, grads_in, w_down, select)
+    )(*arrays, tokens, w_down, select, *g_parts)
 
 
 def expert_kernel(
@@ -699,7 +714,7 @@
         "ffn": (["base", "gain"], ["resid_out", "all_out"]),
         "grad": (["base", "gain", "resid", "add"], ["grad_out", "gain_out", "all_out"]),
         "last": (
-            ["base", "gain", "resid", "inputs", "length", "gout", "gqkv"],
+            ["base", "gain", "resid", "inputs", "heads", "length", "gout", "gqkv"],
             ["grad_out", "low_out", "gains_all", "gout_out", "gqkv_out"],
         ),
     }[mode]
@@ -857,8 +872,10 @@
         return pltpu.make_async_copy(gain_stage, given["gains_all"].at[me], gain_own.at[0])
 
     def send_gains():
-        for j in range(gain_stage.shape[0]):
+        number = gain_sum.shape[1] // 128
+        for j in range(number):
             gain_stage[j : j + 1, :] = gain_sum[:, j * 128 : (j + 1) * 128]
+        gain_stage[number:, :] = given["heads"][...]
         own_gains().start()
         for step in range(1, N):
             gain_copy(step).start()
@@ -1017,13 +1034,13 @@
         outs = [
             full,
             jax.ShapeDtypeStruct((rows, width), BF),
-            jax.ShapeDtypeStruct((S * F, width // 128, 128), F32),
+            jax.ShapeDtypeStruct((S * F, width // 128 + 2, 128), F32),
             jax.ShapeDtypeStruct(gout.shape[1:], F32),
             jax.ShapeDtypeStruct((owned[0], owned[1] * S), F32),
         ]
         out_specs = [VM, VM, ANY, VM, VM]
         N = S * F
-        scratch += [pltpu.VMEM((1, width), F32), pltpu.VMEM((width // 128, 128), F32)]
+        scratch += [pltpu.VMEM((1, width), F32), pltpu.VMEM((width // 128 + 2, 128), F32)]
         scratch += [DMA((N,)), DMA((N,)), DMA((1,))]
         scratch += [
             pltpu.VMEM(gout.shape, BF),
@@ -1052,6 +1069,25 @@
     )(part, *others, *extras)
 
 
+def widen_kernel(*refs):
+    half = len(refs) // 2
+    for narrow, wide in zip(refs[:half], refs[half:]):
+        wide[...] = narrow[...].astype(F32)
+
+
+def widen(arrays):
+    specs = [pl.BlockSpec((1,) + array.shape[1:], lambda i: (i, 0, 0)) for array in arrays]
+    return pl.pallas_call(
+        widen_kernel,
+        grid=(arrays[0].shape[0],),
+        out_shape=[jax.ShapeDtypeStruct(array.shape, F32) for array in arrays],
+        in_specs=specs,
+        out_specs=specs,
+        compiler_params=pltpu.CompilerParams(vmem_limit_bytes=40 << 20),
+        name="widen",
+    )(*arrays)
+
+
 def turn(values, cosine, sine):
     return values * cosine + pltpu.roll(values, HD // 2, 1) * sine
 
@@ -1074,20 +1110,86 @@
         body(pl.ds(pl.multiple_of(n * step, step), step))
 
 
-def attend_kernel(sizes, heads, blocks, specs, *refs):
+class Rows:
+    def __init__(self, sizes, early, source, target, sems):
+        F = sizes["fsdp"]
+        f = lax.axis_index("fsdp")
+        send_sem, recv_sem, own_sem = sems
+        self.copies = []
+        for b in range(early):
+            own = pltpu.make_async_copy(source(b, f), target(b, f), own_sem.at[b])
+            self.copies.append([own])
+            for step in range(1, F):
+                away = lax.rem(f + step, F)
+                self.copies[b].append(
+                    pltpu.make_async_remote_copy(
+                        src_ref=source(b, away), dst_ref=target(b, f),
+                        send_sem=send_sem.at[b, step], recv_sem=recv_sem.at[b, step],
+                        device_id={"fsdp": away}, device_id_type=MESH,
+                    )
+                )
+
+    def start(self, b):
+        for copy in self.copies[b]:
+            copy.start()
+
+    def wait(self, b):
+        for copy in self.copies[b]:
+            copy.wait()
+
+
+def row_scratch(sizes, early, slots, width):
+    if not early:
+        return []
+    F = sizes["fsdp"]
+    return [pltpu.VMEM((early, F * slots, width), BF), DMA((early, F)), DMA((early, F)), DMA((early,))]
+
+
+def rows_at(ref, slots):
+    return lambda b, i: ref.at[b, pl.ds(pl.multiple_of(i * slots, 16), slots)]
+
+
+def attend_kernel(sizes, heads, blocks, early, specs, *refs):
     count = len(specs)
     length_ref, tok_ref, gain_ref, wq_ref, cos_ref, sin_ref, gains_ref, wo_ref = refs[:8]
     select_ref, cot_ref = refs[8:10]
-    sources = refs[10 : 10 + count]
-    attn_ref, proj_ref, low_ref, out_ref, part_ref, rows_ref = refs[10 + count : 16 + count]
-    results = refs[16 + count : 16 + 2 * count]
-    k_all, v_all, *sems = refs[16 + 2 * count :]
+    refs = list(refs[10:])
+
+    def take(number):
+        taken, refs[:number] = refs[:number], []
+        return taken
+
+    first = take(2 if early else 0)
+    sources = take(count)
+    attn_ref, proj_ref, low_ref, out_ref, part_ref, rows_ref = take(6)
+    early_out = take(1 if early else 0)
+    results = take(count)
+    k_all, v_all = take(2)
+    row_refs = take(4 if early else 0)
+    sems = refs
     step = pl.program_id(0)
+
+    def early_rows():
+        slots = early_out[0].shape[2]
+        return Rows(
+            sizes, early, rows_at(row_refs[0], slots), lambda b, i: early_out[0].at[i, b], row_refs[1:]
+        )
 
     @pl.when(step == 0)
     def _():
         greet(sizes)()
         Blocks(sizes, specs, sources, results, sems).start()
+        if early:
+            rows_away = early_rows()
+            for b in range(early):
+
+                def pick_first(at):
+                    row_refs[0][b, :, at] = jnp.dot(
+                        first[0][b], first[1][b, :, at], preferred_element_type=F32
+                    ).astype(BF)
+
+                tiles(row_refs[0].shape[2], 512, pick_first)
+                rows_away.start(b)
 
     rows, width = proj_ref.shape
     length = length_ref[0]
@@ -1142,19 +1244,27 @@
             select_ref[0], cot_ref[0, :, at], preferred_element_type=F32
         ).astype(BF)
 
-    tiles(rows_ref.shape[2], 512, pick)
+    @pl.when(step >= early)
+    def _():
+        tiles(rows_ref.shape[2], 512, pick)
 
     @pl.when(step == blocks - 1)
     def _():
+        if early:
+            rows_away = early_rows()
+            for b in range(early):
+                rows_away.wait(b)
         Blocks(sizes, specs, sources, results, sems).wait()
 
 
 def attend(
-    length, tokens, gain, w_proj, cosine, sine, gains, w_out, select, cot, heads, extras, specs,
-    sizes, collective_id,
+    length, tokens, gain, w_proj, cosine, sine, gains, w_out, select, cot, heads, early, extras,
+    specs, sizes, collective_id,
 ):
     total, width = tokens.shape
     blocks = select.shape[0]
+    F = sizes["fsdp"]
+    slots = select.shape[1] // F
     own_width = w_proj.shape[1]
     rows = total // blocks
     q_width = heads * HD
@@ -1162,6 +1272,11 @@
     def by_rows(columns):
         return pl.BlockSpec((rows, columns), lambda i: (i, 0))
 
+    def leading(array):
+        return pl.BlockSpec(
+            (early,) + array.shape[1:], lambda i: (0, 0, 0), pipeline_mode=pl.Buffered(1)
+        )
+
     def by_block(array):
         return pl.BlockSpec((1,) + array.shape[1:], lambda i: (i, 0, 0))
 
@@ -1169,7 +1284,7 @@
         return pl.BlockSpec(array.shape, lambda i: (0, 0), pipeline_mode=pl.Buffered(1))
 
     return pl.pallas_call(
-        functools.partial(attend_kernel, sizes, heads, blocks, specs),
+        functools.partial(attend_kernel, sizes, heads, blocks, early, specs),
         grid=(blocks,),
         out_shape=[
             jax.ShapeDtypeStruct((total, width), BF),
@@ -1177,8 +1292,10 @@
             jax.ShapeDtypeStruct((total, own_width), BF),
             jax.ShapeDtypeStruct((total, q_width), BF),
             jax.ShapeDtypeStruct((total, width), BF),
-            jax.ShapeDtypeStruct(select.shape[:2] + (width,), BF),
-        ] + block_outs(sizes, extras, specs),
+            jax.ShapeDtypeStruct((blocks - early, select.shape[1], width), BF),
+        ]
+        + ([jax.ShapeDtypeStruct((F, early, slots, width), BF)] if early else [])
+        + block_outs(sizes, extras, specs),
         in_specs=[
             pl.BlockSpec(memory_space=pltpu.SMEM),
             by_rows(width),
@@ -1190,30 +1307,49 @@
             whole(w_out),
             by_block(select),
             by_block(cot),
-        ] + [ANY] * len(extras),
+        ]
+        + ([leading(select), leading(cot)] if early else [])
+        + [ANY] * len(extras),
         out_specs=[
             by_rows(width), by_rows(own_width), by_rows(own_width), by_rows(q_width), by_rows(width),
-            pl.BlockSpec((1, select.shape[1], width), lambda i: (i, 0, 0)),
-        ] + [ANY] * len(extras),
+            pl.BlockSpec((1, select.shape[1], width), lambda i: (jnp.maximum(i - early, 0), 0, 0)),
+        ] + [ANY] * (len(extras) + (1 if early else 0)),
         scratch_shapes=[pltpu.VMEM((total, HD), BF), pltpu.VMEM((total, HD), BF)]
+        + row_scratch(sizes, early, slots, width)
         + block_scratch(sizes, extras, specs),
         compiler_params=pltpu.CompilerParams(
             collective_id=collective_id, has_side_effects=True, vmem_limit_bytes=58 << 20
         ),
         name="attend",
-    )(length, tokens, gain, w_proj, cosine, sine, gains, w_out, select, cot, *extras)
-
-
-def attend_back_kernel(sizes, heads, blocks, specs, *refs):
+    )(
+        length, tokens, gain, w_proj, cosine, sine, gains, w_out, select, cot,
+        *([select, cot] if early else []), *extras,
+    )
+
+
+def attend_back_kernel(sizes, heads, blocks, early, specs, *refs):
     count = len(specs)
     length_ref, proj_ref, low_ref, kv_ref, grad_ref, wo_ref, wq_ref, cos_ref, sin_ref, gains_ref = refs[:10]
-    select_ref, back_ref, attn_any, o_any, ga_any = refs[10:15]
-    sources = refs[15 : 15 + count]
-    part_ref, gains_out, gqkv_out, gout_out = refs[15 + count : 19 + count]
-    results = refs[19 + count : 19 + 2 * count]
-    gk_all, gv_all, go_ref, out_all, attn_all, o_all, ga_all, gqkv_stage, gout_stage, all_sem, out_sem, *sems = refs[
-        19 + 2 * count :
-    ]
+    select_ref, back_ref, attn_any, o_any, ga_any, moe_any = refs[10:16]
+    refs = list(refs[16:])
+
+    def take(number):
+        taken, refs[:number] = refs[:number], []
+        return taken
+
+    sources = take(count)
+    part_ref, gains_out, gqkv_out, gout_out = take(4)
+    results = take(count)
+    gk_all, gv_all, go_ref, out_all, attn_all, o_all, ga_all, gqkv_stage, gout_stage, all_sem, out_sem = take(11)
+    row_refs = take(4 if early else 0)
+    sems = refs
+    slots = moe_any.shape[2]
+
+    def early_rows():
+        return Rows(
+            sizes, early, lambda b, i: moe_any.at[i, b], rows_at(row_refs[0], slots), row_refs[1:]
+        )
+
     inward = [
         pltpu.make_async_copy(source, target, all_sem.at[i])
         for i, (source, target) in enumerate(((attn_any, attn_all), (o_any, o_all), (ga_any, ga_all)))
@@ -1243,6 +1379,10 @@
         Blocks(sizes, specs, sources, results, sems).start()
         for copy in inward:
             copy.start()
+        if early:
+            rows_away = early_rows()
+            for b in range(early - 1, -1, -1):
+                rows_away.start(b)
         gk_all[...] = jnp.zeros_like(gk_all)
         gv_all[...] = jnp.zeros_like(gv_all)
         gains_out[...] = jnp.zeros_like(gains_out)
@@ -1296,12 +1436,24 @@
     tiles(part_ref.shape[2], 256, leave)
     over_rows = (((0,), (0,)), ((), ()))
 
-    def combine(at):
-        part_ref[1, :, at] = lax.dot_general(
-            select_ref[0], back_ref[0, :, at], over_rows, preferred_element_type=F32
-        ).astype(BF)
-
-    tiles(part_ref.shape[2], 512, combine)
+    def combine(rows_of):
+        def one_part(at):
+            part_ref[1, :, at] = lax.dot_general(
+                select_ref[0], rows_of(at), over_rows, preferred_element_type=F32
+            ).astype(BF)
+
+        tiles(part_ref.shape[2], 512, one_part)
+
+    @pl.when(block_at >= early)
+    def _():
+        combine(lambda at: back_ref[0, :, at])
+
+    for b in range(early):
+        @pl.when(block_at == b)
+        def _():
+            early_rows().wait(b)
+            combine(lambda at: row_refs[0][b, :, at])
+
 
     @pl.when(step == blocks - 1)
     def _():
@@ -1332,7 +1484,7 @@
 
 def attend_back(
     length, projected, low, grad, w_out, w_proj, cosine, sine, gains, select, back, attn_low, o_low,
-    heads, extras, specs, sizes, collective_id,
+    moe_rows, heads, early, extras, specs, sizes, collective_id,
 ):
     total, own_width = projected.shape
     width = w_out.shape[1]
@@ -1351,7 +1503,7 @@
         return pl.BlockSpec(array.shape, lambda i: (0, 0), pipeline_mode=pl.Buffered(1))
 
     return pl.pallas_call(
-        functools.partial(attend_back_kernel, sizes, heads, blocks, specs),
+        functools.partial(attend_back_kernel, sizes, heads, blocks, early, specs),
         grid=(blocks,),
         out_shape=[
             jax.ShapeDtypeStruct((2, total, width), BF),
@@ -1371,8 +1523,10 @@
             by_rows(HD),
             whole(gains),
             by_block(select),
-            by_block(back),
-        ] + [ANY] * (3 + len(extras)),
+            pl.BlockSpec(
+                (1,) + back.shape[1:], lambda i: (jnp.maximum(blocks - 1 - i - early, 0), 0, 0)
+            ),
+        ] + [ANY] * (4 + len(extras)),
         out_specs=[
             pl.BlockSpec((2, rows, width), lambda i: (0, blocks - 1 - i, 0)),
             pl.BlockSpec((2, HD), lambda i: (0, 0)),
@@ -1389,14 +1543,16 @@
             pltpu.VMEM((2, span, width), BF),
             DMA((3,)),
             DMA((2, 2)),
-        ] + block_scratch(sizes, extras, specs),
+        ]
+        + row_scratch(sizes, early, moe_rows.shape[2], width)
+        + block_scratch(sizes, extras, specs),
         compiler_params=pltpu.CompilerParams(
             collective_id=collective_id, has_side_effects=True, vmem_limit_bytes=58 << 20
         ),
         name="attend_back",
     )(
         length, projected, low, low, grad, w_out, w_proj, cosine, sine, gains, select, back,
-        attn_low, o_low, grad, *extras,
+        attn_low, o_low, grad, moe_rows, *extras,
     )
 
 
@@ -1490,13 +1646,15 @@
     select = one_hot.astype(BF).reshape(S, F * own_experts * capacity, tok_count)
     grouped = (S, F, own_experts * capacity, width)
 
-    attn_low, projected, qkv_low, o_low, o_part, cot_rows, down_w = attend(
+    fused = capacity % 16 == 0
+    early = S // 2 if fused else 0
+    attn_low, projected, qkv_low, o_low, o_part, cot_rows, *g_first, down_w = attend(
         lengths, tok_all.reshape(seq_total, width), gain_attn[None], w_proj, cosine, sine,
-        gain_heads, out_own, select, cot_all, heads, [w_down.reshape((S, own_experts) + w_down.shape[1:])],
+        gain_heads, out_own, select, cot_all, heads, early, [w_down.reshape((S, own_experts) + w_down.shape[1:])],
         ((("seq",), 0, "columns"),), sizes, 3,
     )
     o_part = o_part.reshape(1, S, tok_count, width)
-    cot_rows = cot_rows.reshape(grouped)
+    cot_rows = cot_rows.reshape((S - early,) + grouped[1:])
 
     residual, ffn_all, g_rows = line(
         "ffn", sizes, o_part, [tokens[0], gain_ffn], [cot_rows], ((("fsdp",), 1, 0),), 2
@@ -1527,17 +1685,17 @@
 
     up_blocks = w_gate_up.reshape((S, own_experts) + w_gate_up.shape[1:])
     side_specs = ((("seq",), 0, 0), (EVERY, 0, 0))
-    g_flat = g_rows.reshape(-1, width)
-    fused = capacity % 16 == 0
     if fused:
-        gate_up_w, gate_got, x_rows, through = dispatch(
-            [up_blocks, gate_send], side_specs, ffn_all, g_flat, down_w[0], select, sizes, 4
+        gate_up_w, gate_got, x_rows, through, g_flat = dispatch(
+            [up_blocks, gate_send], side_specs, ffn_all, [*g_first, g_rows], down_w[0], select,
+            sizes, 4,
         )
     else:
         ffn_rows = mm("brt,btd->brd", select, ffn_all).astype(BF).reshape(grouped)
         gate_up_w, gate_got, x_rows = exchange(
             [up_blocks, gate_send, ffn_rows], side_specs + ((("fsdp",), 1, 0),), sizes, 4
         )
+        g_flat = g_rows.reshape(-1, width)
         through = mm("rd,hd->rh", g_flat, down_w[0])
     row_gate = gate_got.reshape(S, F, -1)[:, :, :capacity].transpose(1, 0, 2).reshape(-1, 1)
     x_flat = x_rows.reshape(-1, width)
@@ -1554,7 +1712,7 @@
         (grad_part,) = grad_part
     else:
         grad_part = mm("brt,brd->btd", select, grad_back.reshape(S, -1, width)).astype(BF)
-    grad_gate_up = up_got.reshape(w_gate_up.shape).astype(F32)
+    moe_rows = moe_rows.reshape(F, S, capacity, width)
     prob_slots = prob_got.reshape(S, F, -1)[:, :, :capacity].transpose(1, 0, 2)
     prob_slots = prob_slots.reshape(expert_count, capacity)
 
@@ -1572,18 +1730,12 @@
     grad_final = jnp.where(valid[:, None], cotangent[0].astype(F32), 0.0)
     grad_residual, grad_gain_ffn, grad_attn_low, moe_back = line(
         "grad", sizes, grad_part[None], [grad_final, gain_ffn, residual, grad_ffn_add],
-        [moe_rows.reshape(F, S, capacity, width)], ((("fsdp",), 0, 1),), 7,
+        [moe_rows], ((("fsdp",), (early, S - early), 1),), 7,
     )
     grad_attn_low = grad_attn_low.reshape(seq_total, width)
 
-    last_parts, grad_gain_heads, grad_qkv_part, grad_out_part, down_got = attend_back(
-        lengths, projected, qkv_low, grad_attn_low, out_own, w_proj, cosine, sine, gain_heads,
-        select, moe_back.reshape(S, -1, width), attn_low, o_low, heads, [down_term[None]],
-        ((("seq",), "columns", 0),), sizes, 9,
-    )
-    grad_qkv_part = grad_qkv_part.reshape(S, F, w_rows, own_width)
     early_gains = jnp.concatenate(
-        [jnp.zeros((width,), F32), grad_gain_ffn[0], grad_gain_heads.reshape(-1)]
+        [jnp.zeros((width,), F32), grad_gain_ffn[0], jnp.zeros((2 * HD,), F32)]
     )
     small_blocks = jnp.concatenate(
         [grad_router_part.reshape(N, -1), early_gains.reshape(N, -1)], axis=1
@@ -1591,22 +1743,29 @@
     small_rows = -(-small_blocks.shape[1] // 1024) * 8
     small_blocks = jnp.pad(small_blocks, ((0, 0), (0, small_rows * 128 - small_blocks.shape[1])))
     small_blocks = small_blocks.reshape(N, small_rows, 128)
+    last_parts, grad_gain_heads, grad_qkv_part, grad_out_part, down_got, small_got = attend_back(
+        lengths, projected, qkv_low, grad_attn_low, out_own, w_proj, cosine, sine, gain_heads,
+        select, moe_back.reshape(S - early, -1, width), attn_low, o_low, moe_rows, heads, early,
+        [down_term[None], small_blocks], ((("seq",), "columns", 0), (EVERY, 0, 0)), sizes, 9,
+    )
+    grad_qkv_part = grad_qkv_part.reshape(S, F, w_rows, own_width)
     (
-        grad_inputs, final, late_gains, grad_out, grad_qkv, small_got
+        grad_inputs, final, late_gains, grad_out, grad_qkv
     ) = line(
         "last", sizes, last_parts.reshape(2, S, tok_count, width),
         [
-            grad_residual, gain_attn[None], residual, tokens[0], lengths,
+            grad_residual, gain_attn[None], residual, tokens[0], grad_gain_heads, lengths,
             grad_out_part.reshape(F, -1, width), grad_qkv_part,
         ],
-        [small_blocks], ((EVERY, 0, 0),), 8,
-    )
-    grad_down = down_got.reshape(w_down.shape).astype(F32)
+        [], (), 8,
+    )
+    grad_gate_up, grad_down = widen(
+        [up_got.reshape(w_gate_up.shape), down_got.reshape(w_down.shape)]
+    )
     small_sum = jnp.sum(small_got, axis=0).reshape(-1)
     grad_router = small_sum[:router_size].reshape(w_router.shape)
-    late_sum = jnp.concatenate(
-        [jnp.sum(late_gains, axis=0).reshape(-1), jnp.zeros((width + 2 * HD,), F32)]
-    )
+    late_flat = jnp.sum(late_gains, axis=0).reshape(-1)
+    late_sum = jnp.concatenate([late_flat[:width], jnp.zeros((width,), F32), late_flat[width:]])
     device_at = seq_at * F + lax.axis_index("fsdp")
     grad_gains = small_sum[router_size : router_size + small] + lax.dynamic_slice_in_dim(
         late_sum, device_at * small, small, 0

time: 1180 us -> 1160 us (0.983)
  other arithmetic: 27.9 us -> 15.1 us
    pallas_call x3, Pallas kernels: 467 us -> 442 us  [line(): pl.pallas_call(functools.partial(line_kernel, sizes, chunks, mode, specs)...]
    convert_element_type x2 -> x0, other arithmetic: 13.1 us -> none  [the longest x1 9.49 us: per_device(): grad_gate_up = up_got.reshape(w_gate_up.shape).astype(F32)]
    pallas_call x2 -> x3, Pallas kernels: 215 us -> 227 us  [the longest x1 150 us: dispatch(): pl.pallas_call(functools.partial(dispatch_kernel, sizes, specs, len(g_par...]
where the time goes in v5:
time: 1160 us
  Pallas kernels  1110 us (96%)
  local copies, waits for them, and re-layouts  22.6 us (2%)
  other arithmetic  15.1 us (1%)
    pallas_call x3, Pallas kernels, line(): pl.pallas_call(functools.partial(line_kernel, sizes, chunks, mode, specs)...  442 us
    pallas_call x1, Pallas kernels, entry(): pl.pallas_call(functools.partial(entry_kernel, sizes), out_shape=[line_ou...  163 us
    pallas_call x1, Pallas kernels, dispatch(): pl.pallas_call(functools.partial(dispatch_kernel, sizes, specs, len(g_par...  150 us
    pallas_call x1, Pallas kernels, grads(): pl.pallas_call(functools.partial(grads_kernel, sizes, specs, combined), o...  136 us
    pallas_call x1, Pallas kernels, attend_back(): pl.pallas_call(functools.partial(attend_back_kernel, sizes, heads, blocks...  92.2 us
    pallas_call x1, Pallas kernels, attend(): pl.pallas_call(functools.partial(attend_kernel, sizes, heads, blocks, ear...  70.2 us
    pallas_call x1, Pallas kernels, expert(): pl.pallas_call(expert_kernel, grid=(steps,), out_shape=[jax.ShapeDtypeStr...  53.1 us

profile of v5, /device:TPU:0, one launch (start us, length us, event | category | flops | bytes accessed | tf_op | source)
XLA Modules:
  0.0 1159.0 jit_solution(5088940642813793213)
XLA Ops:
  0.6 1.3 pad_add_fusion.table_ref
  4.2 162.5 %entry.1 = (bf16[4,256,2048]{2,1,0:T(8,128)(2,1)}, bf16[4,256,2048]{2,1,0:T(8,128)(2,1)}, s32[4,16,256]{2,1,0:T(8,128)}, bf16[4,8,64,1280]{3,2,1,0:T(8,128)(2,1)...) custom-call(bf16[256,2048]{1,0:T(8,128)(2,1)} %bitcast.102, bf16[256,2048]{1,0:T(8,128)(2,1)} %bitcast.113, ...), custom_call_target="tpu_custom_call" | custom-call | tf_op jit(solution)/shard_map/entry/pallas_call | solution.py:383
  167.7 1.3 fusion.refs_8_.refs_10_.refs_4_.refs_6_
  171.5 1.9 fusion.9
  173.5 1.3 pad_maximum_fusion
  175.4 70.2 %attend.1 = (bf16[1024,2048]{1,0:T(8,128)(2,1)}, f32[1024,1280]{1,0:T(8,128)}, bf16[1024,1280]{1,0:T(8,128)(2,1)}, bf16[1024,1024]{1,0:T(8,128)(2,1)}, bf16[1024...) custom-call(s32[1]{0:T(128)} %copy.70.refs_0_.refs_6_, ...), custom_call_target="tpu_custom_call" | custom-call | tf_op jit(solution)/shard_map/attend/pallas_call | solution.py:1286
  245.6 128.4 %line_ffn.1 = (f32[256,2048]{1,0:T(8,128)}, bf16[4,256,2048]{2,1,0:T(8,128)(2,1)}, bf16[8,2,80,2048]{3,2,1,0:T(8,128)(2,1)}) custom-call(bf16[1,4,256,2048]{3,2,1,0:T(8,128)(2,1)} %bitcast.114, bf16[256,2048]{1,0:T(8,128)(2,1)} %bitcast.103, f32[1,2048]{1,0:T(1,128)} %bitcast.133, bf16[2,8,80,2048]{3,2,1,0:T(8,128)(2,1)} %bitcast.109), custom_call_target="tpu_custom_call" | custom-call | tf_op jit(solution)/shard_map/line_ffn/pallas_call | solution.py:1059
  374.5 1.6 fusion.4
  377.8 150.4 %dispatch.1 = (bf16[4,1,512,1536]{3,2,1,0:T(8,128)(2,1)}, f32[32,16,128]{2,1,0:T(8,128)}, bf16[8,4,80,2048]{3,2,1,0:T(8,128)(2,1)}, f32[2560,768]{1,0:T(8,128)}, bf16[2560,2048]{1,0:T(8,128)(2,1)}) custom-call(bf16[4,1,512,1536]{3,2,1,0:T(8,128)(2,1)} %bitcast.107, f32[32,16,128]{2,1,0:T(8,128)} %bitcast.121, ...), custom_call_target="tpu_custom_call" | custom-call | tf_op jit(solution)/shard_map/dispatch/pallas_call | solution.py:623
  529.3 1.7 reshape.289.gate_ref
  530.9 53.1 %expert.1 = (bf16[2560,2048]{1,0:T(8,128)(2,1)}, bf16[2560,2048]{1,0:T(8,128)(2,1)}, bf16[2560,1536]{1,0:T(8,128)(2,1)}, bf16[2560,768]{1,0:T(8,128)(2,1)}, f32[2560,1]{1,0:T(8,128)}) custom-call(bf16[2560,2048]{1,0:T(8,128)(2,1)} %bitcast.91, f32[2560,1]{1,0:T(8,128)} %reshape.289.gate_ref, f32[2560,768]{1,0:T(8,128)} %get-tuple-element.72.through_ref, ...), custom_call_target="tpu_custom_call" | custom-call | tf_op jit(solution)/shard_map/expert/pallas_call | solution.py:692
  584.0 1.7 reduce.1
  586.7 136.5 %grads.1 = (bf16[4,8,80,2048]{3,2,1,0:T(8,128)(2,1)}, f32[32,16,128]{2,1,0:T(8,128)}, bf16[4,512,1536]{2,1,0:T(8,128)(2,1)}, bf16[768,2048]{1,0:T(8,128)(2,1)}, bf16[4,256,2048]{2,1,0:T(8,128)(2,1)}) custom-call(bf16[8,4,80,2048]{3,2,1,0:T(8,128)(2,1)} %bitcast.101, f32[32,16,128]{2,1,0:T(8,128)} %bitcast.120, bf16[2560,2048]{1,0:T(8,128)(2,1)} %bitcast.92, ...), custom_call_target="tpu_custom_call" | custom-call | tf_op jit(solution)/shard_map/grads/pallas_call | solution.py:511
  724.9 1.7 fusion.2
  727.1 1.8 fusion.23.refs_4_
  728.9 1.5 convert_select_fusion.refs_1_
  730.4 138.5 %line_grad.1 = (f32[256,2048]{1,0:T(8,128)}, f32[1,2048]{1,0:T(1,128)}, bf16[4,256,2048]{2,1,0:T(8,128)(2,1)}, bf16[2,8,80,2048]{3,2,1,0:T(8,128)(2,1)}) custom-call(bf16[1,4,256,2048]{3,2,1,0:T(8,128)(2,1)} %bitcast.111, f32[256,2048]{1,0:T(8,128)} %convert_select_fusion.refs_1_, f32[1,2048]{1,0:T(1,128)} %bitcast.134, ...), custom_call_target="tpu_custom_call" | custom-call | tf_op jit(solution)/shard_map/line_grad/pallas_call | solution.py:1059
  870.6 92.2 %attend_back.1 = (bf16[2,1024,2048]{2,1,0:T(8,128)(2,1)}, f32[2,128]{1,0:T(2,128)}, bf16[2048,1280]{1,0:T(8,128)(2,1)}, bf16[1024,2048]{1,0:T(8,128)(2,1)}, bf16...) custom-call(s32[1]{0:T(128)} %copy.70.refs_0_.refs_6_, f32[1024,1280]{1,0:T(8,128)} %get-tuple-element.62.refs_1_, ...), custom_call_target="tpu_custom_call" | custom-call | tf_op jit(solution)/shard_map/attend_back/pallas_call | solution.py:1505
  962.7 2.8 copy-done
  965.5 1.9 copy-done.1
  967.4 6.7 widen.1
  974.1 175.2 %line_last.1 = (f32[256,2048]{1,0:T(8,128)}, bf16[256,2048]{1,0:T(8,128)(2,1)}, f32[32,18,128]{2,1,0:T(8,128)}, f32[128,2048]{1,0:T(8,128)}, f32[64,5120]{1,0:T(8,128)}) custom-call(bf16[2,4,256,2048]{3,2,1,0:T(8,128)(2,1)} %bitcast.105, f32[256,2048]{1,0:T(8,128)} %get-tuple-element.90.refs_1_, f32[1,2048]{1,0:T(1,128)} %bitcast.136, ...), custom_call_target="tpu_custom_call" | custom-call | tf_op jit(solution)/shard_map/line_last/pallas_call | solution.py:1059
  1153.0 2.4 copy.71
  1155.4 1.3 copy.72
  (76 shorter events, 19.1 us)
Async XLA Ops:
  245.6 130.5 %copy-start.6 = (s32[1,256,8]{1,2,0:T(8,128)S(1)}, s32[1,256,8]{1,2,0:T(8,128)}, u32[]{:S(2)}) copy-start(s32[1,256,8]{1,2,0:T(8,128)} %param.14) | copy-start | bytes 24580
  245.6 130.7 %copy-start.7 = (s32[1,256,8]{1,2,0:T(8,128)S(1)}, s32[1,256,8]{1,2,0:T(8,128)}, u32[]{:S(2)}) copy-start(s32[1,256,8]{1,2,0:T(8,128)} %param.15) | copy-start | bytes 24580
  723.1 5.7 copy-start.2
  962.7 2.8 copy-start
  965.5 1.9 copy-start.1
  1149.3 6.1 copy-start.3
  1149.3 7.4 copy-start.4
  1153.0 4.8 copy-start.5

commit v6 on v5

--- a/solution.py
+++ b/solution.py
@@ -45,15 +45,24 @@
     return {axes[0]: at // sizes[axes[1]], axes[1]: at % sizes[axes[1]]}
 
 
+def each(total, body):
+    @pl.loop(1, total)
+    def _(step):
+        body(step)
+
+
 def greet(sizes):
     total = count_of(sizes, EVERY)
     me = index_of(sizes, EVERY)
     barrier = pltpu.get_barrier_semaphore()
-    for step in range(1, total):
+
+    def signal(step):
         pl.semaphore_signal(
             barrier, inc=1, device_id=place_of(sizes, EVERY, lax.rem(me + step, total)),
             device_id_type=MESH,
         )
+
+    each(total, signal)
     return lambda: pl.semaphore_wait(barrier, total - 1)
 
 
@@ -83,24 +92,23 @@
                     pltpu.make_async_copy(stages[i], result, own_sem.at[i, 1]),
                 )
             )
-            self.parted.append([])
-            for step in range(1, total):
+
+            def away(step, i=i, axes=axes, before=before, after=after, me=me, total=total):
                 target = lax.rem(me + step, total)
-                self.parted[-1].append(
-                    pltpu.make_async_remote_copy(
-                        src_ref=block_of(sources[i], before, target, total),
-                        dst_ref=block_of(results[i], after, me, total),
-                        send_sem=send_sem.at[i, step],
-                        recv_sem=recv_sem.at[i, step],
-                        device_id=place_of(sizes, axes, target),
-                        device_id_type=MESH,
-                    )
+                return pltpu.make_async_remote_copy(
+                    src_ref=block_of(sources[i], before, target, total),
+                    dst_ref=block_of(results[i], after, me, total),
+                    send_sem=send_sem.at[i, step],
+                    recv_sem=recv_sem.at[i, step],
+                    device_id=place_of(sizes, axes, target),
+                    device_id_type=MESH,
                 )
 
+            self.parted.append((total, away))
+
     def start(self):
-        for copies in self.parted:
-            for copy in copies:
-                copy.start()
+        for total, away in self.parted:
+            each(total, lambda step: away(step).start())
         for inward, _ in self.own:
             inward.start()
 
@@ -113,8 +121,8 @@
         inward.wait()
         outward.start()
         outward.wait()
-        for copy in self.parted[i]:
-            copy.wait()
+        total, away = self.parted[i]
+        each(total, lambda step: away(step).wait())
 
 
 def block_scratch(sizes, arrays, specs):
@@ -310,13 +318,12 @@
             to_chip(slot, step).wait_recv()
             to_other(slot, step).start()
 
-    smalls = []
-    for step in range(1, N):
+    def small_copy(step):
         target = lax.rem(me + step, N)
-        copy = remote(small_ref, small_out.at[me], sm_send.at[step], sm_recv.at[step],
+        return remote(small_ref, small_out.at[me], sm_send.at[step], sm_recv.at[step],
                       place_of(sizes, EVERY, target))
-        copy.start()
-        smalls.append(copy)
+
+    each(N, lambda step: small_copy(step).start())
     for i, copy in enumerate(inward):
         copy.wait()
         outward[i].start()
@@ -357,8 +364,9 @@
             block = plane_block(slot, lax.rem(other - 2 * step + F, F))
             remote(block, block, sib_send.at[slot, step], sib_recv.at[slot, step],
                    {"fsdp": other}).wait_recv()
-    for copy in tables + smalls:
+    for copy in tables:
         copy.wait()
+    each(N, lambda step: small_copy(step).wait())
 
 
 def entry(tokens, cotangent, table, w_qkv, w_out, small, sizes, collective_id, chunks=4):
@@ -560,6 +568,7 @@
         copy.start()
     blocks = Blocks(sizes, specs, sources, results, sems)
     met()
+    blocks.start()
     sent = []
     for b in range(S):
         inward[b].wait()
@@ -585,8 +594,6 @@
         )
         copy.start()
         sent.append(copy)
-        if b == 0:
-            blocks.start()
     for copy in inward[S:]:
         copy.wait()
     whole_g.start()
@@ -724,11 +731,22 @@
         taken, refs[:number] = refs[:number], []
         return taken
 
-    (part,) = take(1)
-    given = dict(zip(names[0], take(len(names[0]))))
+    loaded = len(names[0]) + 1 - (3 if mode == "last" else 0)
+    outside = take(loaded)
+    kept = names[0][loaded - 1 :]
+    given = dict(zip(kept, take(len(kept))))
     sources = take(count)
     given.update(zip(names[1], take(len(names[1]))))
     results = take(count)
+    part, *inner = take(loaded)
+    given.update(zip(names[0], inner))
+    (load_sem,) = take(1)
+    loads = [
+        pltpu.make_async_copy(source, target, load_sem.at[i])
+        for i, (source, target) in enumerate(zip(outside, [part] + inner))
+    ]
+    for copy in loads:
+        copy.start()
     landings = take(2)
     gather = mode != "last"
     if gather:
@@ -749,6 +767,8 @@
     met = greet(sizes)
     blocks = Blocks(sizes, extra, sources, results, refs)
     met()
+    for copy in loads:
+        copy.wait()
     if mode == "grad":
         given["gain_out"][...] = jnp.zeros_like(given["gain_out"])
     if mode == "last":
@@ -877,8 +897,7 @@
             gain_stage[j : j + 1, :] = gain_sum[:, j * 128 : (j + 1) * 128]
         gain_stage[number:, :] = given["heads"][...]
         own_gains().start()
-        for step in range(1, N):
-            gain_copy(step).start()
+        each(N, lambda step: gain_copy(step).start())
 
     plane = None
     if mode == "last":
@@ -939,7 +958,7 @@
     def final_lag(z):
         return 1 + jnp.maximum(jnp.maximum(z - 2, S - 3 - z), 0)
 
-    ahead = min(steps, AHEAD if gather else 4)
+    ahead = min(steps, AHEAD if gather else steps)
     for c in range(ahead):
         end_step(c)
     if plane:
@@ -1010,19 +1029,21 @@
     if mode == "last":
         columns_step()
         own_gains().wait()
-        for step in range(1, N):
-            gain_copy(step).wait()
+        each(N, lambda step: gain_copy(step).wait())
     blocks.wait()
 
 
-def line(mode, sizes, part, others, extras, specs, collective_id, chunks=CHUNKS):
+def line(mode, sizes, part, others, extras, specs, collective_id):
+    chunks = CHUNKS if mode != "last" else CHUNKS // 2
     S, F = sizes["seq"], sizes["fsdp"]
     parts, _, rows, width = part.shape
     full = jax.ShapeDtypeStruct((rows, width), F32)
     everyone = jax.ShapeDtypeStruct((S, rows, width), BF)
     steps = chunks * parts
-    scratch = [pltpu.VMEM((parts, S, rows, width), BF)] * 2
-    in_specs = [VM] * (1 + len(others))
+    loaded = [part] + list(others[:-3] if mode == "last" else others)
+    scratch = [pltpu.VMEM(array.shape, array.dtype) for array in loaded] + [DMA((len(loaded),))]
+    scratch += [pltpu.VMEM((parts, S, rows, width), BF)] * 2
+    in_specs = [ANY] * (1 + len(others))
     sems = [DMA((2, S, steps)), DMA((2, S, steps))]
     if mode == "ffn":
         outs, out_specs = [full, everyone], [VM, ANY]
@@ -1051,7 +1072,6 @@
             DMA((S,)),
         ]
         scratch += block_scratch(sizes, [gout, gqkv], ((("fsdp",), 0, 0), (("fsdp",), 1, 0)))
-        in_specs[-2:] = [ANY, ANY]
         in_specs[-3] = pl.BlockSpec(memory_space=pltpu.SMEM)
     if mode != "last":
         scratch.append(pltpu.VMEM((rows, width), BF))
@@ -1096,9 +1116,9 @@
     scores = lax.dot_general(
         query, keys, (((1,), (1,)), ((), ())), preferred_element_type=F32
     ) * scale
-    row = first_row + lax.broadcasted_iota(jnp.int32, scores.shape, 0)
+    row = first_row + lax.broadcasted_iota(jnp.int32, (scores.shape[0], 1), 0)
     column = lax.broadcasted_iota(jnp.int32, scores.shape, 1)
-    scores = jnp.where((column <= row) & (column < length), scores, MASKED)
+    scores = jnp.where(column <= jnp.minimum(row, length - 1), scores, MASKED)
     peak = jnp.max(scores, axis=-1, keepdims=True)
     weights = jnp.exp(scores - peak)
     return weights * (1.0 / jnp.sum(weights, axis=-1, keepdims=True))
@@ -1108,6 +1128,12 @@
     @pl.loop(0, width // step)
     def _(n):
         body(pl.ds(pl.multiple_of(n * step, step), step))
+
+
+def each_head(heads, body):
+    @pl.loop(0, heads)
+    def _(n):
+        body(pl.ds(pl.multiple_of(n * HD, HD), HD))
 
 
 class Rows:
@@ -1230,7 +1256,7 @@
                 mixed = jnp.dot(probs.astype(BF), v_all[:reach, :], preferred_element_type=F32)
                 out_ref[:, column] = mixed.astype(BF)
 
-            tiles(heads * HD, HD, one)
+            each_head(heads, one)
 
     def leave(at):
         part_ref[:, at] = jnp.dot(
@@ -1420,7 +1446,7 @@
                 out_all[here, column] = grad_raw.astype(BF)
                 gains_out[0:1, :] += gained
 
-            tiles(heads * HD, HD, one)
+            each_head(heads, one)
 
     grad_k = (gk_all[here, :] * scale).astype(BF).astype(F32)
     grad_raw, gained = back(proj_ref[:, heads * HD : (heads + 1) * HD], k_gain, grad_k)

time: 1160 us -> 1150 us (level)
  Pallas kernels: 1110 us -> 1090 us
    pallas_call x3, Pallas kernels: 442 us -> 423 us  [line(): pl.pallas_call(functools.partial(line_kernel, sizes, chunks, mode, specs)...]
where the time goes in v6:
time: 1150 us; the launch traced here: 1140 us
  Pallas kernels  1090 us (95%)
  local copies, waits for them, and re-layouts  22.6 us (2%)
  other arithmetic  15.1 us (1%)
    pallas_call x3, Pallas kernels, line(): pl.pallas_call(functools.partial(line_kernel, sizes, chunks, mode, specs)...  423 us
    pallas_call x1, Pallas kernels, entry(): pl.pallas_call(functools.partial(entry_kernel, sizes), out_shape=[line_ou...  163 us
    pallas_call x1, Pallas kernels, dispatch(): pl.pallas_call(functools.partial(dispatch_kernel, sizes, specs, len(g_par...  149 us
    pallas_call x1, Pallas kernels, grads(): pl.pallas_call(functools.partial(grads_kernel, sizes, specs, combined), o...  137 us
    pallas_call x1, Pallas kernels, attend_back(): pl.pallas_call(functools.partial(attend_back_kernel, sizes, heads, blocks...  92.2 us
    pallas_call x1, Pallas kernels, attend(): pl.pallas_call(functools.partial(attend_kernel, sizes, heads, blocks, ear...  70.2 us
    pallas_call x1, Pallas kernels, expert(): pl.pallas_call(expert_kernel, grid=(steps,), out_shape=[jax.ShapeDtypeStr...  53.1 us

profile of v6, /device:TPU:0, one launch (start us, length us, event | category | flops | bytes accessed | tf_op | source)
XLA Modules:
  0.0 1138.6 jit_solution(13339623010661673677)
XLA Ops:
  0.6 1.3 pad_add_fusion.table_ref
  4.2 162.7 %entry.1 = (bf16[4,256,2048]{2,1,0:T(8,128)(2,1)}, bf16[4,256,2048]{2,1,0:T(8,128)(2,1)}, s32[4,16,256]{2,1,0:T(8,128)}, bf16[4,8,64,1280]{3,2,1,0:T(8,128)(2,1)...) custom-call(bf16[256,2048]{1,0:T(8,128)(2,1)} %bitcast.102, bf16[256,2048]{1,0:T(8,128)(2,1)} %bitcast.113, ...), custom_call_target="tpu_custom_call" | custom-call | tf_op jit(solution)/shard_map/entry/pallas_call | solution.py:391
  167.9 1.3 fusion.refs_8_.refs_10_.refs_4_.refs_6_
  171.7 1.9 fusion.9
  173.6 1.3 pad_maximum_fusion
  175.6 70.2 %attend.1 = (bf16[1024,2048]{1,0:T(8,128)(2,1)}, f32[1024,1280]{1,0:T(8,128)}, bf16[1024,1280]{1,0:T(8,128)(2,1)}, bf16[1024,1024]{1,0:T(8,128)(2,1)}, bf16[1024...) custom-call(s32[1]{0:T(128)} %copy.70.refs_0_.refs_6_, ...), custom_call_target="tpu_custom_call" | custom-call | tf_op jit(solution)/shard_map/attend/pallas_call | solution.py:1312
  245.8 126.1 %line_ffn.1 = (f32[256,2048]{1,0:T(8,128)}, bf16[4,256,2048]{2,1,0:T(8,128)(2,1)}, bf16[8,2,80,2048]{3,2,1,0:T(8,128)(2,1)}) custom-call(bf16[1,4,256,2048]{3,2,1,0:T(8,128)(2,1)} %bitcast.114, bf16[256,2048]{1,0:T(8,128)(2,1)} %bitcast.103, f32[1,2048]{1,0:T(1,128)} %bitcast.133, bf16[2,8,80,2048]{3,2,1,0:T(8,128)(2,1)} %bitcast.109), custom_call_target="tpu_custom_call" | custom-call | tf_op jit(solution)/shard_map/line_ffn/pallas_call | solution.py:1079
  372.2 1.6 fusion.4
  375.6 148.9 %dispatch.1 = (bf16[4,1,512,1536]{3,2,1,0:T(8,128)(2,1)}, f32[32,16,128]{2,1,0:T(8,128)}, bf16[8,4,80,2048]{3,2,1,0:T(8,128)(2,1)}, f32[2560,768]{1,0:T(8,128)}, bf16[2560,2048]{1,0:T(8,128)(2,1)}) custom-call(bf16[4,1,512,1536]{3,2,1,0:T(8,128)(2,1)} %bitcast.107, f32[32,16,128]{2,1,0:T(8,128)} %bitcast.121, ...), custom_call_target="tpu_custom_call" | custom-call | tf_op jit(solution)/shard_map/dispatch/pallas_call | solution.py:630
  525.5 1.7 reshape.289.gate_ref
  527.2 53.1 %expert.1 = (bf16[2560,2048]{1,0:T(8,128)(2,1)}, bf16[2560,2048]{1,0:T(8,128)(2,1)}, bf16[2560,1536]{1,0:T(8,128)(2,1)}, bf16[2560,768]{1,0:T(8,128)(2,1)}, f32[2560,1]{1,0:T(8,128)}) custom-call(bf16[2560,2048]{1,0:T(8,128)(2,1)} %bitcast.91, f32[2560,1]{1,0:T(8,128)} %reshape.289.gate_ref, f32[2560,768]{1,0:T(8,128)} %get-tuple-element.72.through_ref, ...), custom_call_target="tpu_custom_call" | custom-call | tf_op jit(solution)/shard_map/expert/pallas_call | solution.py:699
  580.3 1.7 reduce.1
  582.9 136.7 %grads.1 = (bf16[4,8,80,2048]{3,2,1,0:T(8,128)(2,1)}, f32[32,16,128]{2,1,0:T(8,128)}, bf16[4,512,1536]{2,1,0:T(8,128)(2,1)}, bf16[768,2048]{1,0:T(8,128)(2,1)}, bf16[4,256,2048]{2,1,0:T(8,128)(2,1)}) custom-call(bf16[8,4,80,2048]{3,2,1,0:T(8,128)(2,1)} %bitcast.101, f32[32,16,128]{2,1,0:T(8,128)} %bitcast.120, bf16[2560,2048]{1,0:T(8,128)(2,1)} %bitcast.92, ...), custom_call_target="tpu_custom_call" | custom-call | tf_op jit(solution)/shard_map/grads/pallas_call | solution.py:519
  721.4 1.7 fusion.2
  723.6 1.8 fusion.23.refs_4_
  725.4 1.5 convert_select_fusion.refs_1_
  726.9 134.8 %line_grad.1 = (f32[256,2048]{1,0:T(8,128)}, f32[1,2048]{1,0:T(1,128)}, bf16[4,256,2048]{2,1,0:T(8,128)(2,1)}, bf16[2,8,80,2048]{3,2,1,0:T(8,128)(2,1)}) custom-call(bf16[1,4,256,2048]{3,2,1,0:T(8,128)(2,1)} %bitcast.111, f32[256,2048]{1,0:T(8,128)} %convert_select_fusion.refs_1_, f32[1,2048]{1,0:T(1,128)} %bitcast.134, ...), custom_call_target="tpu_custom_call" | custom-call | tf_op jit(solution)/shard_map/line_grad/pallas_call | solution.py:1079
  863.4 92.2 %attend_back.1 = (bf16[2,1024,2048]{2,1,0:T(8,128)(2,1)}, f32[2,128]{1,0:T(2,128)}, bf16[2048,1280]{1,0:T(8,128)(2,1)}, bf16[1024,2048]{1,0:T(8,128)(2,1)}, bf16...) custom-call(s32[1]{0:T(128)} %copy.70.refs_0_.refs_6_, f32[1024,1280]{1,0:T(8,128)} %get-tuple-element.62.refs_1_, ...), custom_call_target="tpu_custom_call" | custom-call | tf_op jit(solution)/shard_map/attend_back/pallas_call | solution.py:1531
  955.6 2.8 copy-done
  958.4 1.9 copy-done.1
  960.3 6.7 widen.1
  967.0 162.0 %line_last.1 = (f32[256,2048]{1,0:T(8,128)}, bf16[256,2048]{1,0:T(8,128)(2,1)}, f32[32,18,128]{2,1,0:T(8,128)}, f32[128,2048]{1,0:T(8,128)}, f32[64,5120]{1,0:T(8,128)}) custom-call(bf16[2,4,256,2048]{3,2,1,0:T(8,128)(2,1)} %bitcast.105, f32[256,2048]{1,0:T(8,128)} %get-tuple-element.90.refs_1_, f32[1,2048]{1,0:T(1,128)} %bitcast.136, ...), custom_call_target="tpu_custom_call" | custom-call | tf_op jit(solution)/shard_map/line_last/pallas_call | solution.py:1079
  1132.6 2.4 copy.71
  1135.0 1.3 copy.72
  (76 shorter events, 19.1 us)
Async XLA Ops:
  245.7 128.2 %copy-start.6 = (s32[1,256,8]{1,2,0:T(8,128)S(1)}, s32[1,256,8]{1,2,0:T(8,128)}, u32[]{:S(2)}) copy-start(s32[1,256,8]{1,2,0:T(8,128)} %param.14) | copy-start | bytes 24580
  245.7 128.3 %copy-start.7 = (s32[1,256,8]{1,2,0:T(8,128)S(1)}, s32[1,256,8]{1,2,0:T(8,128)}, u32[]{:S(2)}) copy-start(s32[1,256,8]{1,2,0:T(8,128)} %param.15) | copy-start | bytes 24580
  719.7 5.7 copy-start.2
  955.6 2.8 copy-start
  958.4 1.9 copy-start.1
  1128.9 6.1 copy-start.3
  1128.9 7.4 copy-start.4
  1132.6 4.8 copy-start.5
